TPU v7x, 32 devices: a whole 2x2x4 slice. The times are simulated.
32 devices in a mesh: tp: 4 (over z), dp: 8 (over y, x, core).
Axes of the slice: x: 2, y: 2, z: 4, core: 2. Of those that a mesh axis runs over, the one named last changes fastest.
Arguments:
- tokens: int32 [8, 2048], P('dp')
- cotangent: bfloat16 [8, 2048, 1024], P('dp')
- emb_table: bfloat16 [30592, 1024], P('tp')
- w_qkv: bfloat16 [1024, 3072], P(None, 'tp')
- b_qkv: bfloat16 [16, 192], P('tp')
- w_out: bfloat16 [1024, 1024], P('tp')
- b_out: bfloat16 [1024], replicated
- ln1_gain: bfloat16 [1024], replicated
- ln1_bias: bfloat16 [1024], replicated
- w_gate: bfloat16 [1024, 4096], P(None, 'tp')
- b_gate: bfloat16 [4096], P('tp')
- w_lin: bfloat16 [1024, 4096], P(None, 'tp')
- b_lin: bfloat16 [4096], P('tp')
- w_down: bfloat16 [4096, 1024], P('tp')
- b_down: bfloat16 [1024], replicated
- ln2_gain: bfloat16 [1024], replicated
Outputs:
- output 1: float32 [30592, 1024], P('tp')
- output 2: float32 [1024, 3072], P(None, 'tp')
- output 3: float32 [16, 192], P('tp')
- output 4: float32 [1024, 1024], P('tp')
- output 5: float32 [1024], replicated
- output 6: float32 [1024], replicated
- output 7: float32 [1024], replicated
- output 8: float32 [1024, 4096], P(None, 'tp')
- output 9: float32 [4096], P('tp')
- output 10: float32 [1024, 4096], P(None, 'tp')
- output 11: float32 [4096], P('tp')
- output 12: float32 [4096, 1024], P('tp')
- output 13: float32 [1024], replicated
- output 14: float32 [1024], replicated
All inputs are finite; a program needn't handle non-finite values.
Results may differ from a plain program's by a relative error of at most 0.0152302.
Values sent between devices are 32-bit elements.
A program may use at most 1 GiB of HBM per device.

v0:
```python
import functools

import jax
import jax.numpy as jnp
from jax import lax
from jax.experimental import pallas as pl
from jax.experimental.pallas import tpu as pltpu
from jax.sharding import PartitionSpec as P

ALPHA = 140.0 ** 0.5
EPS = 1e-5
SHRINK = 0.1
ROPE_BASE = 10000.0
WEIGHT_SPECS = (P(None, 'tp'), P('tp', None), P('tp', None), P(), P(), P(), P(None, 'tp'), P('tp'), P(None, 'tp'), P('tp'), P('tp', None), P(), P())
ALL = ('tp', 'dp')
BF = jnp.bfloat16
N0, N1, N2 = range(3)
F32 = jnp.float32
MESH = pl.DeviceIdType.MESH
ANY = pl.BlockSpec(memory_space=pl.ANY)
VMEM = pl.BlockSpec(memory_space=pltpu.VMEM)


def norm_scaled(values, gain):
    mean_val = jnp.mean(values, axis=-1, keepdims=True)
    centered = values - mean_val
    variance = jnp.mean(centered * centered, axis=-1, keepdims=True)
    return centered * lax.rsqrt(variance + EPS) * gain


def geglu(gate_pre, lin_pre):
    return jax.nn.gelu(gate_pre, approximate=False) * lin_pre


def rope_tables(seq_len, head_dim):
    half_dim = head_dim // 2
    inv_freq = ROPE_BASE ** (-2.0 * jnp.arange(half_dim, dtype=F32) / head_dim)
    angles = jnp.arange(seq_len, dtype=F32)[:, None] * inv_freq[None, :]
    return jnp.cos(angles)[:, None, :], jnp.sin(angles)[:, None, :]


def apply_rope(values, cos_tab, sin_tab):
    half_dim = values.shape[-1] // 2
    first_half = values[..., :half_dim]
    second_half = values[..., half_dim:]
    return jnp.concatenate([first_half * cos_tab - second_half * sin_tab, second_half * cos_tab + first_half * sin_tab], axis=-1)


def rcopy(src, dst, send, recv, **where):
    return pltpu.make_async_remote_copy(src_ref=src, dst_ref=dst, send_sem=send, recv_sem=recv, device_id=dict(where), device_id_type=MESH)


def plane():
    p = lax.axis_index('dp')
    y, x, c = p // 4, (p // 2) % 2, p % 2

    def at(rel):
        yy = 1 - y if rel & 4 else y
        xx = 1 - x if rel & 2 else x
        cc = 1 - c if rel & 1 else c
        return yy * 4 + xx * 2 + cc
    return p, at


def entry_barrier(z, n, at):
    bar = pltpu.get_barrier_semaphore()
    for rel in range(1, 8):
        pl.semaphore_signal(bar, inc=1, device_id={'dp': at(rel)}, device_id_type=MESH)

    @pl.when(z > 0)
    def _():
        pl.semaphore_signal(bar, inc=1, device_id={'tp': z - 1}, device_id_type=MESH)

    @pl.when(z < n - 1)
    def _():
        pl.semaphore_signal(bar, inc=1, device_id={'tp': z + 1}, device_id_type=MESH)
    inner = (z > 0) & (z < n - 1)

    @pl.when(inner)
    def _():
        pl.semaphore_wait(bar, 9)

    @pl.when(jnp.logical_not(inner))
    def _():
        pl.semaphore_wait(bar, 8)


LAG = 3


def chain_sum(k, z, n, rows, chunks, part, left, right, done, send_r, send_l, recv_l, recv_r):
    last = n - 1

    def cut(ref, c):
        return ref.at[pl.ds(pl.multiple_of(c * rows, rows), rows)]

    def load(ref, c):
        return ref[pl.ds(pl.multiple_of(c * rows, rows), rows)]

    def store(ref, c, value):
        ref[pl.ds(pl.multiple_of(c * rows, rows), rows)] = value
    cl, cr = k - LAG * z, k - LAG * (last - z)
    okl, okr = (cl >= 0) & (cl < chunks), (cr >= 0) & (cr < chunks)

    @pl.when(okl & (z > 0))
    def _():
        rcopy(cut(left, cl), cut(left, cl), send_r, recv_l.at[cl], tp=z).wait_recv()

    @pl.when(okl & (z == last))
    def _():
        done(cl, load(left, cl) + load(part, cl))

    @pl.when(okl & (z > 0) & (z < last))
    def _():
        run = load(left, cl)

        @pl.when(z >= n // 2)
        def _():
            done(cl, run + load(right, cl))
        store(left, cl, run + load(part, cl))

    @pl.when(okr & (z < last))
    def _():
        rcopy(cut(right, cr), cut(right, cr), send_l, recv_r.at[cr], tp=z).wait_recv()

    @pl.when(okr & (z == 0))
    def _():
        done(cr, load(part, cr) + load(right, cr))

    @pl.when(okr & (z > 0) & (z < last))
    def _():
        run = load(right, cr)

        @pl.when(z < n // 2)
        def _():
            done(cr, load(left, cr) + run)
        store(right, cr, run + load(part, cr))

    @pl.when(okl & (z == 0))
    def _():
        rcopy(cut(part, cl), cut(left, cl), send_r, recv_l.at[cl], tp=z + 1).start()

    @pl.when(okl & (z > 0) & (z < last))
    def _():
        rcopy(cut(left, cl), cut(left, cl), send_r, recv_l.at[cl], tp=z + 1).start()

    @pl.when(okr & (z == last))
    def _():
        rcopy(cut(part, cr), cut(right, cr), send_l, recv_r.at[cr], tp=z - 1).start()

    @pl.when(okr & (z > 0) & (z < last))
    def _():
        rcopy(cut(right, cr), cut(right, cr), send_l, recv_r.at[cr], tp=z - 1).start()


def chain_drain(z, n, part, left, right, send_r, send_l, recv_l, recv_r):
    @pl.when(z < n - 1)
    def _():
        rcopy(part, left, send_r, recv_l.at[0], tp=z + 1).wait_send()

    @pl.when(z > 0)
    def _():
        rcopy(part, right, send_l, recv_r.at[0], tp=z - 1).wait_send()


EDGES = ((0, 0, 2), (0, 0, 4), (0, 0, 1), (2, 1, 4), (4, 2, 2), (2, 0, 1), (4, 0, 1), (6, 1, 1), (6, 2, 1))
CROSS, DIAGONAL, LAST = ((0, 3, 5), (1, 4, 6)), ((3, 7), (4, 8)), {1: (2,), 3: (5,), 5: (6,), 7: (7, 8)}
STEPS = (3, 8, 13, 19, 22, 26)
FIRST = 17
ORDER = (0, 2, 4, 1, 3, 5, 6, 7)


def emb_kernel(n, rows, chunks, cuts, part, piece, toks, *refs):
    m = len(cuts)
    local, outs = refs[:m], refs[m + N1:N2 * m + N1]
    out, (bias, tok_all, wall, left, right, raw, low, send_r, send_l, recv_l, recv_r, tsend, trecv, tself, zsend, zrecv, psend, precv, lsem, isem, osem, bsem) = refs[m], refs[N2 * m + N1:]
    z = lax.axis_index('tp')
    p, at = plane()
    entry_barrier(z, n, at)
    half = piece.shape[N0] // N2

    @pl.when(z < n - N1)
    def _():
        rcopy(piece, wall.at[z, p], zsend.at[z], zrecv.at[z], tp=z + N1).start()

    @pl.when(z > N0)
    def _():
        rcopy(piece, wall.at[z, p], bsem.at[N1], zrecv.at[z], tp=z - N1).start()
    mine = [pltpu.make_async_copy(toks, tok_all.at[p], tself)]
    mine += [pltpu.make_async_copy(src, dst.at[z], lsem.at[i]) for i, (src, dst) in enumerate(zip(local, outs))]
    for copy in mine:
        copy.start()
    for rel in range(N1, 8):
        rcopy(toks, tok_all.at[p], tsend.at[rel], trecv.at[rel], dp=at(rel)).start()

    def others(d, body):
        @pl.when(z >= d)
        def _():
            body(z - d, -N1)

        @pl.when(z + d < n)
        def _():
            body(z + d, N1)

    def region(t, rel, side):
        blk = wall.at[t, at(rel)]
        return blk if side == N0 else wall.at[t, at(rel), pl.ds((side - N1) * half, half)]

    def give(t, j):
        rel, side, to = EDGES[j]
        rcopy(region(t, rel, side), region(t, rel, side), psend.at[t, j], precv.at[t, j], dp=at(to)).start()

    def take(t, j):
        rel, side, to = EDGES[j]
        blk = region(t, rel ^ to, side)
        rcopy(blk, blk, psend.at[t, j], precv.at[t, j], dp=p).wait_recv()

    def gave(t, j):
        rel, side, to = EDGES[j]
        rcopy(region(t, rel, side), region(t, rel, side), psend.at[t, j], precv.at[t, j], dp=p).wait_send()

    def arrive(d):
        def body(t, sign):
            blk = wall.at[t, p]
            rcopy(blk, blk, zsend.at[t], zrecv.at[t], tp=z).wait_recv()

            @pl.when((z - sign >= N0) & (z - sign < n))
            def _():
                rcopy(blk, blk, zsend.at[t], zrecv.at[t], tp=z - sign).start()
            for j in range(3):
                give(t, j)
        others(d, body)

    def relay(d, moves):
        def body(t, sign):
            for first, *rest in moves:
                take(t, first)
                for j in rest:
                    give(t, j)
        others(d, body)

    for d in range(N1, n):
        arrive(d)

    def done(c, value):
        out[pl.ds(pl.multiple_of(c * rows, rows), rows)] = value.astype(out.dtype)

    def other(i):
        return i + (i + n - z) // n

    def loaded(i, rel, slot):
        return pltpu.make_async_copy(wall.at[other(i), at(rel), pl.ds(N0, cuts[-N1][N1])], raw.at[slot], isem.at[slot])

    def stored(i, rel, slot):
        return [pltpu.make_async_copy(low.at[slot, pl.ds(lo, hi - lo)], dst.at[other(i), at(rel)], osem.at[slot, k]) for k, ((lo, hi), dst) in enumerate(zip(cuts, outs))]
    plan = [(i, rel) for rel in ORDER for i in range(n - N1)]

    def prefetch(s):
        i, rel = plan[s]
        for j in LAST.get(rel, ()):
            take(other(i), j)
        loaded(i, rel, s % N2).start()

    def convert(s):
        i, rel = plan[s]
        loaded(i, rel, s % N2).wait()
        if s >= N2:
            for copy in stored(*plan[s - N2], s % N2):
                copy.wait()
        low[s % N2] = raw[s % N2].astype(low.dtype)
        if s + N1 < len(plan):
            prefetch(s + N1)
        for copy in stored(i, rel, s % N2):
            copy.start()
    events = [(STEPS[d - N1], functools.partial(relay, d, CROSS)) for d in range(N1, n)] + [(STEPS[d + n - N2], functools.partial(relay, d, DIAGONAL)) for d in range(N1, n)]
    events += [(FIRST - N1, functools.partial(prefetch, N0))] + [(FIRST + s, functools.partial(convert, s)) for s in range(len(plan))]

    @pl.loop(N0, max(chunks + LAG * (n - N1), FIRST + len(plan)))
    def _(k):
        chain_sum(k, z, n, rows, chunks, part, left, right, done, send_r, send_l, recv_l, recv_r)
        for at_step, event in events:
            pl.when(k == at_step)(event)

    chain_drain(z, n, part, left, right, send_r, send_l, recv_l, recv_r)
    for s in (len(plan) - N2, len(plan) - N1):
        for copy in stored(*plan[s], s % N2):
            copy.wait()

    def finish(t, sign):
        for j in range(len(EDGES)):
            gave(t, j)
        tail = pltpu.make_async_copy(wall.at[t, p, pl.ds(cuts[-N1][N1], bias.shape[N1])], bias.at[t], bsem.at[N0])
        tail.start()
        tail.wait()

        @pl.when((z - sign >= N0) & (z - sign < n))
        def _():
            rcopy(wall.at[t, p], wall.at[t, p], zsend.at[t], zrecv.at[t], tp=z).wait_send()
    for d in range(N1, n):
        others(d, finish)
    for copy in mine:
        copy.wait()
    for rel in range(N1, 8):
        rcopy(toks, tok_all.at[at(rel)], tsend.at[rel], trecv.at[rel], dp=at(rel)).wait()

    @pl.when(z < n - N1)
    def _():
        rcopy(piece, wall.at[z, p], zsend.at[z], zrecv.at[z], tp=z + N1).wait_send()

    @pl.when(z > N0)
    def _():
        rcopy(piece, wall.at[z, p], bsem.at[N1], zrecv.at[z], tp=z - N1).wait_send()


def embed(part, piece, toks, local, n_tp, n_dp):
    seq, width = part.shape
    rows = min(64, seq // 4)
    chunks = seq // rows
    cuts, lo = [], 0
    for weight in local:
        cuts.append((lo, lo + weight.shape[0] // n_dp))
        lo = cuts[-1][1]
    dma = pltpu.SemaphoreType.DMA
    shapes = [jax.ShapeDtypeStruct((seq, width), BF)]
    shapes += [jax.ShapeDtypeStruct((n_tp, n_dp, w.shape[0] // n_dp, w.shape[1]), BF) for w in local]
    shapes += [jax.ShapeDtypeStruct((n_tp, piece.shape[0] - lo, width), F32), jax.ShapeDtypeStruct((n_dp,) + toks.shape, toks.dtype), jax.ShapeDtypeStruct((n_tp, n_dp) + piece.shape, F32)]
    out = pl.pallas_call(
        functools.partial(emb_kernel, n_tp, rows, chunks, cuts),
        name='embed',
        out_shape=shapes,
        in_specs=[VMEM] + [ANY] * (2 + len(local)),
        out_specs=[VMEM] + [ANY] * (len(shapes) - 1),
        scratch_shapes=[pltpu.VMEM((seq, width), F32)] * 2 + [pltpu.VMEM((2, lo, width), F32), pltpu.VMEM((2, lo, width), BF), dma, dma, dma((chunks,)), dma((chunks,)),
                        dma((8,)), dma((8,)), dma, dma((n_tp,)), dma((n_tp,)), dma((n_tp, len(EDGES))), dma((n_tp, len(EDGES))), dma((len(local),)), dma((2,)), dma((2, len(local))), dma((2,))],
        compiler_params=pltpu.CompilerParams(collective_id=0, has_side_effects=True, vmem_limit_bytes=56 * 2 ** 20),
        cost_estimate=pl.CostEstimate(flops=20 * 10 ** 9, bytes_accessed=80 * 2 ** 20, transcendentals=0),
    )(part, piece, toks, *[w.reshape(n_dp, w.shape[0] // n_dp, w.shape[1]) for w in local])
    return out[0], [w.reshape(n_tp, -1, w.shape[3]) for w in out[1:-3]], out[-3], out[-2]


RING = 8
HOLD = 6
OPEN, ADD, CROSSED, PLANE, HOP = 1, 2, 6, 10, 2


def sums_kernel(n, rows, chunks, jobs, part, *refs):
    odd, even = refs[:jobs], refs[jobs:N2 * jobs]
    out, grads, landed, left, right, total, work, fresh, cross, last, along, final, send_r, send_l, recv_l, recv_r, osend, orecv, csend, crecv, esem, fsem, xsend, xrecv, ysend, yrecv, zsend, zrecv, frecv, gsem = refs[N2 * jobs:]
    z = lax.axis_index('tp')
    p, at = plane()
    entry_barrier(z, n, at)
    block = out.shape[N2]
    lead = jnp.maximum(z, n - N1 - z)
    span = N2 * n
    units = jobs * span
    size = work.shape[N2]

    for m in range(jobs):
        @pl.loop(N0, span)
        def _(u, m=m):
            dst = landed.at[m * span + u]
            rcopy(odd[m].at[u // N2, :, pl.ds(pl.multiple_of((u % N2) * size, size), size)], dst, csend, crecv.at[m * span + u], dp=at(N1)).start()

    def here(u):
        return (u >= N0) & (u < units)

    def sides(u):
        side = u % N2
        return side, at(N2) * (N1 - side) + at(4) * side, at(4) * (N1 - side) + at(N2) * side

    def fetch(u):
        slot = u % HOLD

        @pl.when(u >= HOLD)
        def _():
            rcopy(work.at[slot, pl.ds(N0, N2)], cross.at[u - HOLD], xsend.at[slot], xrecv.at[u - HOLD], dp=p).wait_send()
        for m in range(jobs):
            @pl.when(u // span == m)
            def _(m=m):
                v = u - m * span
                pltpu.make_async_copy(even[m].at[v // N2, :, pl.ds(pl.multiple_of((v % N2) * size, size), size)], work.at[slot], esem.at[slot]).start()
        rcopy(landed.at[u], landed.at[u], csend, crecv.at[u], dp=p).wait_recv()
        pltpu.make_async_copy(landed.at[u], fresh.at[u % N2], fsem.at[u % N2]).start()

    def add(u):
        slot = u % HOLD
        pltpu.make_async_copy(landed.at[u], work.at[slot], esem.at[slot]).wait()
        pltpu.make_async_copy(landed.at[u], fresh.at[u % N2], fsem.at[u % N2]).wait()
        for q in range(4):
            work[slot, q] = work[slot, q] + fresh[u % N2, q]

    def add_send(u):
        slot = u % HOLD
        side, first, second = sides(u)
        rcopy(work.at[slot, N1 + side], cross.at[u, N0], xsend.at[slot], xrecv.at[u], dp=first).start()
        rcopy(work.at[slot, 3], cross.at[u, N1], xsend.at[slot], xrecv.at[u], dp=first).start()

    def crossed(u):
        slot = u % HOLD
        rcopy(cross.at[u], cross.at[u], xsend.at[slot], xrecv.at[u], dp=p).wait_recv()
        cross[u, N0] = cross[u, N0] + work[slot, N0]
        cross[u, N1] = cross[u, N1] + work[slot, N2 - u % N2]

    def crossed_send(u):
        side, first, second = sides(u)
        rcopy(cross.at[u, N1], last.at[u], ysend, yrecv.at[u], dp=second).start()

    def in_plane(u):
        rcopy(last.at[u], last.at[u], ysend, yrecv.at[u], dp=p).wait_recv()
        cross[u, N0] = cross[u, N0] + last[u]

    def along_tp(k, t, send):
        toward = jnp.where(z < t, z, n - N1 - z)
        late = HOP * jnp.where(z == t, max(t, n - N1 - t), toward)
        u = k - PLANE - N1 - late
        mine = (u // span) * N2 + u % N2
        ok = here(u) & ((u // N2) % n == t)

        def add_from(ref, sem):
            rcopy(ref, ref, zsend, sem, tp=z).wait_recv()
            cross[u, N0] = cross[u, N0] + ref[...]
        if send:
            @pl.when(ok & (z < t))
            def _():
                rcopy(cross.at[u, N0], along.at[u], zsend, zrecv.at[u], tp=z + N1).start()

            @pl.when(ok & (z > t + N1))
            def _():
                rcopy(cross.at[u, N0], along.at[u], zsend, zrecv.at[u], tp=z - N1).start()

            @pl.when(ok & (z == t + N1))
            def _():
                rcopy(cross.at[u, N0], final.at[mine], zsend, frecv.at[mine], tp=z - N1).start()

            @pl.when(ok & (z == t))
            def _():
                pltpu.make_async_copy(cross.at[u, N0], grads.at[mine], gsem).start()
        else:
            @pl.when(ok & (((z > N0) & (z <= t)) | ((z > t) & (z < n - N1))))
            def _():
                add_from(along.at[u], zrecv.at[u])
            if t < n - N1:
                @pl.when(ok & (z == t))
                def _():
                    add_from(final.at[mine], frecv.at[mine])

    def chunk(c):
        return total.at[c % RING]

    def done(c, value):
        @pl.when(c >= RING)
        def _():
            pltpu.make_async_copy(chunk(c), chunk(c), osend.at[c % RING]).wait()
        total[c % RING] = value

    @pl.loop(N0, max(chunks + LAG * (n - N1) + N1, units + PLANE + N1 + HOP * (n - N1)))
    def _(k):
        c = k - LAG * lead - N1

        @pl.when((c >= N0) & (c < chunks))
        def _():
            where = out.at[p, pl.ds(pl.multiple_of(c * rows, rows), rows)]
            for rel in range(8):
                src = total.at[c % RING, :, pl.ds(pl.multiple_of(at(rel) * block, block), block)]
                if rel == N0:
                    pltpu.make_async_copy(src, where, osend.at[c % RING]).start()
                else:
                    rcopy(src, where, osend.at[c % RING], orecv.at[rel], dp=at(rel)).start()
        chain_sum(k, z, n, rows, chunks, part, left, right, done, send_r, send_l, recv_l, recv_r)
        stages = ((OPEN, fetch, None), (ADD, add, add_send), (CROSSED, crossed, crossed_send), (PLANE, in_plane, None))
        for offset, stage, _ in stages:
            pl.when(here(k - offset))(functools.partial(stage, k - offset))
        for t in range(n):
            along_tp(k, t, False)
        for offset, _, stage in stages:
            if stage:
                pl.when(here(k - offset))(functools.partial(stage, k - offset))
        for t in range(n):
            along_tp(k, t, True)

    chain_drain(z, n, part, left, right, send_r, send_l, recv_l, recv_r)
    for c in range(max(N0, chunks - RING), chunks):
        pltpu.make_async_copy(chunk(c), chunk(c), osend.at[c % RING]).wait()
    for rel in range(N1, 8):
        rcopy(out.at[at(rel)], out.at[at(rel)], ysend, orecv.at[rel], dp=p).wait_recv()
    for u in range(units - HOLD, units):
        rcopy(work.at[u % HOLD, pl.ds(N0, N2)], cross.at[u], xsend.at[u % HOLD], xrecv.at[u], dp=p).wait_send()
    rcopy(landed, landed, csend, crecv.at[N0], dp=p).wait_send()
    rcopy(last, last, ysend, yrecv.at[N0], dp=p).wait_send()
    kept = units - units // n
    rcopy(along.at[pl.ds(N0, kept)], along.at[pl.ds(N0, kept)], zsend, zrecv.at[N0], tp=z).wait_send()
    pltpu.make_async_copy(grads, grads, gsem).wait()


def sums(part, odd, even, n_tp, n_dp):
    seq, width = part.shape
    rows = min(64, seq // 4)
    chunks = seq // rows
    jobs = len(odd)
    size = odd[0].shape[2] // 2
    wide = odd[0].shape[3]
    units = jobs * 2 * n_tp
    dma = pltpu.SemaphoreType.DMA
    piece = (size, wide)
    vmem = [(RING, rows, width), (HOLD, 4) + piece, (2, 4) + piece, (units, 2) + piece, (units,) + piece, (units,) + piece, (2 * jobs,) + piece]
    cols, grads, _ = pl.pallas_call(
        functools.partial(sums_kernel, n_tp, rows, chunks, jobs),
        name='sums',
        out_shape=(jax.ShapeDtypeStruct((n_dp, seq, width // n_dp), F32), jax.ShapeDtypeStruct((2 * jobs,) + piece, F32), jax.ShapeDtypeStruct((units, 4) + piece, F32)),
        in_specs=[VMEM] + [ANY] * (2 * jobs),
        out_specs=(ANY,) * 3,
        scratch_shapes=[pltpu.VMEM((seq, width), F32)] * 2 + [pltpu.VMEM(shape, F32) for shape in vmem] + [
            dma, dma, dma((chunks,)), dma((chunks,)), dma((RING,)), dma((8,)), dma, dma((units,)), dma((HOLD,)), dma((2,)),
            dma((HOLD,)), dma((units,)), dma, dma((units,)), dma, dma((units,)), dma((2 * jobs,)), dma],
        compiler_params=pltpu.CompilerParams(collective_id=1, has_side_effects=True, vmem_limit_bytes=63 * 2 ** 20),
        cost_estimate=pl.CostEstimate(flops=20 * 10 ** 9, bytes_accessed=100 * 2 ** 20, transcendentals=0),
    )(part, *odd, *even)
    return cols, grads.reshape(jobs, 2 * size, wide)


WAYS = 4


def table_kernel(ids, rows_ref, out, *tables):
    step = pl.program_id(0)
    count = rows_ref.shape[0]
    part = count // WAYS

    @pl.when(step == 0)
    def _():
        for table in tables:
            table[...] = jnp.zeros_like(table)

    @pl.loop(0, part, unroll=4)
    def _(r):
        for way, table in enumerate(tables):
            row = way * part + r
            where = pl.ds(ids[step * count + row], 1)
            table[where, :] = table[where, :] + rows_ref[pl.ds(row, 1), :]

    @pl.when(step == pl.num_programs(0) - 1)
    def _():
        total = tables[0][...]
        for table in tables[1:]:
            total = total + table[...]
        out[...] = SHRINK * total[:out.shape[0]]


def table_rows(ids, rows, vocab_loc):
    count, block = rows.shape
    step = min(1024, count // 2)
    return pl.pallas_call(
        table_kernel,
        name='table_rows',
        grid_spec=pltpu.PrefetchScalarGridSpec(
            num_scalar_prefetch=1,
            grid=(count // step,),
            in_specs=[pl.BlockSpec((step, block), lambda i, ids: (i, 0))],
            out_specs=pl.BlockSpec((vocab_loc, block), lambda i, ids: (0, 0)),
            scratch_shapes=[pltpu.VMEM((vocab_loc + 8, block), F32)] * WAYS,
        ),
        out_shape=jax.ShapeDtypeStruct((vocab_loc, block), F32),
        compiler_params=pltpu.CompilerParams(dimension_semantics=('arbitrary',), vmem_limit_bytes=48 * 2 ** 20),
        cost_estimate=pl.CostEstimate(flops=3 * 10 ** 9, bytes_accessed=16 * 2 ** 20, transcendentals=0),
    )(ids, rows)


SPREAD = ((0, 2), (0, 4), (0, 1), (2, 4), (4, 2), (2, 1), (4, 1), (6, 1))


def gather_kernel(parts, block_in, out, send, recv, oself):
    p, at = plane()
    bar = pltpu.get_barrier_semaphore()
    for rel in (1, 2, 4):
        pl.semaphore_signal(bar, inc=1, device_id={'dp': at(rel)}, device_id_type=MESH)
    pl.semaphore_wait(bar, 3)
    size, block = block_in.shape
    rows = size // parts
    half = parts // 2

    def copy(j, rel, i, to):
        dst = out.at[pl.ds(i * rows, rows), pl.ds(pl.multiple_of(at(rel) * block, block), block)]
        src = block_in.at[pl.ds(i * rows, rows)] if rel == 0 else dst
        return rcopy(src, dst, send.at[j, i], recv.at[j, i], dp=at(to))

    def give(j, i):
        copy(j, SPREAD[j][0], i, SPREAD[j][1]).start()

    def take(j, i):
        rel, to = SPREAD[j]
        copy(j, rel ^ to, i, 0).wait_recv()
    own = pltpu.make_async_copy(block_in, out.at[:, pl.ds(pl.multiple_of(p * block, block), block)], oself)
    own.start()
    order_x = list(range(parts))
    order_y = order_x[half:] + order_x[:half]
    for i, j in zip(order_x, order_y):
        give(0, i)
        give(1, j)
    for i in order_x:
        give(2, i)
    for i, j in zip(order_x, order_y):
        take(0, i)
        if i < half:
            give(3, i)
        give(5, i)
        take(1, j)
        if j >= half:
            give(4, j)
        give(6, j)
    for i in order_x[:half]:
        for via, part in ((3, i), (4, i + half)):
            take(via, part)
            give(7, part)
    for i in order_x:
        for j in (2, 5, 6, 7):
            take(j, i)
    for i in order_x:
        for j, (rel, to) in enumerate(SPREAD):
            if j != (4 if i < half else 3):
                copy(j, rel, i, 0).wait_send()
    own.wait()


def gathered_columns(block_in, n_dp):
    size, block = block_in.shape
    parts = 4
    dma = pltpu.SemaphoreType.DMA
    return pl.pallas_call(
        functools.partial(gather_kernel, parts),
        name='gathered_columns',
        out_shape=jax.ShapeDtypeStruct((size, n_dp * block), F32),
        in_specs=[ANY],
        out_specs=ANY,
        scratch_shapes=[dma((len(SPREAD), parts)), dma((len(SPREAD), parts)), dma],
        compiler_params=pltpu.CompilerParams(collective_id=2, has_side_effects=True),
        cost_estimate=pl.CostEstimate(flops=10 * 10 ** 9, bytes_accessed=60 * 2 ** 20, transcendentals=0),
    )(block_in)


def dot(a, b, dims):
    return lax.dot_general(a, b, (dims, ((), ())), preferred_element_type=F32)


NT, TN, NN = ((1,), (1,)), ((0,), (0,)), ((1,), (0,))


def attention_kernel(scale, kb, q_ref, k_ref, v_ref, ctx_ref, m_ref, l_ref, s_ref):
    i = pl.program_id(1)
    qb = q_ref.shape[1]
    q = q_ref[0]
    blocks = ((i + 1) * qb + kb - 1) // kb

    def scores(j, top):
        at_k = pl.ds(pl.multiple_of(j * kb, kb), kb)
        s = dot(k_ref[0, at_k, :], q, NT) * scale
        key = j * kb + lax.broadcasted_iota(jnp.int32, (kb, qb), 0)
        query = i * qb + lax.broadcasted_iota(jnp.int32, (kb, qb), 1)
        s = jnp.where(query >= key, s, -1e30)
        s_ref[at_k, :] = s
        return jnp.maximum(top, jnp.max(s, axis=0, keepdims=True))
    top = lax.fori_loop(0, blocks, scores, jnp.full((1, qb), -1e30, F32))

    def weigh(j, total):
        at_k = pl.ds(pl.multiple_of(j * kb, kb), kb)
        e = jnp.exp(s_ref[at_k, :] - top)
        s_ref[at_k, :] = e
        return total + jnp.sum(e, axis=0, keepdims=True)
    total = lax.fori_loop(0, blocks, weigh, jnp.zeros((1, qb), F32))
    inv = 1.0 / total

    def mix(j, acc):
        at_k = pl.ds(pl.multiple_of(j * kb, kb), kb)
        probs = (s_ref[at_k, :] * inv).astype(BF)
        return acc + dot(probs, v_ref[0, at_k, :], TN)
    ctx_ref[0] = lax.fori_loop(0, blocks, mix, jnp.zeros((qb, v_ref.shape[2]), F32))
    m_ref[0] = top
    l_ref[0] = inv


def attention(q, k, v):
    heads, seq, dim = q.shape
    qb, kb = seq // 8, seq // 4
    spec_q = pl.BlockSpec((1, qb, dim), lambda h, i: (h, i, 0))
    spec_k = pl.BlockSpec((1, seq, dim), lambda h, i: (h, 0, 0))
    spec_s = pl.BlockSpec((1, 1, qb), lambda h, i: (h, 0, i))
    stat = jax.ShapeDtypeStruct((heads, 1, seq), F32)
    return pl.pallas_call(
        functools.partial(attention_kernel, dim ** -0.5, kb),
        name='attention',
        grid=(heads, seq // qb),
        in_specs=[spec_q, spec_k, spec_k],
        out_specs=(spec_q, spec_s, spec_s),
        out_shape=(jax.ShapeDtypeStruct((heads, seq, dim), F32), stat, stat),
        scratch_shapes=[pltpu.VMEM((seq, qb), F32)],
        compiler_params=pltpu.CompilerParams(dimension_semantics=('arbitrary', 'arbitrary'), vmem_limit_bytes=32 * 2 ** 20),
        cost_estimate=pl.CostEstimate(flops=3 * 10 ** 9, bytes_accessed=8 * 2 ** 20, transcendentals=10 ** 7),
    )(q, k, v)


def attention_grad_kernel(scale, kb, q_ref, k_ref, v_ref, c_ref, dc_ref, m_ref, l_ref, dq_ref, dk_ref, dv_ref):
    i = pl.program_id(1)
    qb = q_ref.shape[1]
    q, dc = q_ref[0], dc_ref[0]
    dc_f = dc.astype(F32)
    top, inv = m_ref[0], l_ref[0]
    ones = jnp.ones((8, dc.shape[1]), F32)
    mean = lax.dot_general(ones, dc_f * c_ref[0], (NT, ((), ())), precision=lax.Precision.HIGHEST, preferred_element_type=F32)[:1]
    blocks = ((i + 1) * qb + kb - 1) // kb

    @pl.when(i == 0)
    def _():
        dk_ref[...] = jnp.zeros_like(dk_ref)
        dv_ref[...] = jnp.zeros_like(dv_ref)

    def step(j, dq):
        at_k = pl.ds(pl.multiple_of(j * kb, kb), kb)
        keys = k_ref[0, at_k, :]
        s = dot(keys, q, NT) * scale
        key = j * kb + lax.broadcasted_iota(jnp.int32, (kb, qb), 0)
        query = i * qb + lax.broadcasted_iota(jnp.int32, (kb, qb), 1)
        probs = (jnp.exp(jnp.where(query >= key, s, -1e30) - top) * inv).astype(BF)
        d_probs = dot(v_ref[0, at_k, :], dc, NT)
        ds = (probs.astype(F32) * (d_probs - mean) * scale).astype(BF)
        dv_ref[0, at_k, :] += dot(probs, dc, NN)
        dk_ref[0, at_k, :] += dot(ds, q, NN)
        return dq + dot(ds, keys, TN)
    dq_ref[0] = lax.fori_loop(0, blocks, step, jnp.zeros((qb, q.shape[1]), F32))


def attention_grad(q, k, v, ctx, dctx, top, inv):
    heads, seq, dim = q.shape
    qb, kb = seq // 8, seq // 4
    spec_q = pl.BlockSpec((1, qb, dim), lambda h, i: (h, i, 0))
    spec_k = pl.BlockSpec((1, seq, dim), lambda h, i: (h, 0, 0))
    spec_s = pl.BlockSpec((1, 1, qb), lambda h, i: (h, 0, i))
    out = jax.ShapeDtypeStruct((heads, seq, dim), F32)
    return pl.pallas_call(
        functools.partial(attention_grad_kernel, dim ** -0.5, kb),
        name='attention_grad',
        grid=(heads, seq // qb),
        in_specs=[spec_q, spec_k, spec_k, spec_q, spec_q, spec_s, spec_s],
        out_specs=(spec_q, spec_k, spec_k),
        out_shape=(out, out, out),
        compiler_params=pltpu.CompilerParams(dimension_semantics=('arbitrary', 'arbitrary'), vmem_limit_bytes=32 * 2 ** 20),
        cost_estimate=pl.CostEstimate(flops=8 * 10 ** 9, bytes_accessed=16 * 2 ** 20, transcendentals=10 ** 7),
    )(q, k, v, ctx, dctx, top, inv)


def solution(mesh):
    n_tp, n_dp = mesh.shape['tp'], mesh.shape['dp']
    in_specs = (P('dp', None), P('dp', None, None), P('tp', None)) + WEIGHT_SPECS
    out_specs = (P('tp', None),) + WEIGHT_SPECS

    def device_step(tokens, cotangent, emb_table, *weights):
        (w_qkv, b_qkv, w_out, b_out, ln1_gain, ln1_bias, w_gate, b_gate, w_lin, b_lin, w_down, b_down, ln2_gain) = weights
        tp, dp = lax.axis_index('tp'), lax.axis_index('dp')
        tokens = tokens[N0]
        seq_len, width = tokens.shape[N0], emb_table.shape[N1]
        heads, head_dim = b_qkv.shape[N0], b_qkv.shape[N1] // 3
        own = seq_len // n_tp
        ffn = w_gate.shape[N1]
        rk, rf, ro = width // n_dp, ffn // n_dp, w_out.shape[N0] // n_dp
        zero = jnp.minimum(tokens[N0], N0).astype(F32)

        def cut(weight):
            rows = weight.shape[N0] // n_dp
            return lax.dynamic_slice_in_dim(weight, dp * rows, rows, N0)
        bias_rows = jnp.concatenate([b_gate[None], b_lin[None], jnp.zeros((14, ffn), BF)], axis=N0)
        piece = jnp.concatenate([cut(w_gate), cut(w_lin), cut(w_down), cut(w_out), bias_rows], axis=N0).astype(F32)

        vocab_loc = emb_table.shape[N0]
        local_ids = tokens - tp * vocab_loc
        in_shard = (local_ids >= N0) & (local_ids < vocab_loc)
        safe_ids = jnp.where(in_shard, local_ids, N0)
        own_rows = jnp.where(in_shard[:, None], jnp.take(emb_table, safe_ids, axis=N0), 0.0).astype(F32)
        emb_bf, (wg_full, wl_full, wd_full, wo_full), biases, tok_all = embed(own_rows, piece, tokens.reshape(-N1, min(128, seq_len // 8)), (w_gate, w_lin, w_down, w_out), n_tp, n_dp)
        is_own = (jnp.arange(n_tp) == tp)[:, None]
        bg_full, bl_full = [jnp.where(is_own, b[None].astype(F32), biases[:, i]) for i, b in enumerate((b_gate, b_lin))]

        qkv_pre = jnp.dot(emb_bf, w_qkv, preferred_element_type=F32) + b_qkv.reshape(-N1).astype(F32)
        qkv_all = qkv_pre.astype(BF).reshape(seq_len, heads, 3, head_dim)
        cos_tab, sin_tab = rope_tables(seq_len, head_dim)
        queries = apply_rope(qkv_all[:, :, N0].astype(F32), cos_tab, sin_tab).astype(BF).transpose(N1, N0, N2)
        keys_rot = apply_rope(qkv_all[:, :, N1].astype(F32), cos_tab, sin_tab).astype(BF).transpose(N1, N0, N2)
        values = qkv_all[:, :, N2].transpose(N1, N0, N2)
        ctx, top, inv = attention(queries, keys_rot, values)
        context = ctx.transpose(N1, N0, N2).reshape(n_tp, own, heads * head_dim)
        ctx_own = (lax.all_to_all(context, 'tp', N0, N0) + zero).astype(BF)

        emb_own = lax.dynamic_slice_in_dim(emb_bf, tp * own, own, N0).astype(F32)
        cot_own = lax.dynamic_slice_in_dim(cotangent[N0], tp * own, own, N0).astype(F32)
        attn_out = jnp.einsum('hse,hed->sd', ctx_own, wo_full, preferred_element_type=F32) + b_out.astype(F32)
        normed_one, norm_one_pull = jax.vjp(norm_scaled, ALPHA * emb_own + attn_out, ln1_gain.astype(F32))
        hidden = (normed_one + ln1_bias.astype(F32)).astype(BF)
        gate_pre = jnp.einsum('sk,tkc->tsc', hidden, wg_full, preferred_element_type=F32) + bg_full[:, None]
        lin_pre = jnp.einsum('sk,tkc->tsc', hidden, wl_full, preferred_element_type=F32) + bl_full[:, None]
        inner_val, act_pull = jax.vjp(geglu, gate_pre, lin_pre)
        inner_act = inner_val.astype(BF)
        ffn_out = jnp.einsum('tsc,tcd->sd', inner_act, wd_full, preferred_element_type=F32) + b_down.astype(F32)
        norm_two_pull = jax.vjp(norm_scaled, ALPHA * hidden.astype(F32) + ffn_out, ln2_gain.astype(F32))[N1]

        rel_blocks = jnp.arange(n_dp // N2) * N2

        def products(lhs, rhs, spec):
            rows = lhs.shape[-N1] // n_dp
            blocks = lhs.reshape(lhs.shape[:-N1] + (n_dp, rows))
            for first in (N1, N0):
                chosen = jnp.take(blocks, (rel_blocks + first) ^ dp, axis=-N2).reshape(lhs.shape[:-N1] + (-N1,))
                yield jnp.einsum(spec, chosen, rhs, preferred_element_type=F32).reshape(n_tp, n_dp // N2, rows, -N1)

        d_resid_two, d_ln2_gain = norm_two_pull(cot_own)
        d_b_down = jnp.sum(d_resid_two, axis=N0)
        d_ffn_bf = d_resid_two.astype(BF)
        pair_down = products(inner_act, d_ffn_bf, 'tsc,sd->tcd')
        d_inner = jnp.einsum('sd,tcd->tsc', d_ffn_bf, wd_full, preferred_element_type=F32).astype(BF)
        d_gate_pre, d_lin_pre = act_pull(d_inner.astype(F32))
        d_b_gate = jnp.sum(d_gate_pre, axis=N1)
        d_b_lin = jnp.sum(d_lin_pre, axis=N1)
        d_gate_bf = d_gate_pre.astype(BF)
        d_lin_bf = d_lin_pre.astype(BF)
        pair_gate = products(hidden, d_gate_bf, 'sk,tsc->tkc')
        pair_lin = products(hidden, d_lin_bf, 'sk,tsc->tkc')
        d_hidden = ALPHA * d_resid_two + jnp.einsum('tsc,tkc->sk', d_gate_bf, wg_full, preferred_element_type=F32) + jnp.einsum('tsc,tkc->sk', d_lin_bf, wl_full, preferred_element_type=F32)
        d_ln1_bias = jnp.sum(d_hidden, axis=N0)
        d_resid_one, d_ln1_gain = norm_one_pull(d_hidden)
        d_b_out = jnp.sum(d_resid_one, axis=N0)
        d_attn_bf = d_resid_one.astype(BF)
        d_w_out = jnp.einsum('hse,sd->hed', ctx_own, d_attn_bf, preferred_element_type=F32)
        d_w_out = lax.all_gather(lax.psum_scatter(d_w_out.reshape(-N1, width), ALL, scatter_dimension=N0, tiled=True), 'dp', axis=N0, tiled=True)
        d_ctx = jnp.einsum('sd,hed->hse', d_attn_bf, wo_full, preferred_element_type=F32)
        d_context = (lax.all_to_all(d_ctx, 'tp', N0, N0) + zero).astype(BF).reshape(seq_len, heads, head_dim).transpose(N1, N0, N2)

        d_queries, d_keys, d_values = attention_grad(queries, keys_rot, values, ctx, d_context, top, inv)
        d_queries = apply_rope(d_queries.transpose(N1, N0, N2), cos_tab, -sin_tab)
        d_keys = apply_rope(d_keys.transpose(N1, N0, N2), cos_tab, -sin_tab)
        d_qkv = jnp.stack([d_queries, d_keys, d_values.transpose(N1, N0, N2)], axis=N2).reshape(seq_len, -N1)
        d_b_qkv = jnp.sum(d_qkv, axis=N0)
        d_qkv_bf = d_qkv.astype(BF)
        d_w_qkv = lax.psum(jnp.dot(emb_bf.T, d_qkv_bf, preferred_element_type=F32), 'dp')
        d_emb_part = jnp.dot(d_qkv_bf, w_qkv.T, preferred_element_type=F32)
        d_emb_part = lax.dynamic_update_slice_in_dim(d_emb_part, lax.dynamic_slice_in_dim(d_emb_part, tp * own, own, N0) + ALPHA * d_resid_one, tp * own, N0)
        odd, even = zip(*[tuple(pair) for pair in (pair_gate, pair_lin, pair_down)])
        d_cols, mine = sums(d_emb_part, odd, even, n_tp, n_dp)
        d_w_gate, d_w_lin, d_w_down = [lax.all_gather(grad, 'dp', axis=N0, tiled=True) for grad in mine]
        all_ids = tok_all.reshape(-N1) - tp * vocab_loc
        all_ids = jnp.where((all_ids >= N0) & (all_ids < vocab_loc), all_ids, vocab_loc)
        d_table = gathered_columns(table_rows(all_ids, d_cols.reshape(n_dp * seq_len, -N1), vocab_loc), n_dp)

        slot = (jnp.arange(n_tp) == tp).astype(F32)[:, None]
        d_bq_rows = jnp.pad(slot * d_b_qkv[None], ((N0, N0), (N0, ffn - d_b_qkv.shape[N0])))
        small = jnp.concatenate([d_b_gate, d_b_lin, d_bq_rows, jnp.stack([d_b_out, d_ln1_gain, d_ln1_bias, d_b_down, d_ln2_gain])], axis=N0)
        small = lax.psum(small, ALL)
        d_b_gate = lax.dynamic_index_in_dim(small[:n_tp], tp, N0, keepdims=False)
        d_b_lin = lax.dynamic_index_in_dim(small[n_tp:N2 * n_tp], tp, N0, keepdims=False)
        d_b_qkv = lax.dynamic_index_in_dim(small[N2 * n_tp:3 * n_tp], tp, N0, keepdims=False)[:d_b_qkv.shape[N0]].reshape(heads, 3 * head_dim)
        d_b_out, d_ln1_gain, d_ln1_bias, d_b_down, d_ln2_gain = [small[3 * n_tp + i] for i in range(5)]
        return (d_table, d_w_qkv, d_b_qkv, d_w_out, d_b_out, d_ln1_gain, d_ln1_bias, d_w_gate, d_b_gate, d_w_lin, d_b_lin, d_w_down, d_b_down, d_ln2_gain)

    return jax.shard_map(device_step, mesh=mesh, in_specs=in_specs, out_specs=out_specs, check_vma=False)
```

profile of v0, /device:TPU:0, one launch (start us, length us, event | category | flops | bytes accessed | tf_op | source)
XLA Modules:
  0.0 1449.7 jit_solution(7256988189729352187)
XLA Ops:
  19.7 18.8 %gather_fusion = bf16[2048,1024]{1,0:T(8,128)(2,1)} fusion(bf16[7648,1024]{1,0:T(8,128)(2,1)} %param.22, s32[2048]{0:T(1024)S(1)} %broadcast_clamp_fusion), kind=kCustom, calls=%fused_computation.4 | custom fusion | bytes 8396800 | tf_op jit(solution)/shard_map/jit(_take)/gather | solution.py:775
  38.4 5.5 select_convert_fusion.part
  43.9 346.4 %embed.1 = (bf16[2048,1024]{1,0:T(8,128)(2,1)}, bf16[4,8,128,1024]{3,2,1,0:T(8,128)(2,1)}, bf16[4,8,128,1024]{3,2,1,0:T(8,128)(2,1)}, bf16[4,8,128,1024]{3,2,1,0...) custom-call(f32[2048,1024]{1,0:T(8,128)} %select_convert_fusion.part, ...), custom_call_target="tpu_custom_call" | custom-call | flops 20000000000 | bytes 83886080 | tf_op jit(solution)/shard_map/embed/pallas_call | solution.py:327
  390.3 6.0 add_convert_fusion
  418.4 50.2 %attention.1 = (f32[4,2048,64]{2,1,0:T(8,128)S(1)}, f32[4,1,2048]{2,1,0:T(1,128)S(1)}, f32[4,1,2048]{2,1,0:T(1,128)S(1)}) custom-call(bf16[4,2048,64]{2,1,0:T(8,128)(2,1)S(1)} %maximum_bitcast_fusion.2.q_ref, bf16[4,2048,64]{2,1,0:T(8,128)(2,1)S(1)} %maximum_bitcast_fusion.3.k_ref, bf16[4,2048,64]{2,1,0:T(8,128)(2,1)S(1)} %bitcast.277), custom_call_target="tpu_custom_call" | custom-call | flops 3000000000 | bytes 8388608 | tf_op jit(solution)/shard_map/attention/pallas_call | solution.py:687
  470.6 10.2 copy.165
  480.8 5.3 reshape.442
  493.4 43.1 %all-to-all-done = f32[4,512,256]{2,1,0:T(8,128)S(1)} async-done(((f32[4,512,256]{2,1,0:T(8,128)}), f32[4,512,256]{2,1,0:T(8,128)S(1)}, u32[]{:S(2)}, u32[]{:S(2)}) %all-to-all-start) | async-done | bytes 2097184 | tf_op jit(solution)/shard_map/all_to_all | solution.py:788
  541.0 8.0 fusion.40
  549.0 29.5 %fusion.3 = (bf16[4,512,1024]{1,2,0:T(8,128)(2,1)S(1)}, f32[4,512,1024]{1,2,0:T(8,128)}, f32[4,512,1024]{1,2,0:T(8,128)}, f32[4,1024,512]{2,1,0:T(8,128)}) fusion(f32[4,1024]{1,0:T(4,128)S(1)} %bitcast.307, f32[4,1024,512]{2,1,0:T(8,128)} %fusion.40, f32[4,1024]{1,0:T(4,128)S(1)} %bitcast.305, bf16[4,1024,1024]{2,1,0:T(8,128)(2,1)S(1)} %bitcast.324, ...), kind=kOutput, calls=%fused_computation.13 | convolution fusion | flops 4440195072 | bytes 48279552 | tf_op jit(solution)/shard_map/sk,tkc->tsc/dot_general | solution.py:796
  578.5 9.1 fusion.67
  589.9 16.3 %fusion.22 = (f32[4,1024]{1,0:T(4,128)S(1)}, bf16[4,512,1024]{1,2,0:T(8,128)(2,1)S(1)}, f32[4,1024]{1,0:T(4,128)S(1)}, bf16[4,512,1024]{1,2,0:T(8,128)(2,1)S(1)}) fusion(f32[4,512,1024]{1,2,0:T(8,128)} %get-tuple-element.58, f32[4,512,1024]{1,2,0:T(8,128)} %get-tuple-element.59, f32[4,1024,512]{2,1,0:T(8,128)} %get-tuple-element.105, ...), kind=kOutput, calls=%fused_computation.40 | convolution fusion | flops 4343193600 | bytes 51445760 | tf_op jit(solution)/shard_map/sd,tcd->tsc/dot_general | solution.py:815
  606.3 9.9 fusion.54
  616.3 8.2 multiply_reduce_fusion
  632.1 6.2 copy.142
  668.5 7.6 fusion.30.refs_2_
  676.1 5.7 fusion.69
  681.8 5.7 fusion.52
  687.5 5.7 fusion.70
  693.1 5.7 fusion.50
  708.0 61.5 %attention_grad.1 = (f32[4,2048,64]{2,1,0:T(8,128)S(1)}, f32[4,2048,64]{2,1,0:T(8,128)S(1)}, f32[4,2048,64]{2,1,0:T(8,128)S(1)}) custom-call(bf16[4,2048,64]{2,1,0:T(8,128)(2,1)S(1)} %copy-done.6, bf16[4,2048,64]{2,1,0:T(8,128)(2,1)S(1)} %copy-done.4, bf16[4,2048,64]{2,1,0:T(8,128)(2,1)S(1)} %bitcast.278, f32[4,2048,64]{2,1,0:T(8,128)} %copy-done.1, ...), custom_call_target="tpu_custom_call" | custom-call | flops 8000000000 | bytes 16777216 | tf_op jit(solution)/shard_map/attention_grad/pallas_call | solution.py:737
  769.5 7.4 multiply_subtract_fusion.1
  788.4 5.2 copy.137
  793.6 6.6 fusion
  800.4 5.1 fusion.68
  811.5 5.7 fusion.28.refs_5_
  817.2 336.6 %sums.1 = (f32[8,2048,128]{2,1,0:T(8,128)}, f32[6,64,1024]{2,1,0:T(8,128)}, f32[24,4,64,1024]{3,2,1,0:T(8,128)}) custom-call(f32[2048,1024]{1,0:T(8,128)} %copy-done.36, f32[4,4,128,1024]{3,2,1,0:T(8,128)} %bitcast.283, f32[4,4,128,1024]{3,2,1,0:T(8,128)} %bitcast.282, f32[4,4,128,1024]{3,2,1,0:T(8,128)} %fusion.30.refs_2_, f32[4,4,128,1024]{3,2,1,0:T(8,128)} %bitcast.285, ...), custom_call_target="tpu_custom_call" | custom-call | flops 20000000000 | bytes 104857600 | tf_op jit(solution)/shard_map/sums/pallas_call | solution.py:506
  1157.8 7.3 fusion.71
  1165.2 33.4 %table_rows.1.block_in = f32[7648,128]{1,0:T(8,128)S(1)} custom-call(s32[16384]{0:T(1024)S(1)} %and_select_fusion.ids, f32[16384,128]{1,0:T(8,128)} %bitcast.281), custom_call_target="tpu_custom_call" | custom-call | flops 3000000000 | bytes 16777216 | tf_op jit(solution)/shard_map/table_rows/pallas_call | solution.py:552
  1200.4 188.3 %gathered_columns.1 = f32[7648,1024]{1,0:T(8,128)} custom-call(f32[7648,128]{1,0:T(8,128)} %copy-done.2), custom_call_target="tpu_custom_call" | custom-call | flops 10000000000 | bytes 62914560 | tf_op jit(solution)/shard_map/gathered_columns/pallas_call | solution.py:628
  1393.2 13.6 all-reduce.4.cloned.1.call-done
  1406.8 22.4 %copy.190 = f32[7648,1024]{1,0:T(8,128)} copy(f32[7648,1024]{1,0:T(8,128)} %gathered_columns.1) | data formatting | bytes 62652416
  (224 shorter events, 137.8 us)
Async XLA Ops:
  19.7 392.3 %copy-start.19 = (f32[2048,32]{1,0:T(8,128)}, f32[2048,32]{1,0:T(8,128)S(1)}, u32[]{:S(2)}) copy-start(f32[2048,32]{1,0:T(8,128)S(1)} %get-tuple-element.102) | copy-start | bytes 786436
  43.9 346.4 %copy-start.46 = (bf16[1024,768]{1,0:T(8,128)(2,1)S(1)}, bf16[1024,768]{1,0:T(8,128)(2,1)}, u32[]{:S(2)}) copy-start(bf16[1024,768]{1,0:T(8,128)(2,1)} %param.23) | copy-start | bytes 4718596
  400.1 18.3 %copy-start.7 = (bf16[2048,4,1,64]{3,0,1,2:T(8,128)(2,1)}, bf16[2048,4,1,64]{3,0,1,2:T(8,128)(2,1)S(1)}, u32[]{:S(2)}) copy-start(bf16[2048,4,1,64]{3,0,1,2:T(8,128)(2,1)S(1)} %copy.173) | copy-start | bytes 3145732
  417.2 51.4 %copy-start.3 = (bf16[4,2048,64]{2,1,0:T(8,128)(2,1)}, bf16[4,2048,64]{2,1,0:T(8,128)(2,1)S(1)}, u32[]{:S(2)}) copy-start(bf16[4,2048,64]{2,1,0:T(8,128)(2,1)S(1)} %maximum_bitcast_fusion.3.k_ref) | copy-start | bytes 3145732
  418.4 50.2 %copy-start.5 = (bf16[4,2048,64]{2,1,0:T(8,128)(2,1)}, bf16[4,2048,64]{2,1,0:T(8,128)(2,1)S(1)}, u32[]{:S(2)}) copy-start(bf16[4,2048,64]{2,1,0:T(8,128)(2,1)S(1)} %maximum_bitcast_fusion.2.q_ref) | copy-start | bytes 3145732
  480.8 10.2 copy-start.38
  480.8 10.2 copy-start.39
  480.8 10.9 copy-start.40
  480.8 10.9 copy-start.41
  480.8 10.9 copy-start.42
  480.8 10.9 copy-start.43
  480.8 10.9 copy-start.44
  486.1 50.4 %all-to-all-start = ((f32[4,512,256]{2,1,0:T(8,128)}), f32[4,512,256]{2,1,0:T(8,128)S(1)}, u32[]{:S(2)}, u32[]{:S(2)}) async-start(f32[4,512,256]{2,1,0:T(8,128)} %reshape.442), calls=%async_computation | async-start | bytes 4194304 | tf_op jit(solution)/shard_map/all_to_all | solution.py:788
  489.8 327.4 %reduce-scatter.2.cloned.1.call-start = ((), (), s32[]{:S(2)}) async-start(), calls=%async_computation.5 | async-start | bytes 4325376 | tf_op jit(solution)/shard_map/reduce_scatter | solution.py:829
  540.3 8.7 slice-start
  541.0 8.1 slice-start.1
  578.5 9.1 copy-start.24
  578.5 9.4 copy-start.35
  589.9 16.3 %copy-start.32 = (bf16[512,1024]{1,0:T(8,128)(2,1)}, bf16[512,1024]{1,0:T(8,128)(2,1)S(1)}, u32[]{:S(2)}) copy-start(bf16[512,1024]{1,0:T(8,128)(2,1)S(1)} %get-tuple-element.78) | copy-start | bytes 3145732
  606.3 10.0 copy-start.14
  606.3 10.0 copy-start.16
  646.8 56.3 %all-to-all-start.1 = ((f32[4,512,256]{2,1,0:T(8,128)}), f32[4,512,256]{2,1,0:T(8,128)S(1)}, u32[]{:S(2)}, u32[]{:S(2)}) async-start(f32[4,512,256]{2,1,0:T(8,128)} %convolution_bitcast_fusion), calls=%async_computation.1 | async-start | bytes 4194304 | tf_op jit(solution)/shard_map/all_to_all | solution.py:831
  650.6 738.3 %all-reduce.6.cloned.1.call-start = ((), (), s32[]{:S(2)}) async-start(), calls=%async_computation.4 | async-start | bytes 196608 | tf_op jit(solution)/shard_map/psum | solution.py:852
  668.5 7.6 copy-start.17
  708.0 61.5 %copy-start.20 = (f32[2048,32]{1,0:T(8,128)S(1)}, f32[2048,32]{1,0:T(8,128)}, u32[]{:S(2)}) copy-start(f32[2048,32]{1,0:T(8,128)} %copy-done.19) | copy-start | bytes 786436
  769.5 13.3 copy-start
  811.4 581.7 %all-gather.5.cloned.1.call-start = ((), (), s32[]{:S(2)}) async-start(), calls=%async_computation.6 | async-start | bytes 1179648 | tf_op jit(solution)/shard_map/all_gather | solution.py:829
  817.2 575.9 %all-gather.9.cloned.1.call-start = ((), (), s32[]{:S(2)}) async-start(), calls=%async_computation.8 | async-start | bytes 4718592 | tf_op jit(solution)/shard_map/all_gather | solution.py:844
  1156.5 236.6 %all-gather.11.cloned.1.call-start = ((), (), s32[]{:S(2)}) async-start(), calls=%async_computation.9 | async-start | bytes 4718592 | tf_op jit(solution)/shard_map/all_gather | solution.py:844
  1157.1 236.0 %all-gather.7.cloned.1.call-start = ((), (), s32[]{:S(2)}) async-start(), calls=%async_computation.7 | async-start | bytes 4718592 | tf_op jit(solution)/shard_map/all_gather | solution.py:844
  1157.7 249.1 %all-reduce.4.cloned.1.call-start = ((), (), s32[]{:S(2)}) async-start(), calls=%async_computation.3 | async-start | bytes 6291456 | tf_op jit(solution)/shard_map/psum | solution.py:839
  1406.8 22.4 %copy-start.26 = (f32[1024,768]{1,0:T(8,128)S(1)}, f32[1024,768]{1,0:T(8,128)}, u32[]{:S(2)}) copy-start(f32[1024,768]{1,0:T(8,128)} %all-reduce.4.cloned.1.call-done) | copy-start | bytes 9437188
  (29 other events, 111.3 us)
Sparse Core Ops, SparseCore 0:
  632.2 142.9 reduce-scatter.1
  811.5 129.2 all-reduce.5
  942.7 27.0 all-gather.4
  1156.6 42.7 all-gather.8
  1201.8 53.8 all-gather.10
  1258.0 53.8 all-gather.6
  1315.7 91.0 all-reduce.3
where the time goes:
time: 1460 us; the launch traced here: 1450 us
  Pallas kernels  1020 us (70%)
  matrix products  145 us (10%)
  local copies, waits for them, and re-layouts  144 us (10%)
  waiting for transfers between devices  62.3 us (4%)
  other arithmetic  58.9 us (4%)
  between operations  16 us (1%)
    pallas_call x1, Pallas kernels, embed(): pl.pallas_call(functools.partial(emb_kernel, n_tp, rows, chunks, cuts), n...  346 us
    pallas_call x1, Pallas kernels, sums(): pl.pallas_call(functools.partial(sums_kernel, n_tp, rows, chunks, jobs),...  337 us
    pallas_call x1, Pallas kernels, gathered_columns(): pl.pallas_call(functools.partial(gather_kernel, parts), name='gathered_co...  188 us
    pallas_call x1, Pallas kernels, attention_grad(): pl.pallas_call(functools.partial(attention_grad_kernel, dim ** (-0.5), kb...  61.5 us
    unnamed x115, local copies, waits for them, and re-layouts  56.5 us
    pallas_call x1, Pallas kernels, attention(): pl.pallas_call(functools.partial(attention_kernel, dim ** (-0.5), kb), na...  50.2 us
    all_to_all x1, waiting for transfers between devices, device_step(): ctx_own = (lax.all_to_all(context, 'tp', N0, N0) + zero).astype(BF)  43.1 us
    dot_general x6, matrix products, products(): jnp.einsum(spec, chosen, rhs, preferred_element_type=F32)  36 us
  transfers between devices with their start and end apart: 9, of which 3 were waited for; matrix products, arithmetic and copies ran while one was open for 9% of the time, Pallas kernels for 43%

commit v1 on v0

--- a/solution.py
+++ b/solution.py
@@ -2,6 +2,7 @@
 
 import jax
 import jax.numpy as jnp
+import numpy as np
 from jax import lax
 from jax.experimental import pallas as pl
 from jax.experimental.pallas import tpu as pltpu
@@ -32,18 +33,16 @@
     return jax.nn.gelu(gate_pre, approximate=False) * lin_pre
 
 
-def rope_tables(seq_len, head_dim):
+def rope_tables(seq_len, head_dim, heads):
     half_dim = head_dim // 2
-    inv_freq = ROPE_BASE ** (-2.0 * jnp.arange(half_dim, dtype=F32) / head_dim)
-    angles = jnp.arange(seq_len, dtype=F32)[:, None] * inv_freq[None, :]
-    return jnp.cos(angles)[:, None, :], jnp.sin(angles)[:, None, :]
-
-
-def apply_rope(values, cos_tab, sin_tab):
-    half_dim = values.shape[-1] // 2
-    first_half = values[..., :half_dim]
-    second_half = values[..., half_dim:]
-    return jnp.concatenate([first_half * cos_tab - second_half * sin_tab, second_half * cos_tab + first_half * sin_tab], axis=-1)
+    inv_freq = (ROPE_BASE ** (-2.0 * np.arange(half_dim) / head_dim)).astype(np.float32)
+    angles = np.arange(seq_len, dtype=np.float32)[:, None] * inv_freq[None, :]
+    return [jnp.asarray(np.tile(table(angles), (1, heads))) for table in (np.cos, np.sin)]
+
+
+def column_order(heads, head_dim):
+    cols = np.arange(3 * heads * head_dim).reshape(heads, 3, 2, head_dim // 2)
+    return np.concatenate([cols[:, part].transpose(1, 0, 2).ravel() for part in (0, 1)] + [cols[:, 2].ravel()])
 
 
 def rcopy(src, dst, send, recv, **where):
@@ -66,23 +65,9 @@
     bar = pltpu.get_barrier_semaphore()
     for rel in range(1, 8):
         pl.semaphore_signal(bar, inc=1, device_id={'dp': at(rel)}, device_id_type=MESH)
-
-    @pl.when(z > 0)
-    def _():
-        pl.semaphore_signal(bar, inc=1, device_id={'tp': z - 1}, device_id_type=MESH)
-
-    @pl.when(z < n - 1)
-    def _():
-        pl.semaphore_signal(bar, inc=1, device_id={'tp': z + 1}, device_id_type=MESH)
-    inner = (z > 0) & (z < n - 1)
-
-    @pl.when(inner)
-    def _():
-        pl.semaphore_wait(bar, 9)
-
-    @pl.when(jnp.logical_not(inner))
-    def _():
-        pl.semaphore_wait(bar, 8)
+    for d in range(1, n):
+        pl.semaphore_signal(bar, inc=1, device_id={'tp': (z + d) % n}, device_id_type=MESH)
+    pl.semaphore_wait(bar, 7 + n - 1)
 
 
 LAG = 3
@@ -170,10 +155,13 @@
 ORDER = (0, 2, 4, 1, 3, 5, 6, 7)
 
 
-def emb_kernel(n, rows, chunks, cuts, part, piece, toks, *refs):
+def emb_kernel(n, rows, chunks, cuts, heads, part, wq, bq, cos, sin, piece, toks, *refs):
     m = len(cuts)
     local, outs = refs[:m], refs[m + N1:N2 * m + N1]
-    out, (bias, tok_all, wall, left, right, raw, low, send_r, send_l, recv_l, recv_r, tsend, trecv, tself, zsend, zrecv, psend, precv, lsem, isem, osem, bsem) = refs[m], refs[N2 * m + N1:]
+    out, (bias, tok_all, wall, ctx_own, q, k_all, v, ctx, top, inv, left, right, raw, low, weights, send_r, send_l, recv_l, recv_r, tsend, trecv, tself, zsend, zrecv, psend, precv, lsem, isem, osem, bsem, asend, arecv, aself) = refs[m], refs[N2 * m + N1:]
+    blocks = 8
+    qb = part.shape[N0] // blocks
+    per = chunks // blocks
     z = lax.axis_index('tp')
     p, at = plane()
     entry_barrier(z, n, at)
@@ -239,6 +227,8 @@
                     give(t, j)
         others(d, body)
 
+    k_all[...] = jnp.zeros_like(k_all)
+    v[...] = jnp.zeros_like(v)
     for d in range(N1, n):
         arrive(d)
 
@@ -275,12 +265,48 @@
     events = [(STEPS[d - N1], functools.partial(relay, d, CROSS)) for d in range(N1, n)] + [(STEPS[d + n - N2], functools.partial(relay, d, DIAGONAL)) for d in range(N1, n)]
     events += [(FIRST - N1, functools.partial(prefetch, N0))] + [(FIRST + s, functools.partial(convert, s)) for s in range(len(plan))]
 
-    @pl.loop(N0, max(chunks + LAG * (n - N1), FIRST + len(plan)))
+    start = per + LAG * (n - N1)
+
+    def context(i):
+        src = ctx.at[pl.ds(pl.multiple_of(i * qb, qb), qb)]
+        to = i // (blocks // n)
+        dst = ctx_own.at[z, pl.ds(pl.multiple_of((i % (blocks // n)) * qb, qb), qb)]
+        return to, pltpu.make_async_copy(src, dst, aself), rcopy(src, dst, asend, arecv.at[z], tp=to)
+
+    @pl.loop(N0, max(start + blocks * heads + N1, FIRST + len(plan)))
     def _(k):
+        step = k - start
+        i = step // heads - N1
+
+        @pl.when((step > N0) & (step % heads == N0) & (step <= blocks * heads))
+        def _():
+            to, local_copy, remote = context(i)
+
+            @pl.when(to == z)
+            def _():
+                local_copy.start()
+
+            @pl.when(to != z)
+            def _():
+                remote.start()
         chain_sum(k, z, n, rows, chunks, part, left, right, done, send_r, send_l, recv_l, recv_r)
         for at_step, event in events:
             pl.when(k == at_step)(event)
 
+        @pl.when((step >= N0) & (step < blocks * heads))
+        def _():
+            @pl.when(step % heads == N0)
+            def _():
+                project(step // heads, qb, out, wq, bq, cos, sin, q, k_all, v)
+            attend(step // heads, step % heads, heads, qb, q, k_all, v, ctx, top, inv, weights)
+
+    kept = blocks // n
+    pltpu.make_async_copy(ctx.at[pl.ds(N0, kept * qb)], ctx_own.at[z], aself).wait()
+    rest = ctx.at[pl.ds(N0, (blocks - kept) * qb)]
+    rcopy(rest, rest, asend, arecv.at[z], tp=z).wait_send()
+    for d in range(N1, n):
+        src = (z + d) % n
+        rcopy(ctx_own.at[src], ctx_own.at[src], asend, arecv.at[src], tp=z).wait_recv()
     chain_drain(z, n, part, left, right, send_r, send_l, recv_l, recv_r)
     for s in (len(plan) - N2, len(plan) - N1):
         for copy in stored(*plan[s], s % N2):
@@ -312,30 +338,35 @@
         rcopy(piece, wall.at[z, p], bsem.at[N1], zrecv.at[z], tp=z - N1).wait_send()
 
 
-def embed(part, piece, toks, local, n_tp, n_dp):
+def embed(part, piece, toks, local, wq, bq, cos, sin, heads, n_tp, n_dp):
     seq, width = part.shape
-    rows = min(64, seq // 4)
-    chunks = seq // rows
+    chunks = 32
+    rows = seq // chunks
+    dims = wq.shape[1] // 3
     cuts, lo = [], 0
     for weight in local:
         cuts.append((lo, lo + weight.shape[0] // n_dp))
         lo = cuts[-1][1]
     dma = pltpu.SemaphoreType.DMA
-    shapes = [jax.ShapeDtypeStruct((seq, width), BF)]
-    shapes += [jax.ShapeDtypeStruct((n_tp, n_dp, w.shape[0] // n_dp, w.shape[1]), BF) for w in local]
-    shapes += [jax.ShapeDtypeStruct((n_tp, piece.shape[0] - lo, width), F32), jax.ShapeDtypeStruct((n_dp,) + toks.shape, toks.dtype), jax.ShapeDtypeStruct((n_tp, n_dp) + piece.shape, F32)]
+    shape = jax.ShapeDtypeStruct
+    shapes = [shape((seq, width), BF)]
+    shapes += [shape((n_tp, n_dp, w.shape[0] // n_dp, w.shape[1]), BF) for w in local]
+    shapes += [shape((n_tp, piece.shape[0] - lo, width), F32), shape((n_dp,) + toks.shape, toks.dtype), shape((n_tp, n_dp) + piece.shape, F32), shape((n_tp, seq // n_tp, dims), F32)]
+    shapes += [shape((seq, dims), BF)] * 3 + [shape((seq, dims), F32)] + [shape((heads, seq), F32)] * 2
     out = pl.pallas_call(
-        functools.partial(emb_kernel, n_tp, rows, chunks, cuts),
+        functools.partial(emb_kernel, n_tp, rows, chunks, cuts, heads),
         name='embed',
         out_shape=shapes,
-        in_specs=[VMEM] + [ANY] * (2 + len(local)),
-        out_specs=[VMEM] + [ANY] * (len(shapes) - 1),
-        scratch_shapes=[pltpu.VMEM((seq, width), F32)] * 2 + [pltpu.VMEM((2, lo, width), F32), pltpu.VMEM((2, lo, width), BF), dma, dma, dma((chunks,)), dma((chunks,)),
-                        dma((8,)), dma((8,)), dma, dma((n_tp,)), dma((n_tp,)), dma((n_tp, len(EDGES))), dma((n_tp, len(EDGES))), dma((len(local),)), dma((2,)), dma((2, len(local))), dma((2,))],
-        compiler_params=pltpu.CompilerParams(collective_id=0, has_side_effects=True, vmem_limit_bytes=56 * 2 ** 20),
+        in_specs=[VMEM] * 5 + [ANY] * (2 + len(local)),
+        out_specs=[VMEM] + [ANY] * (4 + len(local)) + [VMEM] * 6,
+        scratch_shapes=[pltpu.VMEM((seq, width), F32)] * 2 + [pltpu.VMEM((2, lo, width), F32), pltpu.VMEM((2, lo, width), BF), pltpu.VMEM((seq, seq // 8), F32), dma, dma, dma((chunks,)), dma((chunks,)),
+                        dma((8,)), dma((8,)), dma, dma((n_tp,)), dma((n_tp,)), dma((n_tp, len(EDGES))), dma((n_tp, len(EDGES))), dma((len(local),)), dma((2,)), dma((2, len(local))), dma((2,)),
+                        dma, dma((n_tp,)), dma],
+        compiler_params=pltpu.CompilerParams(collective_id=0, has_side_effects=True, vmem_limit_bytes=60 * 2 ** 20),
         cost_estimate=pl.CostEstimate(flops=20 * 10 ** 9, bytes_accessed=80 * 2 ** 20, transcendentals=0),
-    )(part, piece, toks, *[w.reshape(n_dp, w.shape[0] // n_dp, w.shape[1]) for w in local])
-    return out[0], [w.reshape(n_tp, -1, w.shape[3]) for w in out[1:-3]], out[-3], out[-2]
+    )(part, wq, bq, cos, sin, piece, toks, *[w.reshape(n_dp, w.shape[0] // n_dp, w.shape[1]) for w in local])
+    m = 1 + len(local)
+    return out[0], [w.reshape(n_tp, -1, w.shape[3]) for w in out[1:m]], out[m], out[m + 1], out[m + 3], out[m + 4:]
 
 
 RING = 8
@@ -644,106 +675,126 @@
 NT, TN, NN = ((1,), (1,)), ((0,), (0,)), ((1,), (0,))
 
 
-def attention_kernel(scale, kb, q_ref, k_ref, v_ref, ctx_ref, m_ref, l_ref, s_ref):
-    i = pl.program_id(1)
-    qb = q_ref.shape[1]
-    q = q_ref[0]
-    blocks = ((i + 1) * qb + kb - 1) // kb
-
-    def scores(j, top):
-        at_k = pl.ds(pl.multiple_of(j * kb, kb), kb)
-        s = dot(k_ref[0, at_k, :], q, NT) * scale
-        key = j * kb + lax.broadcasted_iota(jnp.int32, (kb, qb), 0)
-        query = i * qb + lax.broadcasted_iota(jnp.int32, (kb, qb), 1)
-        s = jnp.where(query >= key, s, -1e30)
-        s_ref[at_k, :] = s
+def lane_head(shape, heads, halves):
+    lane = lax.broadcasted_iota(jnp.int32, shape, 1)
+    dims = shape[1] // halves
+    return (lane % dims) // (dims // heads)
+
+
+def turned(both, cos, sin):
+    half = both.shape[1] // 2
+    x1, x2 = both[:, :half], both[:, half:]
+    return jnp.concatenate([x1 * cos - x2 * sin, x2 * cos + x1 * sin], axis=1)
+
+
+def project(i, qb, emb, wq, bq, cos, sin, q, k, v):
+    at_q = pl.ds(pl.multiple_of(i * qb, qb), qb)
+    dims = q.shape[1]
+    qkv = (dot(emb[at_q, :], wq[...], NN) + bq[...]).astype(BF)
+    for ref, part in ((q, 0), (k, 1)):
+        ref[at_q, :] = turned(qkv[:, part * dims:(part + 1) * dims].astype(F32), cos[at_q, :], sin[at_q, :]).astype(BF)
+    v[at_q, :] = qkv[:, 2 * dims:]
+
+
+def scores(i, j, kb, qb, scale, keys, q):
+    s = dot(keys, q, NT) * scale
+    key = j * kb + lax.broadcasted_iota(jnp.int32, (kb, qb), 0)
+    query = i * qb + lax.broadcasted_iota(jnp.int32, (kb, qb), 1)
+    return jnp.where(query >= key, s, -1e30)
+
+
+def attend(i, h, heads, qb, q_ref, k_ref, v_ref, ctx_ref, top_ref, inv_ref, s_ref):
+    kb = 2 * qb
+    dims = q_ref.shape[1]
+    scale = (dims // heads) ** -0.5
+    at_q = pl.ds(pl.multiple_of(i * qb, qb), qb)
+    q = jnp.where(lane_head((qb, dims), heads, 2) == h, q_ref[at_q, :].astype(F32), 0.0).astype(BF)
+    count = (i + 2) // 2
+
+    def at_key(j):
+        return pl.ds(pl.multiple_of(j * kb, kb), kb)
+
+    def first(j, top):
+        s = scores(i, j, kb, qb, scale, k_ref[at_key(j), :], q)
+        s_ref[at_key(j), :] = s
         return jnp.maximum(top, jnp.max(s, axis=0, keepdims=True))
-    top = lax.fori_loop(0, blocks, scores, jnp.full((1, qb), -1e30, F32))
+    top = lax.fori_loop(0, count, first, jnp.full((1, qb), -1e30, F32))
 
     def weigh(j, total):
-        at_k = pl.ds(pl.multiple_of(j * kb, kb), kb)
-        e = jnp.exp(s_ref[at_k, :] - top)
-        s_ref[at_k, :] = e
+        e = jnp.exp(s_ref[at_key(j), :] - top)
+        s_ref[at_key(j), :] = e
         return total + jnp.sum(e, axis=0, keepdims=True)
-    total = lax.fori_loop(0, blocks, weigh, jnp.zeros((1, qb), F32))
-    inv = 1.0 / total
+    inv = 1.0 / lax.fori_loop(0, count, weigh, jnp.zeros((1, qb), F32))
 
     def mix(j, acc):
-        at_k = pl.ds(pl.multiple_of(j * kb, kb), kb)
-        probs = (s_ref[at_k, :] * inv).astype(BF)
-        return acc + dot(probs, v_ref[0, at_k, :], TN)
-    ctx_ref[0] = lax.fori_loop(0, blocks, mix, jnp.zeros((qb, v_ref.shape[2]), F32))
-    m_ref[0] = top
-    l_ref[0] = inv
-
-
-def attention(q, k, v):
-    heads, seq, dim = q.shape
-    qb, kb = seq // 8, seq // 4
-    spec_q = pl.BlockSpec((1, qb, dim), lambda h, i: (h, i, 0))
-    spec_k = pl.BlockSpec((1, seq, dim), lambda h, i: (h, 0, 0))
-    spec_s = pl.BlockSpec((1, 1, qb), lambda h, i: (h, 0, i))
-    stat = jax.ShapeDtypeStruct((heads, 1, seq), F32)
-    return pl.pallas_call(
-        functools.partial(attention_kernel, dim ** -0.5, kb),
-        name='attention',
-        grid=(heads, seq // qb),
-        in_specs=[spec_q, spec_k, spec_k],
-        out_specs=(spec_q, spec_s, spec_s),
-        out_shape=(jax.ShapeDtypeStruct((heads, seq, dim), F32), stat, stat),
-        scratch_shapes=[pltpu.VMEM((seq, qb), F32)],
-        compiler_params=pltpu.CompilerParams(dimension_semantics=('arbitrary', 'arbitrary'), vmem_limit_bytes=32 * 2 ** 20),
-        cost_estimate=pl.CostEstimate(flops=3 * 10 ** 9, bytes_accessed=8 * 2 ** 20, transcendentals=10 ** 7),
-    )(q, k, v)
-
-
-def attention_grad_kernel(scale, kb, q_ref, k_ref, v_ref, c_ref, dc_ref, m_ref, l_ref, dq_ref, dk_ref, dv_ref):
-    i = pl.program_id(1)
-    qb = q_ref.shape[1]
-    q, dc = q_ref[0], dc_ref[0]
-    dc_f = dc.astype(F32)
-    top, inv = m_ref[0], l_ref[0]
-    ones = jnp.ones((8, dc.shape[1]), F32)
-    mean = lax.dot_general(ones, dc_f * c_ref[0], (NT, ((), ())), precision=lax.Precision.HIGHEST, preferred_element_type=F32)[:1]
-    blocks = ((i + 1) * qb + kb - 1) // kb
-
-    @pl.when(i == 0)
-    def _():
-        dk_ref[...] = jnp.zeros_like(dk_ref)
-        dv_ref[...] = jnp.zeros_like(dv_ref)
+        return acc + dot((s_ref[at_key(j), :] * inv).astype(BF), v_ref[at_key(j), :], TN)
+    mixed = lax.fori_loop(0, count, mix, jnp.zeros((qb, dims), F32))
+    ctx_ref[at_q, :] = jnp.where(lane_head((qb, dims), heads, 1) == h, mixed, ctx_ref[at_q, :])
+    top_ref[pl.ds(h, 1), at_q] = top
+    inv_ref[pl.ds(h, 1), at_q] = inv
+
+
+def attend_grad(i, h, heads, qb, q_ref, k_ref, v_ref, ctx_ref, dctx_ref, top_ref, inv_ref, dq_ref, dk_ref, dv_ref):
+    kb = 2 * qb
+    dims = q_ref.shape[1]
+    scale = (dims // heads) ** -0.5
+    at_q = pl.ds(pl.multiple_of(i * qb, qb), qb)
+    q = jnp.where(lane_head((qb, dims), heads, 2) == h, q_ref[at_q, :].astype(F32), 0.0).astype(BF)
+    dc = jnp.where(lane_head((qb, dims), heads, 1) == h, dctx_ref[at_q, :], 0.0).astype(BF)
+    ones = jnp.ones((8, dims), F32)
+    mean = lax.dot_general(ones, dc.astype(F32) * ctx_ref[at_q, :], (NT, ((), ())), precision=lax.Precision.HIGHEST, preferred_element_type=F32)[:1]
+    top, inv = top_ref[pl.ds(h, 1), at_q], inv_ref[pl.ds(h, 1), at_q]
 
     def step(j, dq):
         at_k = pl.ds(pl.multiple_of(j * kb, kb), kb)
-        keys = k_ref[0, at_k, :]
-        s = dot(keys, q, NT) * scale
-        key = j * kb + lax.broadcasted_iota(jnp.int32, (kb, qb), 0)
-        query = i * qb + lax.broadcasted_iota(jnp.int32, (kb, qb), 1)
-        probs = (jnp.exp(jnp.where(query >= key, s, -1e30) - top) * inv).astype(BF)
-        d_probs = dot(v_ref[0, at_k, :], dc, NT)
-        ds = (probs.astype(F32) * (d_probs - mean) * scale).astype(BF)
-        dv_ref[0, at_k, :] += dot(probs, dc, NN)
-        dk_ref[0, at_k, :] += dot(ds, q, NN)
+        keys = k_ref[at_k, :]
+        probs = (jnp.exp(scores(i, j, kb, qb, scale, keys, q) - top) * inv).astype(BF)
+        ds = (probs.astype(F32) * (dot(v_ref[at_k, :], dc, NT) - mean) * scale).astype(BF)
+        dv_ref[at_k, :] += dot(probs, dc, NN)
+        dk_ref[at_k, :] += dot(ds, q, NN)
         return dq + dot(ds, keys, TN)
-    dq_ref[0] = lax.fori_loop(0, blocks, step, jnp.zeros((qb, q.shape[1]), F32))
-
-
-def attention_grad(q, k, v, ctx, dctx, top, inv):
-    heads, seq, dim = q.shape
-    qb, kb = seq // 8, seq // 4
-    spec_q = pl.BlockSpec((1, qb, dim), lambda h, i: (h, i, 0))
-    spec_k = pl.BlockSpec((1, seq, dim), lambda h, i: (h, 0, 0))
-    spec_s = pl.BlockSpec((1, 1, qb), lambda h, i: (h, 0, i))
-    out = jax.ShapeDtypeStruct((heads, seq, dim), F32)
+    dq = lax.fori_loop(0, (i + 2) // 2, step, jnp.zeros((qb, dims), F32))
+    dq_ref[...] = jnp.where(lane_head((qb, dims), heads, 2) == h, dq, dq_ref[...])
+
+
+def grad_rows(i, qb, cos, sin, dq, dk, dv, d_bias):
+    at_q = pl.ds(pl.multiple_of(i * qb, qb), qb)
+    back = [turned(values, cos[at_q, :], -sin[at_q, :]) for values in (dq[...], dk[at_q, :])]
+    rows = jnp.concatenate(back + [dv[at_q, :]], axis=1)
+    d_bias[...] += jnp.sum(rows, axis=0, keepdims=True)
+    return rows.astype(BF)
+
+
+def attention_grad_kernel(heads, q, k, v, ctx, dctx, top, inv, cos, sin, d_qkv, d_bias, dq, dk, dv):
+    blocks = 8
+    qb = q.shape[0] // blocks
+    dk[...] = jnp.zeros_like(dk)
+    dv[...] = jnp.zeros_like(dv)
+    d_bias[...] = jnp.zeros_like(d_bias)
+
+    @pl.loop(0, blocks)
+    def _(step):
+        i = blocks - 1 - step
+
+        @pl.loop(0, heads)
+        def _(h):
+            attend_grad(i, h, heads, qb, q, k, v, ctx, dctx, top, inv, dq, dk, dv)
+        d_qkv[pl.ds(pl.multiple_of(i * qb, qb), qb), :] = grad_rows(i, qb, cos, sin, dq, dk, dv, d_bias)
+
+
+def attention_grad(saved, dctx, cos, sin, heads):
+    q, k, v, ctx, top, inv = saved
+    seq, dims = q.shape
     return pl.pallas_call(
-        functools.partial(attention_grad_kernel, dim ** -0.5, kb),
+        functools.partial(attention_grad_kernel, heads),
         name='attention_grad',
-        grid=(heads, seq // qb),
-        in_specs=[spec_q, spec_k, spec_k, spec_q, spec_q, spec_s, spec_s],
-        out_specs=(spec_q, spec_k, spec_k),
-        out_shape=(out, out, out),
-        compiler_params=pltpu.CompilerParams(dimension_semantics=('arbitrary', 'arbitrary'), vmem_limit_bytes=32 * 2 ** 20),
+        in_specs=[VMEM] * 9,
+        out_specs=(VMEM, VMEM),
+        out_shape=(jax.ShapeDtypeStruct((seq, 3 * dims), BF), jax.ShapeDtypeStruct((1, 3 * dims), F32)),
+        scratch_shapes=[pltpu.VMEM((seq // 8, dims), F32), pltpu.VMEM((seq, dims), F32), pltpu.VMEM((seq, dims), F32)],
+        compiler_params=pltpu.CompilerParams(vmem_limit_bytes=48 * 2 ** 20),
         cost_estimate=pl.CostEstimate(flops=8 * 10 ** 9, bytes_accessed=16 * 2 ** 20, transcendentals=10 ** 7),
-    )(q, k, v, ctx, dctx, top, inv)
+    )(q, k, v, ctx, dctx, top, inv, cos, sin)
 
 
 def solution(mesh):
@@ -760,7 +811,6 @@
         own = seq_len // n_tp
         ffn = w_gate.shape[N1]
         rk, rf, ro = width // n_dp, ffn // n_dp, w_out.shape[N0] // n_dp
-        zero = jnp.minimum(tokens[N0], N0).astype(F32)
 
         def cut(weight):
             rows = weight.shape[N0] // n_dp
@@ -773,19 +823,16 @@
         in_shard = (local_ids >= N0) & (local_ids < vocab_loc)
         safe_ids = jnp.where(in_shard, local_ids, N0)
         own_rows = jnp.where(in_shard[:, None], jnp.take(emb_table, safe_ids, axis=N0), 0.0).astype(F32)
-        emb_bf, (wg_full, wl_full, wd_full, wo_full), biases, tok_all = embed(own_rows, piece, tokens.reshape(-N1, min(128, seq_len // 8)), (w_gate, w_lin, w_down, w_out), n_tp, n_dp)
+        dims = heads * head_dim
+        place = column_order(heads, head_dim)
+        swap = (jnp.arange(3 * dims)[:, None] == jnp.asarray(place)[None, :]).astype(BF)
+        wq = jnp.dot(w_qkv, swap, preferred_element_type=F32).astype(BF)
+        bq = jnp.dot(b_qkv.reshape(N1, -1), swap, preferred_element_type=F32)
+        cos_tab, sin_tab = rope_tables(seq_len, head_dim, heads)
+        emb_bf, (wg_full, wl_full, wd_full, wo_full), biases, tok_all, ctx_own, saved = embed(own_rows, piece, tokens.reshape(-N1, min(128, seq_len // 8)), (w_gate, w_lin, w_down, w_out), wq, bq, cos_tab, sin_tab, heads, n_tp, n_dp)
+        ctx_own = ctx_own.astype(BF)
         is_own = (jnp.arange(n_tp) == tp)[:, None]
         bg_full, bl_full = [jnp.where(is_own, b[None].astype(F32), biases[:, i]) for i, b in enumerate((b_gate, b_lin))]
-
-        qkv_pre = jnp.dot(emb_bf, w_qkv, preferred_element_type=F32) + b_qkv.reshape(-N1).astype(F32)
-        qkv_all = qkv_pre.astype(BF).reshape(seq_len, heads, 3, head_dim)
-        cos_tab, sin_tab = rope_tables(seq_len, head_dim)
-        queries = apply_rope(qkv_all[:, :, N0].astype(F32), cos_tab, sin_tab).astype(BF).transpose(N1, N0, N2)
-        keys_rot = apply_rope(qkv_all[:, :, N1].astype(F32), cos_tab, sin_tab).astype(BF).transpose(N1, N0, N2)
-        values = qkv_all[:, :, N2].transpose(N1, N0, N2)
-        ctx, top, inv = attention(queries, keys_rot, values)
-        context = ctx.transpose(N1, N0, N2).reshape(n_tp, own, heads * head_dim)
-        ctx_own = (lax.all_to_all(context, 'tp', N0, N0) + zero).astype(BF)
 
         emb_own = lax.dynamic_slice_in_dim(emb_bf, tp * own, own, N0).astype(F32)
         cot_own = lax.dynamic_slice_in_dim(cotangent[N0], tp * own, own, N0).astype(F32)
@@ -828,16 +875,11 @@
         d_w_out = jnp.einsum('hse,sd->hed', ctx_own, d_attn_bf, preferred_element_type=F32)
         d_w_out = lax.all_gather(lax.psum_scatter(d_w_out.reshape(-N1, width), ALL, scatter_dimension=N0, tiled=True), 'dp', axis=N0, tiled=True)
         d_ctx = jnp.einsum('sd,hed->hse', d_attn_bf, wo_full, preferred_element_type=F32)
-        d_context = (lax.all_to_all(d_ctx, 'tp', N0, N0) + zero).astype(BF).reshape(seq_len, heads, head_dim).transpose(N1, N0, N2)
-
-        d_queries, d_keys, d_values = attention_grad(queries, keys_rot, values, ctx, d_context, top, inv)
-        d_queries = apply_rope(d_queries.transpose(N1, N0, N2), cos_tab, -sin_tab)
-        d_keys = apply_rope(d_keys.transpose(N1, N0, N2), cos_tab, -sin_tab)
-        d_qkv = jnp.stack([d_queries, d_keys, d_values.transpose(N1, N0, N2)], axis=N2).reshape(seq_len, -N1)
-        d_b_qkv = jnp.sum(d_qkv, axis=N0)
-        d_qkv_bf = d_qkv.astype(BF)
-        d_w_qkv = lax.psum(jnp.dot(emb_bf.T, d_qkv_bf, preferred_element_type=F32), 'dp')
-        d_emb_part = jnp.dot(d_qkv_bf, w_qkv.T, preferred_element_type=F32)
+        d_context = lax.all_to_all(d_ctx, 'tp', N0, N0).reshape(seq_len, dims)
+        d_qkv, d_b_qkv = attention_grad(saved, d_context, cos_tab, sin_tab, heads)
+        d_b_qkv = jnp.dot(d_b_qkv, swap.astype(F32).T, precision=lax.Precision.HIGHEST)[N0]
+        d_w_qkv = lax.psum(jnp.dot(emb_bf.T, jnp.dot(d_qkv, swap.T, preferred_element_type=F32).astype(BF), preferred_element_type=F32), 'dp')
+        d_emb_part = jnp.dot(d_qkv, wq.T, preferred_element_type=F32)
         d_emb_part = lax.dynamic_update_slice_in_dim(d_emb_part, lax.dynamic_slice_in_dim(d_emb_part, tp * own, own, N0) + ALPHA * d_resid_one, tp * own, N0)
         odd, even = zip(*[tuple(pair) for pair in (pair_gate, pair_lin, pair_down)])
         d_cols, mine = sums(d_emb_part, odd, even, n_tp, n_dp)

time: 1460 us -> 1370 us (0.938)
  waiting for transfers between devices: 62.3 us -> 8.43 us
  other arithmetic: 58.9 us -> 19.6 us
  local copies, waits for them, and re-layouts: 144 us -> 108 us
  starting transfers between devices: 7.63 us -> 29.4 us
    all_to_all x2 -> x1, waiting for transfers between devices: 47.5 us -> 0.01 us  [device_step(): d_context = lax.all_to_all(d_ctx, 'tp', N0, N0).reshape(seq_len, dims)]
    all_to_all x2 -> x1, starting transfers between devices: 7.35 us -> 29.1 us  [device_step(): d_context = lax.all_to_all(d_ctx, 'tp', N0, N0).reshape(seq_len, dims)]
    reshape x4 -> x0, local copies, waits for them, and re-layouts: 19.3 us -> none  [the longest x2 15.5 us: device_step(): context = ctx.transpose(N1, N0, N2).reshape(n_tp, own, heads * head_dim)]
    pallas_call x3 -> x2, Pallas kernels: 458 us -> 476 us  [the longest x1 401 us: embed(): pl.pallas_call(functools.partial(emb_kernel, n_tp, rows, chunks, cuts, he...]
    unnamed x115 -> x108, local copies, waits for them, and re-layouts: 56.5 us -> 44.6 us
  transfers between devices with their start and end apart: 9 -> 8, of which waited for: 3 -> 1; matrix products, arithmetic and copies ran while one was open for 9% -> 8% of each run, Pallas kernels for 43% -> 46%
where the time goes in v1:
time: 1370 us; the launch traced here: 1360 us
  Pallas kernels  1030 us (75%)
  matrix products  153 us (11%)
  local copies, waits for them, and re-layouts  108 us (8%)
  starting transfers between devices  29.4 us (2%)
  other arithmetic  19.6 us (1%)
  between operations  15.1 us (1%)
    pallas_call x1, Pallas kernels, embed(): pl.pallas_call(functools.partial(emb_kernel, n_tp, rows, chunks, cuts, he...  401 us
    pallas_call x1, Pallas kernels, sums(): pl.pallas_call(functools.partial(sums_kernel, n_tp, rows, chunks, jobs),...  331 us
    pallas_call x1, Pallas kernels, gathered_columns(): pl.pallas_call(functools.partial(gather_kernel, parts), name='gathered_co...  189 us
    pallas_call x1, Pallas kernels, attention_grad(): pl.pallas_call(functools.partial(attention_grad_kernel, heads), name='att...  74.8 us
    unnamed x108, local copies, waits for them, and re-layouts  44.6 us
    dot_general x6, matrix products, products(): jnp.einsum(spec, chosen, rhs, preferred_element_type=F32)  35.3 us
    pallas_call x1, Pallas kernels, table_rows(): pl.pallas_call(table_kernel, name='table_rows', grid_spec=pltpu.PrefetchS...  33.6 us
    dot_general x1, matrix products, device_step(): jnp.einsum('sk,tkc->tsc', hidden, wl_full, preferred_element_type=F32)  29.5 us
  transfers between devices with their start and end apart: 8, of which 1 were waited for; matrix products, arithmetic and copies ran while one was open for 8% of the time, Pallas kernels for 46%

profile of v1, /device:TPU:0, one launch (start us, length us, event | category | flops | bytes accessed | tf_op | source)
XLA Modules:
  0.0 1363.1 jit_solution(1010424447485137233)
XLA Ops:
  19.3 18.4 %gather_fusion = bf16[2048,1024]{1,0:T(8,128)(2,1)} fusion(bf16[7648,1024]{1,0:T(8,128)(2,1)} %param.25, s32[2048]{0:T(1024)S(1)} %broadcast_clamp_fusion), kind=kCustom, calls=%fused_computation.4 | custom fusion | bytes 8396800 | tf_op jit(solution)/shard_map/jit(_take)/gather | solution.py:825
  37.7 5.5 select_convert_fusion.part
  43.1 401.4 %embed.1 = (bf16[2048,1024]{1,0:T(8,128)(2,1)}, bf16[4,8,128,1024]{3,2,1,0:T(8,128)(2,1)}, bf16[4,8,128,1024]{3,2,1,0:T(8,128)(2,1)}, bf16[4,8,128,1024]{3,2,1,0...) custom-call(f32[2048,1024]{1,0:T(8,128)} %select_convert_fusion.part, ...), custom_call_target="tpu_custom_call" | custom-call | flops 20000000000 | bytes 83886080 | tf_op jit(solution)/shard_map/embed/pallas_call | solution.py:356
  444.5 4.0 fusion.73
  451.0 8.2 fusion.47
  459.2 29.5 %fusion.1 = (bf16[4,512,1024]{1,2,0:T(8,128)(2,1)S(1)}, f32[4,512,1024]{1,2,0:T(8,128)}, f32[4,512,1024]{1,2,0:T(8,128)}, f32[4,1024,512]{2,1,0:T(8,128)}) fusion(f32[4,1024]{1,0:T(4,128)S(1)} %bitcast.271, f32[4,1024,512]{2,1,0:T(8,128)} %fusion.47, f32[4,1024]{1,0:T(4,128)S(1)} %bitcast.273, bf16[4,1024,1024]{2,1,0:T(8,128)(2,1)S(1)} %bitcast.290, ...), kind=kOutput, calls=%fused_computation.10 | convolution fusion | flops 4440195072 | bytes 48279552 | tf_op jit(solution)/shard_map/sk,tkc->tsc/dot_general | solution.py:843
  488.8 9.0 fusion.74
  500.1 16.3 %fusion.20 = (f32[4,1024]{1,0:T(4,128)S(1)}, bf16[4,512,1024]{1,2,0:T(8,128)(2,1)S(1)}, f32[4,1024]{1,0:T(4,128)S(1)}, bf16[4,512,1024]{1,2,0:T(8,128)(2,1)S(1)}) fusion(f32[4,512,1024]{1,2,0:T(8,128)} %get-tuple-element.64, f32[4,512,1024]{1,2,0:T(8,128)} %get-tuple-element.65, f32[4,1024,512]{2,1,0:T(8,128)} %get-tuple-element.93, ...), kind=kOutput, calls=%fused_computation.36 | convolution fusion | flops 4343193600 | bytes 51445760 | tf_op jit(solution)/shard_map/sd,tcd->tsc/dot_general | solution.py:862
  516.5 9.9 fusion.62
  526.5 8.3 multiply_reduce_fusion
  539.7 4.3 convolution_bitcast_fusion
  544.0 29.1 %all-to-all-start = ((f32[4,512,256]{1,2,0:T(8,128)}), f32[4,512,256]{1,2,0:T(8,128)}, u32[]{:S(2)}, u32[]{:S(2)}) async-start(f32[4,512,256]{1,2,0:T(8,128)} %convolution_bitcast_fusion), calls=%async_computation | async-start | bytes 4194304 | tf_op jit(solution)/shard_map/all_to_all | solution.py:878
  573.1 6.2 copy.75
  579.3 4.5 gather_fusion.4
  585.7 4.3 gather_fusion.2
  593.1 4.3 copy.82
  599.4 4.5 copy.76
  606.1 7.0 fusion.29.refs_5_
  613.1 5.7 fusion.77
  618.8 5.7 fusion.58
  624.4 5.7 fusion.76
  630.1 5.7 fusion.60
  641.3 74.8 %attention_grad.1 = (bf16[2048,768]{1,0:T(8,128)(2,1)}, f32[1,768]{1,0:T(1,128)S(1)}) custom-call(bf16[2048,256]{1,0:T(8,128)(2,1)S(1)} %copy-done.3, bf16[2048,256]{1,0:T(8,128)(2,1)S(1)} %copy-done.4, bf16[2048,256]{1,0:T(8,128)(2,1)S(1)} %copy-done.5, f32[2048,256]{1,0:T(8,128)} %get-tuple-element.38.ctx, f32[2048,256]{1,0:T(8,128)} %bitcast.259, ...), custom_call_target="tpu_custom_call" | custom-call | flops 8000000000 | bytes 16777216 | tf_op jit(solution)/shard_map/attention_grad/pallas_call | solution.py:788
  717.4 5.5 fusion.75
  723.6 3.4 copy-done.32
  728.9 5.7 fusion.31.refs_2_
  734.7 331.3 %sums.1 = (f32[8,2048,128]{2,1,0:T(8,128)}, f32[6,64,1024]{2,1,0:T(8,128)}, f32[24,4,64,1024]{3,2,1,0:T(8,128)}) custom-call(f32[2048,1024]{1,0:T(8,128)} %copy-done.32, f32[4,4,128,1024]{3,2,1,0:T(8,128)} %bitcast.253, f32[4,4,128,1024]{3,2,1,0:T(8,128)} %bitcast.252, f32[4,4,128,1024]{3,2,1,0:T(8,128)} %fusion.31.refs_2_, f32[4,4,128,1024]{3,2,1,0:T(8,128)} %bitcast.251, ...), custom_call_target="tpu_custom_call" | custom-call | flops 20000000000 | bytes 104857600 | tf_op jit(solution)/shard_map/sums/pallas_call | solution.py:537
  1069.9 33.6 %table_rows.1.block_in = f32[7648,128]{1,0:T(8,128)S(1)} custom-call(s32[16384]{0:T(1024)S(1)} %and_select_fusion.ids, f32[16384,128]{1,0:T(8,128)} %bitcast.249), custom_call_target="tpu_custom_call" | custom-call | flops 3000000000 | bytes 16777216 | tf_op jit(solution)/shard_map/table_rows/pallas_call | solution.py:583
  1105.4 14.4 %fusion.49 = f32[1024,768]{1,0:T(8,128)} fusion(bf16[2048,1024]{1,0:T(8,128)(2,1)} %get-tuple-element.40, bf16[2048,768]{1,0:T(8,128)(2,1)S(1)} %copy-done.47, s32[768]{0:T(1024)S(1)} %copy-done.46), kind=kOutput, calls=%fused_computation.91 | convolution fusion | flops 5639307264 | bytes 10488832 | tf_op jit(solution)/shard_map/dot_general | solution.py:881
  1119.8 188.8 %gathered_columns.1 = f32[7648,1024]{1,0:T(8,128)} custom-call(f32[7648,128]{1,0:T(8,128)} %copy-done), custom_call_target="tpu_custom_call" | custom-call | flops 10000000000 | bytes 62914560 | tf_op jit(solution)/shard_map/gathered_columns/pallas_call | solution.py:659
  1312.9 7.2 all-reduce.4.cloned.1.call-done
  1320.2 22.4 %copy.113 = f32[7648,1024]{1,0:T(8,128)} copy(f32[7648,1024]{1,0:T(8,128)} %gathered_columns.1) | data formatting | bytes 62652416
  (194 shorter events, 63.5 us)
Async XLA Ops:
  7.2 8.4 copy-start.45
  7.2 8.2 copy-start.34
  7.2 8.3 copy-start.40
  7.2 8.4 copy-start.42
  7.2 727.4 %reduce-scatter.2.cloned.1.call-start = ((), (), s32[]{:S(2)}) async-start(), calls=%async_computation.4 | async-start | bytes 4325376 | tf_op jit(solution)/shard_map/reduce_scatter | solution.py:876
  444.5 6.5 copy-start.38
  444.5 6.5 copy-start.43
  448.6 86.2 %copy-start.10 = (f32[512,1024]{1,0:T(8,128)}, f32[512,1024]{1,0:T(8,128)S(1)}, u32[]{:S(2)}) copy-start(f32[512,1024]{1,0:T(8,128)S(1)} %get-tuple-element.92) | copy-start | bytes 6291460
  448.6 10.6 slice-start
  451.0 8.2 slice-start.1
  488.7 9.0 copy-start.21
  488.8 9.4 copy-start.39
  488.8 9.4 copy-start.31
  500.1 16.3 %copy-start.28 = (bf16[512,1024]{1,0:T(8,128)(2,1)}, bf16[512,1024]{1,0:T(8,128)(2,1)S(1)}, u32[]{:S(2)}) copy-start(bf16[512,1024]{1,0:T(8,128)(2,1)S(1)} %get-tuple-element.73) | copy-start | bytes 3145732
  516.5 10.0 copy-start.12
  516.5 10.0 copy-start.14
  544.0 91.8 %all-to-all-start = ((f32[4,512,256]{1,2,0:T(8,128)}), f32[4,512,256]{1,2,0:T(8,128)}, u32[]{:S(2)}, u32[]{:S(2)}) async-start(f32[4,512,256]{1,2,0:T(8,128)} %convolution_bitcast_fusion), calls=%async_computation | async-start | bytes 4194304 | tf_op jit(solution)/shard_map/all_to_all | solution.py:878
  573.1 735.5 %all-reduce.6.cloned.1.call-start = ((), (), s32[]{:S(2)}) async-start(), calls=%async_computation.3 | async-start | bytes 196608 | tf_op jit(solution)/shard_map/psum | solution.py:894
  584.3 7.2 copy-start.16
  599.0 7.1 copy-start.25
  606.1 7.0 copy-start.15
  641.3 74.8 %copy-start.46 = (s32[768]{0:T(1024)S(1)}, s32[768]{0:T(1024)}, u32[]{:S(2)}) copy-start(s32[768]{0:T(1024)} %constant.165.clone) | copy-start | bytes 9220
  641.3 75.9 %copy-start.41 = (f32[4]{0:T(128)S(1)}, f32[4]{0:T(128)}, u32[]{:S(2)}) copy-start(f32[4]{0:T(128)} %get-tuple-element.98) | copy-start | bytes 52
  641.3 76.0 %copy-start.44 = (bf16[768,1024]{0,1:T(8,128)(2,1)S(1)}, bf16[768,1024]{0,1:T(8,128)(2,1)}, u32[]{:S(2)}) copy-start(bf16[768,1024]{0,1:T(8,128)(2,1)} %fusion.35) | copy-start | bytes 4718596
  722.9 6.0 copy-start.24
  728.9 584.0 %all-gather.5.cloned.1.call-start = ((), (), s32[]{:S(2)}) async-start(), calls=%async_computation.5 | async-start | bytes 1179648 | tf_op jit(solution)/shard_map/all_gather | solution.py:876
  734.6 578.3 %all-gather.7.cloned.1.call-start = ((), (), s32[]{:S(2)}) async-start(), calls=%async_computation.6 | async-start | bytes 4718592 | tf_op jit(solution)/shard_map/all_gather | solution.py:886
  1068.6 244.3 %all-gather.9.cloned.1.call-start = ((), (), s32[]{:S(2)}) async-start(), calls=%async_computation.7 | async-start | bytes 4718592 | tf_op jit(solution)/shard_map/all_gather | solution.py:886
  1069.2 243.7 %all-gather.11.cloned.1.call-start = ((), (), s32[]{:S(2)}) async-start(), calls=%async_computation.8 | async-start | bytes 4718592 | tf_op jit(solution)/shard_map/all_gather | solution.py:886
  1069.8 250.4 %all-reduce.4.cloned.1.call-start = ((), (), s32[]{:S(2)}) async-start(), calls=%async_computation.2 | async-start | bytes 6291456 | tf_op jit(solution)/shard_map/psum | solution.py:881
  1069.9 35.5 %copy-start.47 = (bf16[2048,768]{1,0:T(8,128)(2,1)S(1)}, bf16[2048,768]{1,0:T(8,128)(2,1)}, u32[]{:S(2)}) copy-start(bf16[2048,768]{1,0:T(8,128)(2,1)} %get-tuple-element.48) | copy-start | bytes 9437188
  1320.2 22.4 %copy-start.22 = (f32[1024,768]{1,0:T(8,128)S(1)}, f32[1024,768]{1,0:T(8,128)}, u32[]{:S(2)}) copy-start(f32[1024,768]{1,0:T(8,128)} %all-reduce.4.cloned.1.call-done) | copy-start | bytes 9437188
  (26 other events, 90.9 us)
Sparse Core Ops, SparseCore 0:
  539.8 168.8 reduce-scatter.1
  729.0 127.5 all-reduce.5
  858.5 27.1 all-gather.4
  1068.8 45.1 all-gather.6
  1116.2 52.4 all-gather.8
  1171.1 54.1 all-gather.10
  1229.1 91.0 all-reduce.3

commit v2 on v1

--- a/solution.py
+++ b/solution.py
@@ -73,17 +73,20 @@
 LAG = 3
 
 
-def chain_sum(k, z, n, rows, chunks, part, left, right, done, send_r, send_l, recv_l, recv_r):
+def chain_sum(k, z, n, rows, chunks, part, left, right, done, send_r, send_l, recv_l, recv_r, place=lambda c: c):
     last = n - 1
 
+    def at_rows(c):
+        return pl.ds(pl.multiple_of(place(c) * rows, rows), rows)
+
     def cut(ref, c):
-        return ref.at[pl.ds(pl.multiple_of(c * rows, rows), rows)]
+        return ref.at[at_rows(c)]
 
     def load(ref, c):
-        return ref[pl.ds(pl.multiple_of(c * rows, rows), rows)]
+        return ref[at_rows(c)]
 
     def store(ref, c, value):
-        ref[pl.ds(pl.multiple_of(c * rows, rows), rows)] = value
+        ref[at_rows(c)] = value
     cl, cr = k - LAG * z, k - LAG * (last - z)
     okl, okr = (cl >= 0) & (cl < chunks), (cr >= 0) & (cr < chunks)
 
@@ -267,11 +270,14 @@
 
     start = per + LAG * (n - N1)
 
-    def context(i):
-        src = ctx.at[pl.ds(pl.multiple_of(i * qb, qb), qb)]
-        to = i // (blocks // n)
-        dst = ctx_own.at[z, pl.ds(pl.multiple_of((i % (blocks // n)) * qb, qb), qb)]
-        return to, pltpu.make_async_copy(src, dst, aself), rcopy(src, dst, asend, arecv.at[z], tp=to)
+    share = qb // n
+
+    def context(i, d):
+        to = (z + d) % n
+        src = ctx.at[pl.ds(pl.multiple_of(i * qb + to * share, share), share)]
+        if d == N0:
+            return pltpu.make_async_copy(src, ctx_own.at[z, i], aself)
+        return rcopy(src, ctx_own.at[z, i], asend, arecv.at[z], tp=to)
 
     @pl.loop(N0, max(start + blocks * heads + N1, FIRST + len(plan)))
     def _(k):
@@ -280,15 +286,8 @@
 
         @pl.when((step > N0) & (step % heads == N0) & (step <= blocks * heads))
         def _():
-            to, local_copy, remote = context(i)
-
-            @pl.when(to == z)
-            def _():
-                local_copy.start()
-
-            @pl.when(to != z)
-            def _():
-                remote.start()
+            for d in range(n):
+                context(i, d).start()
         chain_sum(k, z, n, rows, chunks, part, left, right, done, send_r, send_l, recv_l, recv_r)
         for at_step, event in events:
             pl.when(k == at_step)(event)
@@ -300,13 +299,10 @@
                 project(step // heads, qb, out, wq, bq, cos, sin, q, k_all, v)
             attend(step // heads, step % heads, heads, qb, q, k_all, v, ctx, top, inv, weights)
 
-    kept = blocks // n
-    pltpu.make_async_copy(ctx.at[pl.ds(N0, kept * qb)], ctx_own.at[z], aself).wait()
-    rest = ctx.at[pl.ds(N0, (blocks - kept) * qb)]
-    rcopy(rest, rest, asend, arecv.at[z], tp=z).wait_send()
+    pltpu.make_async_copy(ctx_own.at[z], ctx_own.at[z], aself).wait()
     for d in range(N1, n):
         src = (z + d) % n
-        rcopy(ctx_own.at[src], ctx_own.at[src], asend, arecv.at[src], tp=z).wait_recv()
+        rcopy(ctx_own.at[src], ctx_own.at[src], asend, arecv.at[src], tp=z).wait()
     chain_drain(z, n, part, left, right, send_r, send_l, recv_l, recv_r)
     for s in (len(plan) - N2, len(plan) - N1):
         for copy in stored(*plan[s], s % N2):
@@ -351,7 +347,7 @@
     shape = jax.ShapeDtypeStruct
     shapes = [shape((seq, width), BF)]
     shapes += [shape((n_tp, n_dp, w.shape[0] // n_dp, w.shape[1]), BF) for w in local]
-    shapes += [shape((n_tp, piece.shape[0] - lo, width), F32), shape((n_dp,) + toks.shape, toks.dtype), shape((n_tp, n_dp) + piece.shape, F32), shape((n_tp, seq // n_tp, dims), F32)]
+    shapes += [shape((n_tp, piece.shape[0] - lo, width), F32), shape((n_dp,) + toks.shape, toks.dtype), shape((n_tp, n_dp) + piece.shape, F32), shape((n_tp, 8, seq // n_tp // 8, dims), F32)]
     shapes += [shape((seq, dims), BF)] * 3 + [shape((seq, dims), F32)] + [shape((heads, seq), F32)] * 2
     out = pl.pallas_call(
         functools.partial(emb_kernel, n_tp, rows, chunks, cuts, heads),
@@ -370,30 +366,85 @@
 
 
 RING = 8
-HOLD = 6
-OPEN, ADD, CROSSED, PLANE, HOP = 1, 2, 6, 10, 2
-
-
-def sums_kernel(n, rows, chunks, jobs, part, *refs):
-    odd, even = refs[:jobs], refs[jobs:N2 * jobs]
-    out, grads, landed, left, right, total, work, fresh, cross, last, along, final, send_r, send_l, recv_l, recv_r, osend, orecv, csend, crecv, esem, fsem, xsend, xrecv, ysend, yrecv, zsend, zrecv, frecv, gsem = refs[N2 * jobs:]
+HOLD, LIVE, PAIR = 4, 8, 4
+ADD, LOAD, CROSSED, LAND, PLANE = 1, 4, 5, 7, 8
+
+
+def backward_kernel(n, rows, chunks, jobs, heads, d_ctx, resid, q, k_all, v, ctx, top, inv, cos, sin, wq, *refs):
+    prods = refs[:jobs]
+    out, grads, d_qkv, d_bias, landed, cross, last, part, left, right, total, dctx, dq, dk, dv, ctx_in, res_in, work, fresh, xin, yin, keep, pass_on, along, final, *sems = refs[jobs:]
+    send_r, send_l, recv_l, recv_r, osend, orecv, csend, crecv, esem, fsem, xsend, xrecv, xsem, ysend, yrecv, ysem, ksem, zrecv, frecv, asend, arecv, aself, isem = sems
     z = lax.axis_index('tp')
     p, at = plane()
     entry_barrier(z, n, at)
+    blocks = 8
+    per = chunks // blocks
+    qb = rows * per
+    share = qb // n
     block = out.shape[N2]
     lead = jnp.maximum(z, n - N1 - z)
     span = N2 * n
     units = jobs * span
     size = work.shape[N2]
 
+    def rows_of(i, to, count):
+        return pl.ds(pl.multiple_of(i * qb + to * count, count), count)
+
+    def exchange(i, d):
+        to = (z + d) % n
+        dst = dctx.at[rows_of(i, z, share)]
+        if d == N0:
+            return pltpu.make_async_copy(d_ctx.at[z, i], dst, aself.at[i])
+        return rcopy(d_ctx.at[to, i], dst, asend, arecv.at[i], tp=to)
+
+    @pl.loop(N0, blocks)
+    def _(b):
+        for d in range(n):
+            exchange(blocks - N1 - b, d).start()
+
+    def piece(m, u, rel):
+        return prods[m].at[(u % span) // N2, at(rel), pl.ds(pl.multiple_of((u % N2) * size, size), size)]
+
     for m in range(jobs):
-        @pl.loop(N0, span)
+        @pl.loop(m * span, (m + N1) * span)
         def _(u, m=m):
-            dst = landed.at[m * span + u]
-            rcopy(odd[m].at[u // N2, :, pl.ds(pl.multiple_of((u % N2) * size, size), size)], dst, csend, crecv.at[m * span + u], dp=at(N1)).start()
-
-    def here(u):
-        return (u >= N0) & (u < units)
+            for i in range(4):
+                rcopy(piece(m, u, N2 * i + N1), landed.at[u, i], csend, crecv.at[u], dp=at(N1)).start()
+
+    def inputs(i):
+        slot = i % N2
+        at_q = rows_of(i, N0, qb)
+        return [pltpu.make_async_copy(ctx.at[at_q], ctx_in.at[slot], isem.at[N0, slot]), pltpu.make_async_copy(resid.at[i], res_in.at[slot], isem.at[N1, slot])]
+
+    dk[...] = jnp.zeros_like(dk)
+    dv[...] = jnp.zeros_like(dv)
+    d_bias[...] = jnp.zeros_like(d_bias)
+    for copy in inputs(blocks - N1):
+        copy.start()
+
+    def attention_step(b, h):
+        i = blocks - N1 - b
+
+        @pl.when(h == N0)
+        def _():
+            for copy in inputs(i):
+                copy.wait()
+
+            @pl.when(b + N1 < blocks)
+            def _():
+                for copy in inputs(i - N1):
+                    copy.start()
+            exchange(i, N0).wait()
+            others = dctx.at[pl.ds(N0, (n - N1) * share)]
+            rcopy(others, others, asend, arecv.at[i], tp=z).wait_recv()
+        attend_grad(i, h, heads, qb, q, k_all, v, ctx_in.at[i % N2], dctx, top, inv, dq, dk, dv)
+
+        @pl.when(h == heads - N1)
+        def _():
+            got = grad_rows(i, qb, cos, sin, dq, dk, dv, d_bias)
+            d_qkv[rows_of(i, N0, qb), :] = got
+            part[rows_of(i, N0, qb), :] = dot(got, wq[...], NT)
+            part[rows_of(i, z, share), :] = part[rows_of(i, z, share), :] + res_in[i % N2]
 
     def sides(u):
         side = u % N2
@@ -404,21 +455,21 @@
 
         @pl.when(u >= HOLD)
         def _():
-            rcopy(work.at[slot, pl.ds(N0, N2)], cross.at[u - HOLD], xsend.at[slot], xrecv.at[u - HOLD], dp=p).wait_send()
+            rcopy(xin.at[N0], cross.at[N0], xsend.at[slot], xrecv.at[N0], dp=p).wait_send()
         for m in range(jobs):
             @pl.when(u // span == m)
             def _(m=m):
-                v = u - m * span
-                pltpu.make_async_copy(even[m].at[v // N2, :, pl.ds(pl.multiple_of((v % N2) * size, size), size)], work.at[slot], esem.at[slot]).start()
+                for i in range(4):
+                    pltpu.make_async_copy(piece(m, u, N2 * i), work.at[slot, i], esem.at[slot]).start()
         rcopy(landed.at[u], landed.at[u], csend, crecv.at[u], dp=p).wait_recv()
-        pltpu.make_async_copy(landed.at[u], fresh.at[u % N2], fsem.at[u % N2]).start()
+        pltpu.make_async_copy(landed.at[u], fresh, fsem).start()
 
     def add(u):
         slot = u % HOLD
         pltpu.make_async_copy(landed.at[u], work.at[slot], esem.at[slot]).wait()
-        pltpu.make_async_copy(landed.at[u], fresh.at[u % N2], fsem.at[u % N2]).wait()
-        for q in range(4):
-            work[slot, q] = work[slot, q] + fresh[u % N2, q]
+        pltpu.make_async_copy(landed.at[u], fresh, fsem).wait()
+        for i in range(4):
+            work[slot, i] = work[slot, i] + fresh[i]
 
     def add_send(u):
         slot = u % HOLD
@@ -426,46 +477,67 @@
         rcopy(work.at[slot, N1 + side], cross.at[u, N0], xsend.at[slot], xrecv.at[u], dp=first).start()
         rcopy(work.at[slot, 3], cross.at[u, N1], xsend.at[slot], xrecv.at[u], dp=first).start()
 
+    def load_cross(u):
+        rcopy(cross.at[u], cross.at[u], xsend.at[N0], xrecv.at[u], dp=p).wait_recv()
+        pltpu.make_async_copy(cross.at[u], xin.at[u % N2], xsem.at[u % N2]).start()
+
     def crossed(u):
         slot = u % HOLD
-        rcopy(cross.at[u], cross.at[u], xsend.at[slot], xrecv.at[u], dp=p).wait_recv()
-        cross[u, N0] = cross[u, N0] + work[slot, N0]
-        cross[u, N1] = cross[u, N1] + work[slot, N2 - u % N2]
+        pltpu.make_async_copy(cross.at[u], xin.at[u % N2], xsem.at[u % N2]).wait()
+
+        @pl.when(u >= LIVE)
+        def _():
+            pltpu.make_async_copy(keep.at[u % LIVE], keep.at[u % LIVE], ksem.at[u % LIVE]).wait()
+
+        @pl.when(u >= PAIR)
+        def _():
+            rcopy(pass_on.at[u % PAIR], last.at[u], ysend.at[u % PAIR], yrecv.at[u], dp=p).wait_send()
+        keep[u % LIVE] = xin[u % N2, N0] + work[slot, N0]
+        pass_on[u % PAIR] = xin[u % N2, N1] + work[slot, N2 - u % N2]
 
     def crossed_send(u):
         side, first, second = sides(u)
-        rcopy(cross.at[u, N1], last.at[u], ysend, yrecv.at[u], dp=second).start()
+        rcopy(pass_on.at[u % PAIR], last.at[u], ysend.at[u % PAIR], yrecv.at[u], dp=second).start()
+
+    def load_last(u):
+        rcopy(last.at[u], last.at[u], ysend.at[N0], yrecv.at[u], dp=p).wait_recv()
+        pltpu.make_async_copy(last.at[u], yin.at[u % N2], ysem.at[u % N2]).start()
 
     def in_plane(u):
-        rcopy(last.at[u], last.at[u], ysend, yrecv.at[u], dp=p).wait_recv()
-        cross[u, N0] = cross[u, N0] + last[u]
+        pltpu.make_async_copy(last.at[u], yin.at[u % N2], ysem.at[u % N2]).wait()
+        keep[u % LIVE] = keep[u % LIVE] + yin[u % N2]
+
+    def unit(k):
+        u = (k // 3) * N2 + k % 3
+        return u, (k >= N0) & (k % 3 < N2) & (u < units)
 
     def along_tp(k, t, send):
         toward = jnp.where(z < t, z, n - N1 - z)
-        late = HOP * jnp.where(z == t, max(t, n - N1 - t), toward)
-        u = k - PLANE - N1 - late
+        late = jnp.where(z == t, max(t, n - N1 - t), toward)
+        u, ok = unit(k - PLANE - N1 - late)
         mine = (u // span) * N2 + u % N2
-        ok = here(u) & ((u // N2) % n == t)
+        slot = u % LIVE
+        ok = ok & ((u // N2) % n == t)
 
         def add_from(ref, sem):
-            rcopy(ref, ref, zsend, sem, tp=z).wait_recv()
-            cross[u, N0] = cross[u, N0] + ref[...]
+            rcopy(ref, ref, csend, sem, tp=z).wait_recv()
+            keep[slot] = keep[slot] + ref[...]
         if send:
             @pl.when(ok & (z < t))
             def _():
-                rcopy(cross.at[u, N0], along.at[u], zsend, zrecv.at[u], tp=z + N1).start()
+                rcopy(keep.at[slot], along.at[u], ksem.at[slot], zrecv.at[u], tp=z + N1).start()
 
             @pl.when(ok & (z > t + N1))
             def _():
-                rcopy(cross.at[u, N0], along.at[u], zsend, zrecv.at[u], tp=z - N1).start()
+                rcopy(keep.at[slot], along.at[u], ksem.at[slot], zrecv.at[u], tp=z - N1).start()
 
             @pl.when(ok & (z == t + N1))
             def _():
-                rcopy(cross.at[u, N0], final.at[mine], zsend, frecv.at[mine], tp=z - N1).start()
+                rcopy(keep.at[slot], final.at[mine], ksem.at[slot], frecv.at[mine], tp=z - N1).start()
 
             @pl.when(ok & (z == t))
             def _():
-                pltpu.make_async_copy(cross.at[u, N0], grads.at[mine], gsem).start()
+                pltpu.make_async_copy(keep.at[slot], grads.at[mine], ksem.at[slot]).start()
         else:
             @pl.when(ok & (((z > N0) & (z <= t)) | ((z > t) & (z < n - N1))))
             def _():
@@ -475,6 +547,9 @@
                 def _():
                     add_from(final.at[mine], frecv.at[mine])
 
+    def place(c):
+        return (blocks - N1 - c // per) * per + c % per
+
     def chunk(c):
         return total.at[c % RING]
 
@@ -484,28 +559,40 @@
             pltpu.make_async_copy(chunk(c), chunk(c), osend.at[c % RING]).wait()
         total[c % RING] = value
 
-    @pl.loop(N0, max(chunks + LAG * (n - N1) + N1, units + PLANE + N1 + HOP * (n - N1)))
+    def hand_out(c):
+        where = out.at[p, pl.ds(pl.multiple_of(place(c) * rows, rows), rows)]
+        for rel in range(8):
+            src = total.at[c % RING, :, pl.ds(pl.multiple_of(at(rel) * block, block), block)]
+            if rel == N0:
+                pltpu.make_async_copy(src, where, osend.at[c % RING]).start()
+            else:
+                rcopy(src, where, osend.at[c % RING], orecv.at[rel], dp=at(rel)).start()
+
+    def staged(k, offset, stage):
+        u, ok = unit(k - offset)
+        pl.when(ok)(functools.partial(stage, u))
+    steps = max(heads + chunks + LAG * (n - N1) + N1, (units // N2) * 3 + PLANE + n)
+
+    @pl.loop(N0, steps)
     def _(k):
-        c = k - LAG * lead - N1
+        c = k - heads - LAG * lead - N1
 
         @pl.when((c >= N0) & (c < chunks))
         def _():
-            where = out.at[p, pl.ds(pl.multiple_of(c * rows, rows), rows)]
-            for rel in range(8):
-                src = total.at[c % RING, :, pl.ds(pl.multiple_of(at(rel) * block, block), block)]
-                if rel == N0:
-                    pltpu.make_async_copy(src, where, osend.at[c % RING]).start()
-                else:
-                    rcopy(src, where, osend.at[c % RING], orecv.at[rel], dp=at(rel)).start()
-        chain_sum(k, z, n, rows, chunks, part, left, right, done, send_r, send_l, recv_l, recv_r)
-        stages = ((OPEN, fetch, None), (ADD, add, add_send), (CROSSED, crossed, crossed_send), (PLANE, in_plane, None))
-        for offset, stage, _ in stages:
-            pl.when(here(k - offset))(functools.partial(stage, k - offset))
+            hand_out(c)
+        chain_sum(k - heads, z, n, rows, chunks, part, left, right, done, send_r, send_l, recv_l, recv_r, place)
+        for offset, stage in ((CROSSED, crossed), (ADD, add), (PLANE, in_plane)):
+            staged(k, offset, stage)
         for t in range(n):
             along_tp(k, t, False)
-        for offset, _, stage in stages:
-            if stage:
-                pl.when(here(k - offset))(functools.partial(stage, k - offset))
+        for offset, stage in ((N0, fetch), (LOAD, load_cross), (LAND, load_last)):
+            staged(k, offset, stage)
+
+        @pl.when(k < blocks * heads)
+        def _():
+            attention_step(k // heads, k % heads)
+        for offset, stage in ((ADD, add_send), (CROSSED, crossed_send)):
+            staged(k, offset, stage)
         for t in range(n):
             along_tp(k, t, True)
 
@@ -513,40 +600,45 @@
     for c in range(max(N0, chunks - RING), chunks):
         pltpu.make_async_copy(chunk(c), chunk(c), osend.at[c % RING]).wait()
     for rel in range(N1, 8):
-        rcopy(out.at[at(rel)], out.at[at(rel)], ysend, orecv.at[rel], dp=p).wait_recv()
-    for u in range(units - HOLD, units):
-        rcopy(work.at[u % HOLD, pl.ds(N0, N2)], cross.at[u], xsend.at[u % HOLD], xrecv.at[u], dp=p).wait_send()
+        rcopy(out.at[at(rel)], out.at[at(rel)], csend, orecv.at[rel], dp=p).wait_recv()
+    for slot in range(HOLD):
+        rcopy(xin.at[N0], cross.at[N0], xsend.at[slot], xrecv.at[N0], dp=p).wait_send()
+    for slot in range(PAIR):
+        rcopy(pass_on.at[slot], last.at[N0], ysend.at[slot], yrecv.at[N0], dp=p).wait_send()
+    for slot in range(LIVE):
+        pltpu.make_async_copy(keep.at[slot], keep.at[slot], ksem.at[slot]).wait()
     rcopy(landed, landed, csend, crecv.at[N0], dp=p).wait_send()
-    rcopy(last, last, ysend, yrecv.at[N0], dp=p).wait_send()
-    kept = units - units // n
-    rcopy(along.at[pl.ds(N0, kept)], along.at[pl.ds(N0, kept)], zsend, zrecv.at[N0], tp=z).wait_send()
-    pltpu.make_async_copy(grads, grads, gsem).wait()
-
-
-def sums(part, odd, even, n_tp, n_dp):
-    seq, width = part.shape
-    rows = min(64, seq // 4)
-    chunks = seq // rows
-    jobs = len(odd)
-    size = odd[0].shape[2] // 2
-    wide = odd[0].shape[3]
+    sent = dctx.at[pl.ds(N0, (n - N1) * share * blocks)]
+    rcopy(sent, sent, asend, arecv.at[N0], tp=z).wait_send()
+
+
+def backward(d_ctx, resid, saved, cos, sin, wq, prods, heads, n_tp, n_dp):
+    q, k, v, ctx, top, inv = saved
+    seq, dims = q.shape
+    width = wq.shape[0]
+    chunks = 32
+    rows = seq // chunks
+    jobs = len(prods)
+    piece = (prods[0].shape[2] // 2, prods[0].shape[3])
     units = jobs * 2 * n_tp
     dma = pltpu.SemaphoreType.DMA
-    piece = (size, wide)
-    vmem = [(RING, rows, width), (HOLD, 4) + piece, (2, 4) + piece, (units, 2) + piece, (units,) + piece, (units,) + piece, (2 * jobs,) + piece]
-    cols, grads, _ = pl.pallas_call(
-        functools.partial(sums_kernel, n_tp, rows, chunks, jobs),
-        name='sums',
-        out_shape=(jax.ShapeDtypeStruct((n_dp, seq, width // n_dp), F32), jax.ShapeDtypeStruct((2 * jobs,) + piece, F32), jax.ShapeDtypeStruct((units, 4) + piece, F32)),
-        in_specs=[VMEM] + [ANY] * (2 * jobs),
-        out_specs=(ANY,) * 3,
-        scratch_shapes=[pltpu.VMEM((seq, width), F32)] * 2 + [pltpu.VMEM(shape, F32) for shape in vmem] + [
-            dma, dma, dma((chunks,)), dma((chunks,)), dma((RING,)), dma((8,)), dma, dma((units,)), dma((HOLD,)), dma((2,)),
-            dma((HOLD,)), dma((units,)), dma, dma((units,)), dma, dma((units,)), dma((2 * jobs,)), dma],
+    shape = jax.ShapeDtypeStruct
+    qb = seq // 8
+    vmem = [(seq, width)] * 3 + [(RING, rows, width), (seq, dims), (qb, dims), (seq, dims), (seq, dims), (2, qb, dims), (2, qb // n_tp, width),
+            (HOLD, 4) + piece, (4,) + piece, (2, 2) + piece, (2,) + piece, (LIVE,) + piece, (PAIR,) + piece, (units,) + piece, (2 * jobs,) + piece]
+    sems = [(), (), (chunks,), (chunks,), (RING,), (8,), (), (units,), (HOLD,), (), (HOLD,), (units,), (2,), (PAIR,), (units,), (2,), (LIVE,), (units,), (2 * jobs,), (), (8,), (8,), (2, 2)]
+    cols, grads, d_qkv, d_bias, *_ = pl.pallas_call(
+        functools.partial(backward_kernel, n_tp, rows, chunks, jobs, heads),
+        name='backward',
+        out_shape=(shape((n_dp, seq, width // n_dp), F32), shape((2 * jobs,) + piece, F32), shape((seq, 3 * dims), BF), shape((1, 3 * dims), F32),
+                   shape((units, 4) + piece, F32), shape((units, 2) + piece, F32), shape((units,) + piece, F32)),
+        in_specs=[ANY, ANY] + [VMEM] * 3 + [ANY] + [VMEM] * 5 + [ANY] * jobs,
+        out_specs=(ANY, ANY, VMEM, VMEM, ANY, ANY, ANY),
+        scratch_shapes=[pltpu.VMEM(size, F32) for size in vmem] + [dma(size) for size in sems],
         compiler_params=pltpu.CompilerParams(collective_id=1, has_side_effects=True, vmem_limit_bytes=63 * 2 ** 20),
         cost_estimate=pl.CostEstimate(flops=20 * 10 ** 9, bytes_accessed=100 * 2 ** 20, transcendentals=0),
-    )(part, *odd, *even)
-    return cols, grads.reshape(jobs, 2 * size, wide)
+    )(d_ctx, resid, q, k, v, ctx, top, inv, cos, sin, wq, *prods)
+    return d_qkv, d_bias, cols, grads.reshape(jobs, 2 * piece[0], piece[1])
 
 
 WAYS = 4
@@ -742,7 +834,7 @@
     q = jnp.where(lane_head((qb, dims), heads, 2) == h, q_ref[at_q, :].astype(F32), 0.0).astype(BF)
     dc = jnp.where(lane_head((qb, dims), heads, 1) == h, dctx_ref[at_q, :], 0.0).astype(BF)
     ones = jnp.ones((8, dims), F32)
-    mean = lax.dot_general(ones, dc.astype(F32) * ctx_ref[at_q, :], (NT, ((), ())), precision=lax.Precision.HIGHEST, preferred_element_type=F32)[:1]
+    mean = lax.dot_general(ones, dc.astype(F32) * ctx_ref[...], (NT, ((), ())), precision=lax.Precision.HIGHEST, preferred_element_type=F32)[:1]
     top, inv = top_ref[pl.ds(h, 1), at_q], inv_ref[pl.ds(h, 1), at_q]
 
     def step(j, dq):
@@ -765,38 +857,6 @@
     return rows.astype(BF)
 
 
-def attention_grad_kernel(heads, q, k, v, ctx, dctx, top, inv, cos, sin, d_qkv, d_bias, dq, dk, dv):
-    blocks = 8
-    qb = q.shape[0] // blocks
-    dk[...] = jnp.zeros_like(dk)
-    dv[...] = jnp.zeros_like(dv)
-    d_bias[...] = jnp.zeros_like(d_bias)
-
-    @pl.loop(0, blocks)
-    def _(step):
-        i = blocks - 1 - step
-
-        @pl.loop(0, heads)
-        def _(h):
-            attend_grad(i, h, heads, qb, q, k, v, ctx, dctx, top, inv, dq, dk, dv)
-        d_qkv[pl.ds(pl.multiple_of(i * qb, qb), qb), :] = grad_rows(i, qb, cos, sin, dq, dk, dv, d_bias)
-
-
-def attention_grad(saved, dctx, cos, sin, heads):
-    q, k, v, ctx, top, inv = saved
-    seq, dims = q.shape
-    return pl.pallas_call(
-        functools.partial(attention_grad_kernel, heads),
-        name='attention_grad',
-        in_specs=[VMEM] * 9,
-        out_specs=(VMEM, VMEM),
-        out_shape=(jax.ShapeDtypeStruct((seq, 3 * dims), BF), jax.ShapeDtypeStruct((1, 3 * dims), F32)),
-        scratch_shapes=[pltpu.VMEM((seq // 8, dims), F32), pltpu.VMEM((seq, dims), F32), pltpu.VMEM((seq, dims), F32)],
-        compiler_params=pltpu.CompilerParams(vmem_limit_bytes=48 * 2 ** 20),
-        cost_estimate=pl.CostEstimate(flops=8 * 10 ** 9, bytes_accessed=16 * 2 ** 20, transcendentals=10 ** 7),
-    )(q, k, v, ctx, dctx, top, inv, cos, sin)
-
-
 def solution(mesh):
     n_tp, n_dp = mesh.shape['tp'], mesh.shape['dp']
     in_specs = (P('dp', None), P('dp', None, None), P('tp', None)) + WEIGHT_SPECS
@@ -827,15 +887,18 @@
         place = column_order(heads, head_dim)
         swap = (jnp.arange(3 * dims)[:, None] == jnp.asarray(place)[None, :]).astype(BF)
         wq = jnp.dot(w_qkv, swap, preferred_element_type=F32).astype(BF)
-        bq = jnp.dot(b_qkv.reshape(N1, -1), swap, preferred_element_type=F32)
+        bq = jnp.dot(b_qkv.reshape(N1, -N1), swap, preferred_element_type=F32)
         cos_tab, sin_tab = rope_tables(seq_len, head_dim, heads)
         emb_bf, (wg_full, wl_full, wd_full, wo_full), biases, tok_all, ctx_own, saved = embed(own_rows, piece, tokens.reshape(-N1, min(128, seq_len // 8)), (w_gate, w_lin, w_down, w_out), wq, bq, cos_tab, sin_tab, heads, n_tp, n_dp)
-        ctx_own = ctx_own.astype(BF)
+        ctx_own = ctx_own.reshape(n_tp, own, dims).astype(BF)
         is_own = (jnp.arange(n_tp) == tp)[:, None]
         bg_full, bl_full = [jnp.where(is_own, b[None].astype(F32), biases[:, i]) for i, b in enumerate((b_gate, b_lin))]
 
-        emb_own = lax.dynamic_slice_in_dim(emb_bf, tp * own, own, N0).astype(F32)
-        cot_own = lax.dynamic_slice_in_dim(cotangent[N0], tp * own, own, N0).astype(F32)
+        blocks = 8
+
+        def owned(values):
+            return lax.dynamic_index_in_dim(values.reshape(blocks, n_tp, -N1, width), tp, N1, keepdims=False).reshape(own, width).astype(F32)
+        emb_own, cot_own = owned(emb_bf), owned(cotangent[N0])
         attn_out = jnp.einsum('hse,hed->sd', ctx_own, wo_full, preferred_element_type=F32) + b_out.astype(F32)
         normed_one, norm_one_pull = jax.vjp(norm_scaled, ALPHA * emb_own + attn_out, ln1_gain.astype(F32))
         hidden = (normed_one + ln1_bias.astype(F32)).astype(BF)
@@ -846,27 +909,21 @@
         ffn_out = jnp.einsum('tsc,tcd->sd', inner_act, wd_full, preferred_element_type=F32) + b_down.astype(F32)
         norm_two_pull = jax.vjp(norm_scaled, ALPHA * hidden.astype(F32) + ffn_out, ln2_gain.astype(F32))[N1]
 
-        rel_blocks = jnp.arange(n_dp // N2) * N2
-
-        def products(lhs, rhs, spec):
-            rows = lhs.shape[-N1] // n_dp
-            blocks = lhs.reshape(lhs.shape[:-N1] + (n_dp, rows))
-            for first in (N1, N0):
-                chosen = jnp.take(blocks, (rel_blocks + first) ^ dp, axis=-N2).reshape(lhs.shape[:-N1] + (-N1,))
-                yield jnp.einsum(spec, chosen, rhs, preferred_element_type=F32).reshape(n_tp, n_dp // N2, rows, -N1)
+        def product(lhs, rhs, spec):
+            return jnp.einsum(spec, lhs, rhs, preferred_element_type=F32).reshape(n_tp, n_dp, -N1, width)
 
         d_resid_two, d_ln2_gain = norm_two_pull(cot_own)
         d_b_down = jnp.sum(d_resid_two, axis=N0)
         d_ffn_bf = d_resid_two.astype(BF)
-        pair_down = products(inner_act, d_ffn_bf, 'tsc,sd->tcd')
+        prod_down = product(inner_act, d_ffn_bf, 'tsc,sd->tcd')
         d_inner = jnp.einsum('sd,tcd->tsc', d_ffn_bf, wd_full, preferred_element_type=F32).astype(BF)
         d_gate_pre, d_lin_pre = act_pull(d_inner.astype(F32))
         d_b_gate = jnp.sum(d_gate_pre, axis=N1)
         d_b_lin = jnp.sum(d_lin_pre, axis=N1)
         d_gate_bf = d_gate_pre.astype(BF)
         d_lin_bf = d_lin_pre.astype(BF)
-        pair_gate = products(hidden, d_gate_bf, 'sk,tsc->tkc')
-        pair_lin = products(hidden, d_lin_bf, 'sk,tsc->tkc')
+        prod_gate = product(hidden, d_gate_bf, 'sk,tsc->tkc')
+        prod_lin = product(hidden, d_lin_bf, 'sk,tsc->tkc')
         d_hidden = ALPHA * d_resid_two + jnp.einsum('tsc,tkc->sk', d_gate_bf, wg_full, preferred_element_type=F32) + jnp.einsum('tsc,tkc->sk', d_lin_bf, wl_full, preferred_element_type=F32)
         d_ln1_bias = jnp.sum(d_hidden, axis=N0)
         d_resid_one, d_ln1_gain = norm_one_pull(d_hidden)
@@ -875,14 +932,11 @@
         d_w_out = jnp.einsum('hse,sd->hed', ctx_own, d_attn_bf, preferred_element_type=F32)
         d_w_out = lax.all_gather(lax.psum_scatter(d_w_out.reshape(-N1, width), ALL, scatter_dimension=N0, tiled=True), 'dp', axis=N0, tiled=True)
         d_ctx = jnp.einsum('sd,hed->hse', d_attn_bf, wo_full, preferred_element_type=F32)
-        d_context = lax.all_to_all(d_ctx, 'tp', N0, N0).reshape(seq_len, dims)
-        d_qkv, d_b_qkv = attention_grad(saved, d_context, cos_tab, sin_tab, heads)
+        d_qkv, d_b_qkv, d_cols, mine = backward(
+            d_ctx.reshape(n_tp, blocks, own // blocks, dims), (ALPHA * d_resid_one).reshape(blocks, own // blocks, width), saved, cos_tab, sin_tab, wq,
+            (prod_gate, prod_lin, prod_down), heads, n_tp, n_dp)
         d_b_qkv = jnp.dot(d_b_qkv, swap.astype(F32).T, precision=lax.Precision.HIGHEST)[N0]
         d_w_qkv = lax.psum(jnp.dot(emb_bf.T, jnp.dot(d_qkv, swap.T, preferred_element_type=F32).astype(BF), preferred_element_type=F32), 'dp')
-        d_emb_part = jnp.dot(d_qkv, wq.T, preferred_element_type=F32)
-        d_emb_part = lax.dynamic_update_slice_in_dim(d_emb_part, lax.dynamic_slice_in_dim(d_emb_part, tp * own, own, N0) + ALPHA * d_resid_one, tp * own, N0)
-        odd, even = zip(*[tuple(pair) for pair in (pair_gate, pair_lin, pair_down)])
-        d_cols, mine = sums(d_emb_part, odd, even, n_tp, n_dp)
         d_w_gate, d_w_lin, d_w_down = [lax.all_gather(grad, 'dp', axis=N0, tiled=True) for grad in mine]
         all_ids = tok_all.reshape(-N1) - tp * vocab_loc
         all_ids = jnp.where((all_ids >= N0) & (all_ids < vocab_loc), all_ids, vocab_loc)

time: 1370 us -> 1310 us (0.956)
  starting transfers between devices: 29.4 us -> 0.29 us
  local copies, waits for them, and re-layouts: 108 us -> 80.8 us
  Pallas kernels: 1030 us -> 1010 us
  waiting for transfers between devices: 8.43 us -> 24.6 us
    all_to_all x1 -> x0, starting transfers between devices: 29.1 us -> none  [device_step(): d_context = lax.all_to_all(d_ctx, 'tp', N0, N0).reshape(seq_len, dims)]
    pallas_call x2 -> x1, Pallas kernels: 406 us -> 390 us  [backward(): pl.pallas_call(functools.partial(backward_kernel, n_tp, rows, chunks, job...]
    psum x1, waiting for transfers between devices: 7.22 us -> 22.8 us  [device_step(): lax.psum(jnp.dot(emb_bf.T, jnp.dot(d_qkv, swap.T, preferred_element_type=...]
    dot_general x8 -> x4, matrix products: 41.9 us -> 29.6 us  [the longest x3 28.6 us: product(): jnp.einsum(spec, lhs, rhs, preferred_element_type=F32)]
    unnamed x108 -> x60, local copies, waits for them, and re-layouts: 44.6 us -> 42.2 us
  transfers between devices with their start and end apart: 8 -> 7, of which waited for: 1 -> 1; matrix products, arithmetic and copies ran while one was open for 8% -> 5% of each run, Pallas kernels for 46% -> 47%
where the time goes in v2:
time: 1310 us; the launch traced here: 1300 us
  Pallas kernels  1010 us (77%)
  matrix products  147 us (11%)
  local copies, waits for them, and re-layouts  80.8 us (6%)
  other arithmetic  27.2 us (2%)
  waiting for transfers between devices  24.6 us (2%)
  between operations  16.1 us (1%)
    pallas_call x1, Pallas kernels, embed(): pl.pallas_call(functools.partial(emb_kernel, n_tp, rows, chunks, cuts, he...  393 us
    pallas_call x1, Pallas kernels, backward(): pl.pallas_call(functools.partial(backward_kernel, n_tp, rows, chunks, job...  390 us
    pallas_call x1, Pallas kernels, gathered_columns(): pl.pallas_call(functools.partial(gather_kernel, parts), name='gathered_co...  188 us
    unnamed x60, local copies, waits for them, and re-layouts  42.2 us
    pallas_call x1, Pallas kernels, table_rows(): pl.pallas_call(table_kernel, name='table_rows', grid_spec=pltpu.PrefetchS...  33.6 us
    dot_general x3, matrix products, product(): jnp.einsum(spec, lhs, rhs, preferred_element_type=F32)  28.6 us
    dot_general x1, matrix products, device_step(): jnp.einsum('sk,tkc->tsc', hidden, wl_full, preferred_element_type=F32)  27 us
  transfers between devices with their start and end apart: 7, of which 1 were waited for; matrix products, arithmetic and copies ran while one was open for 5% of the time, Pallas kernels for 47%

profile of v2, /device:TPU:0, one launch (start us, length us, event | category | flops | bytes accessed | tf_op | source)
XLA Modules:
  0.0 1301.4 jit_solution(12989998543294415398)
XLA Ops:
  22.1 4.0 fusion.36.wq
  26.1 18.4 %gather_fusion = bf16[2048,1024]{1,0:T(8,128)(2,1)} fusion(bf16[7648,1024]{1,0:T(8,128)(2,1)} %param.21, s32[2048]{0:T(1024)S(1)} %broadcast_clamp_fusion), kind=kCustom, calls=%fused_computation | custom fusion | bytes 8396800 | tf_op jit(solution)/shard_map/jit(_take)/gather | solution.py:885
  44.5 5.5 select_convert_fusion.part
  50.0 393.4 %embed.1 = (bf16[2048,1024]{1,0:T(8,128)(2,1)}, bf16[4,8,128,1024]{3,2,1,0:T(8,128)(2,1)}, bf16[4,8,128,1024]{3,2,1,0:T(8,128)(2,1)}, bf16[4,8,128,1024]{3,2,1,0...) custom-call(f32[2048,1024]{1,0:T(8,128)} %select_convert_fusion.part, ...), custom_call_target="tpu_custom_call" | custom-call | flops 20000000000 | bytes 83886080 | tf_op jit(solution)/shard_map/embed/pallas_call | solution.py:352
  450.7 3.1 fusion.70
  454.8 6.8 fusion.47
  461.6 27.0 %fusion.1 = (bf16[4,512,1024]{2,1,0:T(8,128)(2,1)S(1)}, f32[4,512,1024]{2,1,0:T(8,128)}, f32[4,512,1024]{2,1,0:T(8,128)}, f32[4,1024,512]{1,2,0:T(8,128)}) fusion(f32[4,1024]{1,0:T(4,128)S(1)} %bitcast.243, f32[4,1024,512]{1,2,0:T(8,128)} %fusion.47, f32[4,1024]{1,0:T(4,128)S(1)} %bitcast.241, bf16[4,1024,1024]{2,1,0:T(8,128)(2,1)S(1)} %bitcast.259, ...), kind=kOutput, calls=%fused_computation.6 | convolution fusion | flops 4437573632 | bytes 47218688 | tf_op jit(solution)/shard_map/sk,tkc->tsc/dot_general | solution.py:906
  488.7 4.7 fusion.71
  494.8 2.1 fusion.65
  496.8 21.5 %fusion.62 = (f32[4,1024]{1,0:T(4,128)S(1)}, bf16[4,512,1024]{2,1,0:T(8,128)(2,1)}, f32[4,1024]{1,0:T(4,128)S(1)}, bf16[4,1024,512]{1,2,0:T(8,128)(2,1)}) fusion(f32[4,512,1024]{2,1,0:T(8,128)} %get-tuple-element.63, f32[4,1024,512]{1,2,0:T(8,128)} %get-tuple-element.86, f32[4,1024]{1,0:T(4,128)S(1)} %bitcast.244, f32[4,1024,512]{1,2,0:T(8,128)} %fusion.47, ...), kind=kOutput, calls=%fused_computation.125 | convolution fusion | flops 4342145024 | bytes 52496384 | tf_op jit(solution)/shard_map/sd,tcd->tsc/dot_general | solution.py:919
  518.4 10.5 fusion.33
  528.9 14.6 %multiply_reduce_fusion = (f32[1024]{0:T(1024)S(1)}, f32[512]{0:T(512)S(1)}, f32[1024]{0:T(1024)S(1)}, f32[512,1024]{1,0:T(8,128)}) fusion(f32[512,1024]{1,0:T(8,128)S(1)} %get-tuple-element.85, f32[512]{0:T(512)S(1)} %fusion.56, f32[512]{0:T(512)S(1)} %broadcast_multiply_fusion.2, f32[1024]{0:T(1024)S(1)} %convert_element_type.108, ...), kind=kOutput, calls=%fused_computation.55 | convolution fusion | flops 4307547648 | bytes 29380608 | tf_op jit(solution)/shard_map/tsc,tkc->sk/dot_general | solution.py:927
  543.5 2.3 fusion.64
  547.2 3.3 fusion.59
  552.1 4.3 convolution_bitcast_fusion
  556.3 3.1 copy.41
  562.4 10.8 fusion.31
  573.2 8.5 fusion.52
  581.8 9.2 fusion.44
  591.0 390.4 %backward.1 = (f32[8,2048,128]{2,1,0:T(8,128)}, f32[6,64,1024]{2,1,0:T(8,128)}, bf16[2048,768]{1,0:T(8,128)(2,1)}, f32[1,768]{1,0:T(1,128)}, f32[24,4,64,1024]{3...) custom-call(f32[4,8,64,256]{3,2,1,0:T(8,128)} %bitcast.225, f32[8,64,1024]{2,1,0:T(8,128)} %bitcast.226, ...), custom_call_target="tpu_custom_call" | custom-call | flops 20000000000 | bytes 104857600 | tf_op jit(solution)/shard_map/backward/pallas_call | solution.py:630
  981.4 1.8 fusion.41
  985.2 1.9 concatenate.7
  987.2 2.5 fusion.67
  991.7 15.4 %fusion.51 = f32[1024,768]{1,0:T(8,128)} fusion(bf16[2048,1024]{1,0:T(8,128)(2,1)} %get-tuple-element.34, bf16[2048,768]{1,0:T(8,128)(2,1)} %get-tuple-element.47, s32[768]{0:T(1024)S(1)} %copy-done.17), kind=kOutput, calls=%fused_computation.87 | convolution fusion | flops 5639307264 | bytes 10488832 | tf_op jit(solution)/shard_map/dot_general | solution.py:939
  1007.1 33.6 %table_rows.1.block_in = f32[7648,128]{1,0:T(8,128)S(1)} custom-call(s32[16384]{0:T(1024)S(1)} %and_select_fusion.ids, f32[16384,128]{1,0:T(8,128)} %bitcast.221), custom_call_target="tpu_custom_call" | custom-call | flops 3000000000 | bytes 16777216 | tf_op jit(solution)/shard_map/table_rows/pallas_call | solution.py:675
  1040.8 1.9 copy-done
  1042.7 188.1 %gathered_columns.1 = f32[7648,1024]{1,0:T(8,128)} custom-call(f32[7648,128]{1,0:T(8,128)} %copy-done), custom_call_target="tpu_custom_call" | custom-call | flops 10000000000 | bytes 62914560 | tf_op jit(solution)/shard_map/gathered_columns/pallas_call | solution.py:751
  1235.2 22.8 %all-reduce.4.cloned.1.call-done = f32[1024,768]{1,0:T(8,128)} async-done(((f32[1024,768]{1,0:T(8,128)}), f32[1024,768]{1,0:T(8,128)}) %all-reduce.4.cloned.1.call-update) | async-done | bytes 3145744 | tf_op jit(solution)/shard_map/psum | solution.py:939
  1258.0 22.4 %copy.66 = f32[7648,1024]{1,0:T(8,128)} copy(f32[7648,1024]{1,0:T(8,128)} %gathered_columns.1) | data formatting | bytes 62652416
  1284.4 2.1 copy.69
  1288.1 2.1 copy.70
  1291.8 2.0 copy.71
  (129 shorter events, 44.8 us)
Async XLA Ops:
  8.0 13.0 %copy-start.16 = (s32[768]{0:T(1024)S(1)}, s32[768]{0:T(1024)}, u32[]{:S(2)}) copy-start(s32[768]{0:T(1024)} %constant.142.clone) | copy-start | bytes 9220
  8.0 982.9 %reduce-scatter.2.cloned.1.call-start = ((), (), s32[]{:S(2)}) async-start(), calls=%async_computation.3 | async-start | bytes 4325376 | tf_op jit(solution)/shard_map/reduce_scatter | solution.py:933
  450.7 3.9 slice-start.4
  450.7 4.1 slice-start.5
  454.2 7.4 slice-start.2
  454.8 6.8 slice-start.3
  454.8 33.9 %slice-start.6 = ((s8[8388608]{0:T(1024)(128)(4,1)}), s8[4194304]{0:T(1024)(128)(4,1)S(1)}, s32[]{:S(2)}) async-start(s8[8388608]{0:T(1024)(128)(4,1)} %bitcast.265), calls=%async_computation.14 | async-start | bytes 8388608
  461.6 27.1 %slice-start.7 = ((s8[8388608]{0:T(1024)(128)(4,1)}), s8[4194304]{0:T(1024)(128)(4,1)S(1)}, s32[]{:S(2)}) async-start(s8[8388608]{0:T(1024)(128)(4,1)} %bitcast.265), calls=%async_computation.15 | async-start | bytes 8388608
  488.7 4.8 copy-start.5
  543.5 3.7 copy-start.8
  550.5 1.6 copy-start.2
  550.5 680.3 %all-reduce.6.cloned.1.call-start = ((), (), s32[]{:S(2)}) async-start(), calls=%async_computation.2 | async-start | bytes 196608 | tf_op jit(solution)/shard_map/psum | solution.py:948
  559.4 2.9 copy-start.4
  562.4 10.9 copy-start.3
  562.4 10.9 copy-start.6
  562.4 19.4 %slice-start = ((s8[8388608]{0:T(1024)(128)(4,1)}), s8[4194304]{0:T(1024)(128)(4,1)S(1)}, s32[]{:S(2)}) async-start(s8[8388608]{0:T(1024)(128)(4,1)} %bitcast.216), calls=%async_computation.8 | async-start | bytes 8388608
  573.2 8.5 slice-start.1
  573.2 8.5 copy-start.7
  591.0 390.4 %copy-start.17 = (s32[768]{0:T(1024)S(1)}, s32[768]{0:T(1024)}, u32[]{:S(2)}) copy-start(s32[768]{0:T(1024)} %constant.142.clone) | copy-start | bytes 9220
  591.0 392.3 %copy-start.15 = (f32[4]{0:T(128)S(1)}, f32[4]{0:T(128)}, u32[]{:S(2)}) copy-start(f32[4]{0:T(128)} %get-tuple-element.92) | copy-start | bytes 52
  987.1 248.0 %all-gather.9.cloned.1.call-start = ((), (), s32[]{:S(2)}) async-start(), calls=%async_computation.6 | async-start | bytes 4718592 | tf_op jit(solution)/shard_map/all_gather | solution.py:940
  989.7 245.4 %all-gather.11.cloned.1.call-start = ((), (), s32[]{:S(2)}) async-start(), calls=%async_computation.7 | async-start | bytes 4718592 | tf_op jit(solution)/shard_map/all_gather | solution.py:940
  990.3 244.8 %all-gather.7.cloned.1.call-start = ((), (), s32[]{:S(2)}) async-start(), calls=%async_computation.5 | async-start | bytes 4718592 | tf_op jit(solution)/shard_map/all_gather | solution.py:940
  990.9 244.3 %all-gather.5.cloned.1.call-start = ((), (), s32[]{:S(2)}) async-start(), calls=%async_computation.4 | async-start | bytes 1179648 | tf_op jit(solution)/shard_map/all_gather | solution.py:933
  991.6 266.3 %all-reduce.4.cloned.1.call-start = ((), (), s32[]{:S(2)}) async-start(), calls=%async_computation.1 | async-start | bytes 6291456 | tf_op jit(solution)/shard_map/psum | solution.py:939
  991.7 15.4 %copy-start.14 = (s32[8,16,128]{2,1,0:T(8,128)S(1)}, s32[8,16,128]{2,1,0:T(8,128)}, u32[]{:S(2)}) copy-start(s32[8,16,128]{2,1,0:T(8,128)} %get-tuple-element.32) | copy-start | bytes 196612
  1040.7 1.9 copy-start
  1258.0 22.4 %copy-start.12 = (f32[1024,768]{1,0:T(8,128)S(1)}, f32[1024,768]{1,0:T(8,128)}, u32[]{:S(2)}) copy-start(f32[1024,768]{1,0:T(8,128)} %all-reduce.4.cloned.1.call-done) | copy-start | bytes 9437188
  1280.4 1.9 copy-start.13
  1280.4 4.0 copy-start.11
  1284.4 3.7 copy-start.9
  1288.1 3.7 copy-start.10
  (1 other events, 1.3 us)
Sparse Core Ops, SparseCore 0:
  550.6 149.9 reduce-scatter.1
  987.2 177.7 all-reduce.5
  1168.9 89.0 all-reduce.3
Sparse Core Ops, SparseCore 1:
  990.0 45.7 all-gather.8
  1038.2 52.1 all-gather.10
  1092.6 54.3 all-gather.6
  1148.9 28.1 all-gather.4

commit v3 on v2

--- a/solution.py
+++ b/solution.py
@@ -153,15 +153,15 @@
 
 EDGES = ((0, 0, 2), (0, 0, 4), (0, 0, 1), (2, 1, 4), (4, 2, 2), (2, 0, 1), (4, 0, 1), (6, 1, 1), (6, 2, 1))
 CROSS, DIAGONAL, LAST = ((0, 3, 5), (1, 4, 6)), ((3, 7), (4, 8)), {1: (2,), 3: (5,), 5: (6,), 7: (7, 8)}
-STEPS = (3, 8, 13, 19, 22, 26)
-FIRST = 17
+STEPS = (4, 10, 17, 21, 25, 29)
+FIRST = 18
 ORDER = (0, 2, 4, 1, 3, 5, 6, 7)
 
 
-def emb_kernel(n, rows, chunks, cuts, heads, part, wq, bq, cos, sin, piece, toks, *refs):
+def emb_kernel(n, rows, chunks, cuts, heads, found, mask, wq, bq, cos, sin, piece, toks, *refs):
     m = len(cuts)
     local, outs = refs[:m], refs[m + N1:N2 * m + N1]
-    out, (bias, tok_all, wall, ctx_own, q, k_all, v, ctx, top, inv, left, right, raw, low, weights, send_r, send_l, recv_l, recv_r, tsend, trecv, tself, zsend, zrecv, psend, precv, lsem, isem, osem, bsem, asend, arecv, aself) = refs[m], refs[N2 * m + N1:]
+    out, (bias, tok_all, wall, ctx_own, q, k_all, v, ctx, top, inv, part, left, right, raw, low, weights, send_r, send_l, recv_l, recv_r, tsend, trecv, tself, zsend, zrecv, psend, precv, lsem, isem, osem, bsem, asend, arecv, aself) = refs[m], refs[N2 * m + N1:]
     blocks = 8
     qb = part.shape[N0] // blocks
     per = chunks // blocks
@@ -232,8 +232,12 @@
 
     k_all[...] = jnp.zeros_like(k_all)
     v[...] = jnp.zeros_like(v)
-    for d in range(N1, n):
-        arrive(d)
+    arrive(N1)
+
+    @pl.loop(N0, blocks)
+    def _(i):
+        at_i = pl.ds(pl.multiple_of(i * qb, qb), qb)
+        part[at_i, :] = jnp.where(mask[at_i, :] > N0, found[at_i, :].astype(F32), 0.0)
 
     def done(c, value):
         out[pl.ds(pl.multiple_of(c * rows, rows), rows)] = value.astype(out.dtype)
@@ -266,6 +270,7 @@
         for copy in stored(i, rel, s % N2):
             copy.start()
     events = [(STEPS[d - N1], functools.partial(relay, d, CROSS)) for d in range(N1, n)] + [(STEPS[d + n - N2], functools.partial(relay, d, DIAGONAL)) for d in range(N1, n)]
+    events += [(N2 * d - N2, functools.partial(arrive, d)) for d in range(N2, n)]
     events += [(FIRST - N1, functools.partial(prefetch, N0))] + [(FIRST + s, functools.partial(convert, s)) for s in range(len(plan))]
 
     start = per + LAG * (n - N1)
@@ -334,8 +339,8 @@
         rcopy(piece, wall.at[z, p], bsem.at[N1], zrecv.at[z], tp=z - N1).wait_send()
 
 
-def embed(part, piece, toks, local, wq, bq, cos, sin, heads, n_tp, n_dp):
-    seq, width = part.shape
+def embed(found, mask, piece, toks, local, wq, bq, cos, sin, heads, n_tp, n_dp):
+    seq, width = found.shape
     chunks = 32
     rows = seq // chunks
     dims = wq.shape[1] // 3
@@ -353,26 +358,26 @@
         functools.partial(emb_kernel, n_tp, rows, chunks, cuts, heads),
         name='embed',
         out_shape=shapes,
-        in_specs=[VMEM] * 5 + [ANY] * (2 + len(local)),
+        in_specs=[VMEM] * 6 + [ANY] * (2 + len(local)),
         out_specs=[VMEM] + [ANY] * (4 + len(local)) + [VMEM] * 6,
-        scratch_shapes=[pltpu.VMEM((seq, width), F32)] * 2 + [pltpu.VMEM((2, lo, width), F32), pltpu.VMEM((2, lo, width), BF), pltpu.VMEM((seq, seq // 8), F32), dma, dma, dma((chunks,)), dma((chunks,)),
+        scratch_shapes=[pltpu.VMEM((seq, width), F32)] * 3 + [pltpu.VMEM((2, lo, width), F32), pltpu.VMEM((2, lo, width), BF), pltpu.VMEM((seq, seq // 8), F32), dma, dma, dma((chunks,)), dma((chunks,)),
                         dma((8,)), dma((8,)), dma, dma((n_tp,)), dma((n_tp,)), dma((n_tp, len(EDGES))), dma((n_tp, len(EDGES))), dma((len(local),)), dma((2,)), dma((2, len(local))), dma((2,)),
                         dma, dma((n_tp,)), dma],
         compiler_params=pltpu.CompilerParams(collective_id=0, has_side_effects=True, vmem_limit_bytes=60 * 2 ** 20),
         cost_estimate=pl.CostEstimate(flops=20 * 10 ** 9, bytes_accessed=80 * 2 ** 20, transcendentals=0),
-    )(part, wq, bq, cos, sin, piece, toks, *[w.reshape(n_dp, w.shape[0] // n_dp, w.shape[1]) for w in local])
+    )(found, mask, wq, bq, cos, sin, piece, toks, *[w.reshape(n_dp, w.shape[0] // n_dp, w.shape[1]) for w in local])
     m = 1 + len(local)
     return out[0], [w.reshape(n_tp, -1, w.shape[3]) for w in out[1:m]], out[m], out[m + 1], out[m + 3], out[m + 4:]
 
 
-RING = 8
+RING = 4
 HOLD, LIVE, PAIR = 4, 8, 4
 ADD, LOAD, CROSSED, LAND, PLANE = 1, 4, 5, 7, 8
 
 
-def backward_kernel(n, rows, chunks, jobs, heads, d_ctx, resid, q, k_all, v, ctx, top, inv, cos, sin, wq, *refs):
+def backward_kernel(n, rows, chunks, jobs, heads, d_ctx, resid, q, k_all, v, ctx, top, inv, cos, sin, wq, back, emb, *refs):
     prods = refs[:jobs]
-    out, grads, d_qkv, d_bias, landed, cross, last, part, left, right, total, dctx, dq, dk, dv, ctx_in, res_in, work, fresh, xin, yin, keep, pass_on, along, final, *sems = refs[jobs:]
+    out, grads, d_w, d_bias, landed, cross, last, part, left, right, total, dctx, dq, dk, dv, ctx_in, res_in, cos_in, sin_in, emb_in, work, fresh, xin, yin, keep, pass_on, along, final, *sems = refs[jobs:]
     send_r, send_l, recv_l, recv_r, osend, orecv, csend, crecv, esem, fsem, xsend, xrecv, xsem, ysend, yrecv, ysem, ksem, zrecv, frecv, asend, arecv, aself, isem = sems
     z = lax.axis_index('tp')
     p, at = plane()
@@ -414,10 +419,12 @@
     def inputs(i):
         slot = i % N2
         at_q = rows_of(i, N0, qb)
-        return [pltpu.make_async_copy(ctx.at[at_q], ctx_in.at[slot], isem.at[N0, slot]), pltpu.make_async_copy(resid.at[i], res_in.at[slot], isem.at[N1, slot])]
+        pairs = ((ctx.at[at_q], ctx_in), (resid.at[i], res_in), (cos.at[at_q], cos_in), (sin.at[at_q], sin_in), (emb.at[at_q], emb_in))
+        return [pltpu.make_async_copy(src, dst.at[slot], isem.at[j, slot]) for j, (src, dst) in enumerate(pairs)]
 
     dk[...] = jnp.zeros_like(dk)
     dv[...] = jnp.zeros_like(dv)
+    d_w[...] = jnp.zeros_like(d_w)
     d_bias[...] = jnp.zeros_like(d_bias)
     for copy in inputs(blocks - N1):
         copy.start()
@@ -441,8 +448,9 @@
 
         @pl.when(h == heads - N1)
         def _():
-            got = grad_rows(i, qb, cos, sin, dq, dk, dv, d_bias)
-            d_qkv[rows_of(i, N0, qb), :] = got
+            slot = i % N2
+            got = grad_rows(i, qb, cos_in[slot], sin_in[slot], dq, dk, dv, d_bias)
+            d_w[...] += dot(emb_in[slot], dot(got, back[...], NN).astype(BF), TN)
             part[rows_of(i, N0, qb), :] = dot(got, wq[...], NT)
             part[rows_of(i, z, share), :] = part[rows_of(i, z, share), :] + res_in[i % N2]
 
@@ -612,7 +620,7 @@
     rcopy(sent, sent, asend, arecv.at[N0], tp=z).wait_send()
 
 
-def backward(d_ctx, resid, saved, cos, sin, wq, prods, heads, n_tp, n_dp):
+def backward(d_ctx, resid, saved, cos, sin, wq, back, emb, prods, heads, n_tp, n_dp):
     q, k, v, ctx, top, inv = saved
     seq, dims = q.shape
     width = wq.shape[0]
@@ -624,21 +632,23 @@
     dma = pltpu.SemaphoreType.DMA
     shape = jax.ShapeDtypeStruct
     qb = seq // 8
-    vmem = [(seq, width)] * 3 + [(RING, rows, width), (seq, dims), (qb, dims), (seq, dims), (seq, dims), (2, qb, dims), (2, qb // n_tp, width),
+    vmem = [(seq, width)] * 3 + [(RING, rows, width), (seq, dims), (qb, dims), (seq, dims), (seq, dims), (2, qb, dims), (2, qb // n_tp, width)] + [(2, qb, dims // 2)] * 2 + [
             (HOLD, 4) + piece, (4,) + piece, (2, 2) + piece, (2,) + piece, (LIVE,) + piece, (PAIR,) + piece, (units,) + piece, (2 * jobs,) + piece]
-    sems = [(), (), (chunks,), (chunks,), (RING,), (8,), (), (units,), (HOLD,), (), (HOLD,), (units,), (2,), (PAIR,), (units,), (2,), (LIVE,), (units,), (2 * jobs,), (), (8,), (8,), (2, 2)]
-    cols, grads, d_qkv, d_bias, *_ = pl.pallas_call(
+    sems = [(), (), (chunks,), (chunks,), (RING,), (8,), (), (units,), (HOLD,), (), (HOLD,), (units,), (2,), (PAIR,), (units,), (2,), (LIVE,), (units,), (2 * jobs,), (), (8,), (8,), (5, 2)]
+    scratch = [pltpu.VMEM(size, F32) for size in vmem]
+    scratch.insert(12, pltpu.VMEM((2, qb, width), BF))
+    cols, grads, d_w, d_bias, *_ = pl.pallas_call(
         functools.partial(backward_kernel, n_tp, rows, chunks, jobs, heads),
         name='backward',
-        out_shape=(shape((n_dp, seq, width // n_dp), F32), shape((2 * jobs,) + piece, F32), shape((seq, 3 * dims), BF), shape((1, 3 * dims), F32),
+        out_shape=(shape((n_dp, seq, width // n_dp), F32), shape((2 * jobs,) + piece, F32), shape((width, 3 * dims), F32), shape((1, 3 * dims), F32),
                    shape((units, 4) + piece, F32), shape((units, 2) + piece, F32), shape((units,) + piece, F32)),
-        in_specs=[ANY, ANY] + [VMEM] * 3 + [ANY] + [VMEM] * 5 + [ANY] * jobs,
+        in_specs=[ANY, ANY] + [VMEM] * 3 + [ANY] + [VMEM] * 2 + [ANY] * 2 + [VMEM] * 2 + [ANY] * (1 + jobs),
         out_specs=(ANY, ANY, VMEM, VMEM, ANY, ANY, ANY),
-        scratch_shapes=[pltpu.VMEM(size, F32) for size in vmem] + [dma(size) for size in sems],
-        compiler_params=pltpu.CompilerParams(collective_id=1, has_side_effects=True, vmem_limit_bytes=63 * 2 ** 20),
+        scratch_shapes=scratch + [dma(size) for size in sems],
+        compiler_params=pltpu.CompilerParams(collective_id=1, has_side_effects=True, vmem_limit_bytes=67_000_000),
         cost_estimate=pl.CostEstimate(flops=20 * 10 ** 9, bytes_accessed=100 * 2 ** 20, transcendentals=0),
-    )(d_ctx, resid, q, k, v, ctx, top, inv, cos, sin, wq, *prods)
-    return d_qkv, d_bias, cols, grads.reshape(jobs, 2 * piece[0], piece[1])
+    )(d_ctx, resid, q, k, v, ctx, top, inv, cos, sin, wq, back, emb, *prods)
+    return d_w, d_bias, cols, grads.reshape(jobs, 2 * piece[0], piece[1])
 
 
 WAYS = 4
@@ -851,7 +861,7 @@
 
 def grad_rows(i, qb, cos, sin, dq, dk, dv, d_bias):
     at_q = pl.ds(pl.multiple_of(i * qb, qb), qb)
-    back = [turned(values, cos[at_q, :], -sin[at_q, :]) for values in (dq[...], dk[at_q, :])]
+    back = [turned(values, cos, -sin) for values in (dq[...], dk[at_q, :])]
     rows = jnp.concatenate(back + [dv[at_q, :]], axis=1)
     d_bias[...] += jnp.sum(rows, axis=0, keepdims=True)
     return rows.astype(BF)
@@ -882,14 +892,14 @@
         local_ids = tokens - tp * vocab_loc
         in_shard = (local_ids >= N0) & (local_ids < vocab_loc)
         safe_ids = jnp.where(in_shard, local_ids, N0)
-        own_rows = jnp.where(in_shard[:, None], jnp.take(emb_table, safe_ids, axis=N0), 0.0).astype(F32)
+        found = jnp.take(emb_table, safe_ids, axis=N0)
         dims = heads * head_dim
         place = column_order(heads, head_dim)
         swap = (jnp.arange(3 * dims)[:, None] == jnp.asarray(place)[None, :]).astype(BF)
         wq = jnp.dot(w_qkv, swap, preferred_element_type=F32).astype(BF)
         bq = jnp.dot(b_qkv.reshape(N1, -N1), swap, preferred_element_type=F32)
         cos_tab, sin_tab = rope_tables(seq_len, head_dim, heads)
-        emb_bf, (wg_full, wl_full, wd_full, wo_full), biases, tok_all, ctx_own, saved = embed(own_rows, piece, tokens.reshape(-N1, min(128, seq_len // 8)), (w_gate, w_lin, w_down, w_out), wq, bq, cos_tab, sin_tab, heads, n_tp, n_dp)
+        emb_bf, (wg_full, wl_full, wd_full, wo_full), biases, tok_all, ctx_own, saved = embed(found, in_shard[:, None].astype(F32), piece, tokens.reshape(-N1, min(128, seq_len // 8)), (w_gate, w_lin, w_down, w_out), wq, bq, cos_tab, sin_tab, heads, n_tp, n_dp)
         ctx_own = ctx_own.reshape(n_tp, own, dims).astype(BF)
         is_own = (jnp.arange(n_tp) == tp)[:, None]
         bg_full, bl_full = [jnp.where(is_own, b[None].astype(F32), biases[:, i]) for i, b in enumerate((b_gate, b_lin))]
@@ -932,11 +942,11 @@
         d_w_out = jnp.einsum('hse,sd->hed', ctx_own, d_attn_bf, preferred_element_type=F32)
         d_w_out = lax.all_gather(lax.psum_scatter(d_w_out.reshape(-N1, width), ALL, scatter_dimension=N0, tiled=True), 'dp', axis=N0, tiled=True)
         d_ctx = jnp.einsum('sd,hed->hse', d_attn_bf, wo_full, preferred_element_type=F32)
-        d_qkv, d_b_qkv, d_cols, mine = backward(
-            d_ctx.reshape(n_tp, blocks, own // blocks, dims), (ALPHA * d_resid_one).reshape(blocks, own // blocks, width), saved, cos_tab, sin_tab, wq,
+        d_w_qkv, d_b_qkv, d_cols, mine = backward(
+            d_ctx.reshape(n_tp, blocks, own // blocks, dims), (ALPHA * d_resid_one).reshape(blocks, own // blocks, width), saved, cos_tab, sin_tab, wq, swap.T, emb_bf,
             (prod_gate, prod_lin, prod_down), heads, n_tp, n_dp)
         d_b_qkv = jnp.dot(d_b_qkv, swap.astype(F32).T, precision=lax.Precision.HIGHEST)[N0]
-        d_w_qkv = lax.psum(jnp.dot(emb_bf.T, jnp.dot(d_qkv, swap.T, preferred_element_type=F32).astype(BF), preferred_element_type=F32), 'dp')
+        d_w_qkv = lax.psum(d_w_qkv, 'dp')
         d_w_gate, d_w_lin, d_w_down = [lax.all_gather(grad, 'dp', axis=N0, tiled=True) for grad in mine]
         all_ids = tok_all.reshape(-N1) - tp * vocab_loc
         all_ids = jnp.where((all_ids >= N0) & (all_ids < vocab_loc), all_ids, vocab_loc)

time: 1310 us -> 1390 us (1.061)
  waiting for transfers between devices: 24.6 us -> 178 us
  Pallas kernels: 1010 us -> 951 us
  matrix products: 147 us -> 132 us
    all_gather x3, waiting for transfers between devices: 0.03 us -> 116 us  [device_step(): lax.all_gather(grad, 'dp', axis=N0, tiled=True)]
    pallas_call x1, Pallas kernels: 188 us -> 147 us  [gathered_columns(): pl.pallas_call(functools.partial(gather_kernel, parts), name='gathered_co...]
    all_gather x1, waiting for transfers between devices: 0.02 us -> 25 us  [device_step(): lax.all_gather(lax.psum_scatter(d_w_out.reshape(-N1, width), ALL, scatter...]
    pallas_call x1, Pallas kernels: 393 us -> 377 us  [embed(): pl.pallas_call(functools.partial(emb_kernel, n_tp, rows, chunks, cuts, he...]
    dot_general x1 -> x0, matrix products: 15.4 us -> none  [device_step(): jnp.dot(emb_bf.T, jnp.dot(d_qkv, swap.T, preferred_element_type=F32).asty...]
    unnamed x60 -> x72, local copies, waits for them, and re-layouts: 42.2 us -> 40.9 us
  transfers between devices with their start and end apart: 7 -> 7, of which waited for: 1 -> 5; matrix products, arithmetic and copies ran while one was open for 5% -> 4% of each run, Pallas kernels for 47% -> 42%
where the time goes in v3:
time: 1390 us; the launch traced here: 1380 us
  Pallas kernels  951 us (68%)
  waiting for transfers between devices  178 us (13%)
  matrix products  132 us (9%)
  local copies, waits for them, and re-layouts  78.5 us (6%)
  other arithmetic  26.3 us (2%)
  between operations  15.1 us (1%)
    pallas_call x1, Pallas kernels, backward(): pl.pallas_call(functools.partial(backward_kernel, n_tp, rows, chunks, job...  393 us
    pallas_call x1, Pallas kernels, embed(): pl.pallas_call(functools.partial(emb_kernel, n_tp, rows, chunks, cuts, he...  377 us
    pallas_call x1, Pallas kernels, gathered_columns(): pl.pallas_call(functools.partial(gather_kernel, parts), name='gathered_co...  147 us
    all_gather x3, waiting for transfers between devices, device_step(): lax.all_gather(grad, 'dp', axis=N0, tiled=True)  116 us
    unnamed x72, local copies, waits for them, and re-layouts  40.9 us
    psum x1, waiting for transfers between devices, device_step(): d_w_qkv = lax.psum(d_w_qkv, 'dp')  34.6 us
    pallas_call x1, Pallas kernels, table_rows(): pl.pallas_call(table_kernel, name='table_rows', grid_spec=pltpu.PrefetchS...  33.4 us
    dot_general x3, matrix products, product(): jnp.einsum(spec, lhs, rhs, preferred_element_type=F32)  28.6 us
  transfers between devices with their start and end apart: 7, of which 5 were waited for; matrix products, arithmetic and copies ran while one was open for 4% of the time, Pallas kernels for 42%

profile of v3, /device:TPU:0, one launch (start us, length us, event | category | flops | bytes accessed | tf_op | source)
XLA Modules:
  0.0 1380.6 jit_solution(15004954248398478828)
XLA Ops:
  19.9 4.0 fusion.37.wq
  23.9 18.4 %gather_fusion = bf16[2048,1024]{1,0:T(8,128)(2,1)} fusion(bf16[7648,1024]{1,0:T(8,128)(2,1)} %param.21, s32[2048]{0:T(1024)S(1)} %broadcast_clamp_fusion), kind=kCustom, calls=%fused_computation | custom fusion | bytes 8396800 | tf_op jit(solution)/shard_map/jit(_take)/gather | solution.py:895
  42.3 3.9 broadcast_select_fusion.found
  46.1 377.2 %embed.1 = (bf16[2048,1024]{1,0:T(8,128)(2,1)}, bf16[4,8,128,1024]{3,2,1,0:T(8,128)(2,1)}, bf16[4,8,128,1024]{3,2,1,0:T(8,128)(2,1)}, bf16[4,8,128,1024]{3,2,1,0...) custom-call(bf16[2048,1024]{1,0:T(8,128)(2,1)} %broadcast_select_fus, ...), custom_call_target="tpu_custom_call" | custom-call | flops 20000000000 | bytes 83886080 | tf_op jit(solution)/shard_map/embed/pallas_call | solution.py:357
  430.5 3.1 fusion.71
  434.6 6.8 fusion.48
  441.4 26.9 %fusion.1 = (bf16[4,512,1024]{2,1,0:T(8,128)(2,1)S(1)}, f32[4,512,1024]{2,1,0:T(8,128)}, f32[4,512,1024]{2,1,0:T(8,128)}, f32[4,1024,512]{1,2,0:T(8,128)}) fusion(f32[4,1024]{1,0:T(4,128)S(1)} %bitcast.240, f32[4,1024,512]{1,2,0:T(8,128)} %fusion.48, f32[4,1024]{1,0:T(4,128)S(1)} %bitcast.238, bf16[4,1024,1024]{2,1,0:T(8,128)(2,1)S(1)} %bitcast.255, ...), kind=kOutput, calls=%fused_computation.6 | convolution fusion | flops 4437573632 | bytes 47218688 | tf_op jit(solution)/shard_map/sk,tkc->tsc/dot_general | solution.py:916
  468.3 4.7 fusion.72
  474.4 2.1 fusion.66
  476.5 22.1 %fusion.63 = (f32[4,1024]{1,0:T(4,128)S(1)}, bf16[4,512,1024]{2,1,0:T(8,128)(2,1)}, f32[4,1024]{1,0:T(4,128)}, bf16[4,1024,512]{1,2,0:T(8,128)(2,1)}) fusion(f32[4,512,1024]{2,1,0:T(8,128)} %get-tuple-element.63, f32[4,1024,512]{1,2,0:T(8,128)} %get-tuple-element.82, f32[4,1024]{1,0:T(4,128)S(1)} %bitcast.241, f32[4,1024,512]{1,2,0:T(8,128)} %fusion.48, ...), kind=kOutput, calls=%fused_computation.125 | convolution fusion | flops 4342145024 | bytes 52496384 | tf_op jit(solution)/shard_map/sd,tcd->tsc/dot_general | solution.py:929
  498.6 10.5 fusion.34
  509.1 14.6 %multiply_reduce_fusion = (f32[1024]{0:T(1024)S(1)}, f32[512]{0:T(512)S(1)}, f32[1024]{0:T(1024)S(1)}, f32[512,1024]{1,0:T(8,128)}) fusion(f32[512,1024]{1,0:T(8,128)S(1)} %get-tuple-element.81, f32[512]{0:T(512)S(1)} %fusion.57, f32[512]{0:T(512)S(1)} %broadcast_multiply_fusion.2, f32[1024]{0:T(1024)S(1)} %convert_element_type.106, ...), kind=kOutput, calls=%fused_computation.57 | convolution fusion | flops 4307547648 | bytes 29380608 | tf_op jit(solution)/shard_map/tsc,tkc->sk/dot_general | solution.py:937
  523.7 2.3 fusion.65
  527.4 3.4 fusion.60
  532.4 4.3 convolution_bitcast_fusion
  536.7 3.1 copy.44
  542.7 10.9 fusion.32
  553.5 8.5 fusion.53
  562.1 9.2 fusion.45
  571.3 392.6 %backward.1 = (f32[8,2048,128]{2,1,0:T(8,128)}, f32[6,64,1024]{2,1,0:T(8,128)}, f32[1024,768]{1,0:T(8,128)}, f32[1,768]{1,0:T(1,128)}, f32[24,4,64,1024]{3,2,1,0...) custom-call(f32[4,8,64,256]{3,2,1,0:T(8,128)} %bitcast.222, f32[8,64,1024]{2,1,0:T(8,128)} %bitcast.223, ...), custom_call_target="tpu_custom_call" | custom-call | flops 20000000000 | bytes 104857600 | tf_op jit(solution)/shard_map/backward/pallas_call | solution.py:640
  968.4 2.7 concatenate.7
  975.0 33.4 %table_rows.1.block_in = f32[7648,128]{1,0:T(8,128)S(1)} custom-call(s32[16384]{0:T(1024)S(1)} %and_select_fusion.ids, f32[16384,128]{1,0:T(8,128)} %bitcast.218), custom_call_target="tpu_custom_call" | custom-call | flops 3000000000 | bytes 16777216 | tf_op jit(solution)/shard_map/table_rows/pallas_call | solution.py:685
  1010.3 147.4 %gathered_columns.1 = f32[7648,1024]{1,0:T(8,128)} custom-call(f32[7648,128]{1,0:T(8,128)} %copy-done), custom_call_target="tpu_custom_call" | custom-call | flops 10000000000 | bytes 62914560 | tf_op jit(solution)/shard_map/gathered_columns/pallas_call | solution.py:761
  1162.0 34.6 %all-reduce.4.cloned.1.call-done = f32[1024,768]{1,0:T(8,128)} async-done(((f32[1024,768]{1,0:T(8,128)}), f32[1024,768]{1,0:T(8,128)}) %all-reduce.4.cloned.1.call-update) | async-done | bytes 3145744 | tf_op jit(solution)/shard_map/psum | solution.py:949
  1196.5 38.6 %all-gather.9.cloned.1.call-done = f32[1024,1024]{1,0:T(8,128)} async-done(((f32[128,1024]{1,0:T(8,128)}), f32[1024,1024]{1,0:T(8,128)}) %all-gather.9.cloned.1.call-update) | async-done | bytes 4194320 | tf_op jit(solution)/shard_map/all_gather | solution.py:950
  1235.2 38.6 %all-gather.11.cloned.1.call-done = f32[1024,1024]{1,0:T(8,128)} async-done(((f32[128,1024]{1,0:T(8,128)}), f32[1024,1024]{1,0:T(8,128)}) %all-gather.11.cloned.1.call-update) | async-done | bytes 4194320 | tf_op jit(solution)/shard_map/all_gather | solution.py:950
  1273.8 38.6 %all-gather.7.cloned.1.call-done = f32[1024,1024]{1,0:T(8,128)} async-done(((f32[128,1024]{1,0:T(8,128)}), f32[1024,1024]{1,0:T(8,128)}) %all-gather.7.cloned.1.call-update) | async-done | bytes 4194320 | tf_op jit(solution)/shard_map/all_gather | solution.py:950
  1312.5 25.0 %all-gather.5.cloned.1.call-done = f32[256,1024]{1,0:T(8,128)} async-done(((f32[32,1024]{1,0:T(8,128)}), f32[256,1024]{1,0:T(8,128)}) %all-gather.5.cloned.1.call-update) | async-done | bytes 1048592 | tf_op jit(solution)/shard_map/all_gather | solution.py:943
  1337.5 22.4 %copy.70 = f32[7648,1024]{1,0:T(8,128)} copy(f32[7648,1024]{1,0:T(8,128)} %gathered_columns.1) | data formatting | bytes 62652416
  1363.9 2.1 copy.73
  1367.6 2.1 copy.74
  1371.3 2.0 copy.75
  (145 shorter events, 49.4 us)
Async XLA Ops:
  7.2 6.7 copy-start.23
  7.2 6.7 copy-start.18
  7.2 6.7 copy-start.19
  7.2 6.7 copy-start.20
  7.2 6.7 copy-start.21
  7.2 6.8 copy-start.22
  7.2 967.1 %reduce-scatter.2.cloned.1.call-start = ((), (), s32[]{:S(2)}) async-start(), calls=%async_computation.3 | async-start | bytes 4325376 | tf_op jit(solution)/shard_map/reduce_scatter | solution.py:943
  12.7 6.1 copy-start.16
  430.5 3.9 slice-start.4
  430.5 4.1 slice-start.5
  434.0 7.4 slice-start.2
  434.6 6.8 slice-start.3
  434.6 33.7 %slice-start.6 = ((s8[8388608]{0:T(1024)(128)(4,1)}), s8[4194304]{0:T(1024)(128)(4,1)S(1)}, s32[]{:S(2)}) async-start(s8[8388608]{0:T(1024)(128)(4,1)} %bitcast.261), calls=%async_computation.14 | async-start | bytes 8388608
  441.4 26.9 %slice-start.7 = ((s8[8388608]{0:T(1024)(128)(4,1)}), s8[4194304]{0:T(1024)(128)(4,1)S(1)}, s32[]{:S(2)}) async-start(s8[8388608]{0:T(1024)(128)(4,1)} %bitcast.261), calls=%async_computation.15 | async-start | bytes 8388608
  468.3 4.8 copy-start.5
  530.8 8.9 copy-start.17
  530.9 626.9 %all-reduce.6.cloned.1.call-start = ((), (), s32[]{:S(2)}) async-start(), calls=%async_computation.2 | async-start | bytes 196608 | tf_op jit(solution)/shard_map/psum | solution.py:958
  542.7 10.9 copy-start.3
  542.7 10.9 copy-start.6
  542.7 19.4 %slice-start = ((s8[8388608]{0:T(1024)(128)(4,1)}), s8[4194304]{0:T(1024)(128)(4,1)S(1)}, s32[]{:S(2)}) async-start(s8[8388608]{0:T(1024)(128)(4,1)} %bitcast.213), calls=%async_computation.8 | async-start | bytes 8388608
  553.5 8.5 slice-start.1
  553.5 8.5 copy-start.7
  963.9 8.0 copy-start.13
  968.4 5.9 copy-start.15
  971.1 225.5 %all-reduce.4.cloned.1.call-start = ((), (), s32[]{:S(2)}) async-start(), calls=%async_computation.1 | async-start | bytes 6291456 | tf_op jit(solution)/shard_map/psum | solution.py:949
  971.8 263.4 %all-gather.9.cloned.1.call-start = ((), (), s32[]{:S(2)}) async-start(), calls=%async_computation.6 | async-start | bytes 4718592 | tf_op jit(solution)/shard_map/all_gather | solution.py:950
  973.1 300.8 %all-gather.11.cloned.1.call-start = ((), (), s32[]{:S(2)}) async-start(), calls=%async_computation.7 | async-start | bytes 4718592 | tf_op jit(solution)/shard_map/all_gather | solution.py:950
  973.7 338.8 %all-gather.7.cloned.1.call-start = ((), (), s32[]{:S(2)}) async-start(), calls=%async_computation.5 | async-start | bytes 4718592 | tf_op jit(solution)/shard_map/all_gather | solution.py:950
  974.2 363.3 %all-gather.5.cloned.1.call-start = ((), (), s32[]{:S(2)}) async-start(), calls=%async_computation.4 | async-start | bytes 1179648 | tf_op jit(solution)/shard_map/all_gather | solution.py:943
  1337.5 22.4 %copy-start.12 = (f32[1024,768]{1,0:T(8,128)S(1)}, f32[1024,768]{1,0:T(8,128)}, u32[]{:S(2)}) copy-start(f32[1024,768]{1,0:T(8,128)} %all-reduce.4.cloned.1.call-done) | copy-start | bytes 9437188
  1359.9 4.0 copy-start.11
  1363.9 3.7 copy-start.9
  (7 other events, 17.0 us)
Sparse Core Ops, SparseCore 0:
  531.0 150.6 reduce-scatter.1
  971.2 136.4 all-reduce.5
  1111.0 85.5 all-reduce.3
  1198.8 36.2 all-gather.8
  1237.5 36.2 all-gather.10
  1276.1 36.2 all-gather.6
  1314.4 23.0 all-gather.4

commit v4 on v3

--- a/solution.py
+++ b/solution.py
@@ -373,12 +373,57 @@
 RING = 4
 HOLD, LIVE, PAIR = 4, 8, 4
 ADD, LOAD, CROSSED, LAND, PLANE = 1, 4, 5, 7, 8
+GATHER = (37, 41)
+
+
+def block_of(ref, at, rel, side):
+    return ref.at[at(rel)] if side == 0 else ref.at[at(rel), side - 1]
+
+
+class Spread:
+    def __init__(self, at, block, send, recv, own=None):
+        self.at, self.block, self.send, self.recv, self.own = at, block, send, recv, own
+
+    def copy(self, j, rel, side, to):
+        dst = self.block(rel, side)
+        src = self.own if rel == 0 and self.own is not None else dst
+        return rcopy(src, dst, self.send.at[j], self.recv.at[j], dp=self.at(to))
+
+    def give(self, j):
+        self.copy(j, *EDGES[j]).start()
+
+    def take(self, j):
+        rel, side, to = EDGES[j]
+        self.copy(j, rel ^ to, side, 0).wait_recv()
+
+    def start(self):
+        for j in range(3):
+            self.give(j)
+
+    def relay(self, moves):
+        for first, *rest in moves:
+            self.take(first)
+            for j in rest:
+                self.give(j)
+
+    def cross(self):
+        self.relay(CROSS)
+
+    def diagonal(self):
+        self.relay(DIAGONAL)
+
+    def finish(self):
+        for j in (2, 5, 6, 7, 8):
+            self.take(j)
+        for j, (rel, side, _) in enumerate(EDGES):
+            self.copy(j, rel, side, 0).wait_send()
 
 
 def backward_kernel(n, rows, chunks, jobs, heads, d_ctx, resid, q, k_all, v, ctx, top, inv, cos, sin, wq, back, emb, *refs):
     prods = refs[:jobs]
-    out, grads, d_w, d_bias, landed, cross, last, part, left, right, total, dctx, dq, dk, dv, ctx_in, res_in, cos_in, sin_in, emb_in, work, fresh, xin, yin, keep, pass_on, along, final, *sems = refs[jobs:]
-    send_r, send_l, recv_l, recv_r, osend, orecv, csend, crecv, esem, fsem, xsend, xrecv, xsem, ysend, yrecv, ysem, ksem, zrecv, frecv, asend, arecv, aself, isem = sems
+    whole = refs[jobs:N2 * jobs - N1]
+    out, grads, d_w, d_bias, landed, cross, last, part, left, right, total, dctx, dq, dk, dv, ctx_in, res_in, cos_in, sin_in, emb_in, work, fresh, xin, yin, keep, pass_on, along, final, *sems = refs[N2 * jobs - N1:]
+    send_r, send_l, recv_l, recv_r, osend, orecv, csend, crecv, esem, fsem, xsend, xrecv, xsem, ysend, yrecv, ysem, ksem, zrecv, frecv, asend, arecv, aself, isem, gsend, grecv = sems
     z = lax.axis_index('tp')
     p, at = plane()
     entry_barrier(z, n, at)
@@ -543,9 +588,11 @@
             def _():
                 rcopy(keep.at[slot], final.at[mine], ksem.at[slot], frecv.at[mine], tp=z - N1).start()
 
-            @pl.when(ok & (z == t))
-            def _():
-                pltpu.make_async_copy(keep.at[slot], grads.at[mine], ksem.at[slot]).start()
+            for m in range(jobs):
+                @pl.when(ok & (z == t) & (u // span == m))
+                def _(m=m):
+                    dst = whole[m].at[p, u % N2] if m < jobs - N1 else grads.at[u % N2]
+                    pltpu.make_async_copy(keep.at[slot], dst, ksem.at[slot]).start()
         else:
             @pl.when(ok & (((z > N0) & (z <= t)) | ((z > t) & (z < n - N1))))
             def _():
@@ -555,6 +602,8 @@
                 def _():
                     add_from(final.at[mine], frecv.at[mine])
 
+    spread = [Spread(at, functools.partial(block_of, whole[m], at), gsend.at[m], grecv.at[m]) for m in range(jobs - N1)]
+
     def place(c):
         return (blocks - N1 - c // per) * per + c % per
 
@@ -603,6 +652,9 @@
             staged(k, offset, stage)
         for t in range(n):
             along_tp(k, t, True)
+        for m, gather in enumerate(spread):
+            for offset, stage in ((N0, gather.start), (3, gather.cross), (6, gather.diagonal)):
+                pl.when(k == GATHER[m] + offset)(stage)
 
     chain_drain(z, n, part, left, right, send_r, send_l, recv_l, recv_r)
     for c in range(max(N0, chunks - RING), chunks):
@@ -616,6 +668,8 @@
     for slot in range(LIVE):
         pltpu.make_async_copy(keep.at[slot], keep.at[slot], ksem.at[slot]).wait()
     rcopy(landed, landed, csend, crecv.at[N0], dp=p).wait_send()
+    for gather in spread:
+        gather.finish()
     sent = dctx.at[pl.ds(N0, (n - N1) * share * blocks)]
     rcopy(sent, sent, asend, arecv.at[N0], tp=z).wait_send()
 
@@ -634,21 +688,22 @@
     qb = seq // 8
     vmem = [(seq, width)] * 3 + [(RING, rows, width), (seq, dims), (qb, dims), (seq, dims), (seq, dims), (2, qb, dims), (2, qb // n_tp, width)] + [(2, qb, dims // 2)] * 2 + [
             (HOLD, 4) + piece, (4,) + piece, (2, 2) + piece, (2,) + piece, (LIVE,) + piece, (PAIR,) + piece, (units,) + piece, (2 * jobs,) + piece]
-    sems = [(), (), (chunks,), (chunks,), (RING,), (8,), (), (units,), (HOLD,), (), (HOLD,), (units,), (2,), (PAIR,), (units,), (2,), (LIVE,), (units,), (2 * jobs,), (), (8,), (8,), (5, 2)]
+    sems = [(), (), (chunks,), (chunks,), (RING,), (8,), (), (units,), (HOLD,), (), (HOLD,), (units,), (2,), (PAIR,), (units,), (2,), (LIVE,), (units,), (2 * jobs,), (), (8,), (8,), (5, 2), (jobs - 1, len(EDGES)), (jobs - 1, len(EDGES))]
     scratch = [pltpu.VMEM(size, F32) for size in vmem]
     scratch.insert(12, pltpu.VMEM((2, qb, width), BF))
-    cols, grads, d_w, d_bias, *_ = pl.pallas_call(
+    full = shape((n_dp, 2) + piece, F32)
+    *whole, cols, grads, d_w, d_bias, _, _, _ = pl.pallas_call(
         functools.partial(backward_kernel, n_tp, rows, chunks, jobs, heads),
         name='backward',
-        out_shape=(shape((n_dp, seq, width // n_dp), F32), shape((2 * jobs,) + piece, F32), shape((width, 3 * dims), F32), shape((1, 3 * dims), F32),
-                   shape((units, 4) + piece, F32), shape((units, 2) + piece, F32), shape((units,) + piece, F32)),
+        out_shape=[full] * (jobs - 1) + [shape((n_dp, seq, width // n_dp), F32), shape((2,) + piece, F32), shape((width, 3 * dims), F32), shape((1, 3 * dims), F32),
+                   shape((units, 4) + piece, F32), shape((units, 2) + piece, F32), shape((units,) + piece, F32)],
         in_specs=[ANY, ANY] + [VMEM] * 3 + [ANY] + [VMEM] * 2 + [ANY] * 2 + [VMEM] * 2 + [ANY] * (1 + jobs),
-        out_specs=(ANY, ANY, VMEM, VMEM, ANY, ANY, ANY),
+        out_specs=[ANY] * (jobs - 1) + [ANY, ANY, VMEM, VMEM, ANY, ANY, ANY],
         scratch_shapes=scratch + [dma(size) for size in sems],
         compiler_params=pltpu.CompilerParams(collective_id=1, has_side_effects=True, vmem_limit_bytes=67_000_000),
         cost_estimate=pl.CostEstimate(flops=20 * 10 ** 9, bytes_accessed=100 * 2 ** 20, transcendentals=0),
     )(d_ctx, resid, q, k, v, ctx, top, inv, cos, sin, wq, back, emb, *prods)
-    return d_w, d_bias, cols, grads.reshape(jobs, 2 * piece[0], piece[1])
+    return d_w, d_bias, cols, whole, grads
 
 
 WAYS = 4
@@ -698,76 +753,138 @@
     )(ids, rows)
 
 
-SPREAD = ((0, 2), (0, 4), (0, 1), (2, 4), (4, 2), (2, 1), (4, 1), (6, 1))
-
-
-def gather_kernel(parts, block_in, out, send, recv, oself):
+def finish_kernel(n, cuts, col, down, proj, d_w, small, table, down_all, proj_all, qkv_all, total, landed, work, cross, last, mine, inbox, sem, send, recv, dsend, drecv, osem, csem, xsend, xrecv, ysend, yrecv, rsend, rrecv):
+    z = lax.axis_index('tp')
     p, at = plane()
-    bar = pltpu.get_barrier_semaphore()
-    for rel in (1, 2, 4):
-        pl.semaphore_signal(bar, inc=1, device_id={'dp': at(rel)}, device_id_type=MESH)
-    pl.semaphore_wait(bar, 3)
-    size, block = block_in.shape
-    rows = size // parts
-    half = parts // 2
-
-    def copy(j, rel, i, to):
-        dst = out.at[pl.ds(i * rows, rows), pl.ds(pl.multiple_of(at(rel) * block, block), block)]
-        src = block_in.at[pl.ds(i * rows, rows)] if rel == 0 else dst
-        return rcopy(src, dst, send.at[j, i], recv.at[j, i], dp=at(to))
-
-    def give(j, i):
-        copy(j, SPREAD[j][0], i, SPREAD[j][1]).start()
-
-    def take(j, i):
-        rel, to = SPREAD[j]
-        copy(j, rel ^ to, i, 0).wait_recv()
-    own = pltpu.make_async_copy(block_in, out.at[:, pl.ds(pl.multiple_of(p * block, block), block)], oself)
-    own.start()
-    order_x = list(range(parts))
-    order_y = order_x[half:] + order_x[:half]
-    for i, j in zip(order_x, order_y):
-        give(0, i)
-        give(1, j)
-    for i in order_x:
-        give(2, i)
-    for i, j in zip(order_x, order_y):
-        take(0, i)
-        if i < half:
-            give(3, i)
-        give(5, i)
-        take(1, j)
-        if j >= half:
-            give(4, j)
-        give(6, j)
-    for i in order_x[:half]:
-        for via, part in ((3, i), (4, i + half)):
-            take(via, part)
-            give(7, part)
-    for i in order_x:
-        for j in (2, 5, 6, 7):
-            take(j, i)
-    for i in order_x:
-        for j, (rel, to) in enumerate(SPREAD):
-            if j != (4 if i < half else 3):
-                copy(j, rel, i, 0).wait_send()
-    own.wait()
-
-
-def gathered_columns(block_in, n_dp):
-    size, block = block_in.shape
-    parts = 4
+    entry_barrier(z, n, at)
+    block = col.shape[N1]
+    half = len(cuts) // N2
+
+    def part(i):
+        def region(rel, side):
+            return table.at[pl.ds(cuts[i][N0], cuts[i][N1] - cuts[i][N0]), pl.ds(pl.multiple_of(at(rel) * block, block), block)]
+        return Spread(at, region, send.at[i], recv.at[i], col.at[pl.ds(cuts[i][N0], cuts[i][N1] - cuts[i][N0])])
+    parts = [part(i) for i in range(len(cuts))]
+    spread = [Spread(at, functools.partial(block_of, ref, at), dsend.at[i], drecv.at[i], own) for i, (ref, own) in enumerate(((down_all, down), (proj_all, proj), (qkv_all, mine)))]
+    own_copies = [pltpu.make_async_copy(col, table.at[:, pl.ds(pl.multiple_of(p * block, block), block)], osem.at[N0])]
+    own_copies += [pltpu.make_async_copy(src, dst.at[p], osem.at[i]) for i, (src, dst) in enumerate(((down, down_all), (proj, proj_all), (mine, qkv_all)), N1)]
+    order = list(range(len(cuts)))
+    flipped = order[half:] + order[:half]
+    peers = [{'dp': at(N1)}, {'dp': at(N2)}, {'dp': at(4)}, {'tp': z + N1 - N2 * (z % N2)}, {'tp': (z + n // N2) % n}]
+
+    def next_part(i):
+        parts[order[i]].give(N0)
+        parts[flipped[i]].give(N1)
+        parts[order[i]].give(N2)
+
+    def relay_part(i):
+        one, two = order[i], flipped[i]
+        parts[one].take(N0)
+        if one < half:
+            parts[one].give(3)
+        parts[one].give(5)
+        parts[two].take(N1)
+        if two >= half:
+            parts[two].give(4)
+        parts[two].give(6)
+
+    def exchange(r):
+        return rcopy(total, inbox.at[r], rsend.at[r], rrecv.at[r], **peers[r])
+
+    def round_end(r):
+        exchange(r).wait()
+        total[...] = total[...] + inbox[r]
+
+    total[...] = small[...]
+    for i in range(4):
+        rcopy(d_w.at[at(N2 * i + N1)], landed.at[i], csem.at[N0], csem.at[N1], dp=at(N1)).start()
+    for copy in own_copies[:3]:
+        copy.start()
+    next_part(N0)
+    exchange(N0).start()
+    spread[N0].start()
+    spread[N1].start()
+    next_part(N1)
+    rcopy(landed, landed, csem.at[N0], csem.at[N1], dp=p).wait()
+    for i in range(4):
+        work[i] = d_w[at(N2 * i)] + landed[i]
+    round_end(N0)
+    for side, first in ((N0, N2), (N1, 4)):
+        rcopy(work.at[N1 + side, side], cross.at[side, N0], xsend.at[side], xrecv.at[side], dp=at(first)).start()
+        rcopy(work.at[3, side], cross.at[side, N1], xsend.at[side], xrecv.at[side], dp=at(first)).start()
+    exchange(N1).start()
+    next_part(N2)
+    relay_part(N0)
+    round_end(N1)
+    for side, first in ((N0, N2), (N1, 4)):
+        rcopy(cross.at[side], cross.at[side], xsend.at[side], xrecv.at[side], dp=p).wait()
+        cross[side, N0] = cross[side, N0] + work[N0, side]
+        cross[side, N1] = cross[side, N1] + work[N2 - side, side]
+    exchange(N2).start()
+    for side, second in ((N0, 4), (N1, N2)):
+        rcopy(cross.at[side, N1], last.at[side], ysend.at[side], yrecv.at[side], dp=at(second)).start()
+    next_part(3)
+    spread[N0].cross()
+    spread[N1].cross()
+    relay_part(N1)
+    round_end(N2)
+    for side in range(N2):
+        rcopy(last.at[side], last.at[side], ysend.at[side], yrecv.at[side], dp=p).wait()
+        mine[side] = cross[side, N0] + last[side]
+    exchange(3).start()
+    next_part(4)
+    spread[N2].start()
+    own_copies[3].start()
+    spread[N0].diagonal()
+    spread[N1].diagonal()
+    relay_part(N2)
+    round_end(3)
+    next_part(5)
+    exchange(4).start()
+    relay_part(3)
+    spread[N2].cross()
+    next_part(6)
+    round_end(4)
+    relay_part(4)
+    next_part(7)
+    spread[N2].diagonal()
+    for i in range(5, len(cuts)):
+        relay_part(i)
+    for i in range(half):
+        for via, where in ((3, i), (4, i + half)):
+            parts[where].take(via)
+            parts[where].give(7)
+    for i in order:
+        for j in (N2, 5, 6, 7):
+            parts[i].take(j)
+        for j in (N0, N1, N2, 3 if i < half else 4, 5, 6, 7):
+            parts[i].copy(j, *EDGES[j]).wait_send()
+    for gather in spread:
+        gather.finish()
+    for copy in own_copies:
+        copy.wait()
+
+
+def finish(col, down, proj, d_w, small, n_tp, n_dp):
+    size, block = col.shape
+    tiles = size // 8
+    cuts = [(8 * (tiles * i // 8), 8 * (tiles * (i + N1) // 8)) for i in range(8)]
     dma = pltpu.SemaphoreType.DMA
-    return pl.pallas_call(
-        functools.partial(gather_kernel, parts),
-        name='gathered_columns',
-        out_shape=jax.ShapeDtypeStruct((size, n_dp * block), F32),
-        in_specs=[ANY],
-        out_specs=ANY,
-        scratch_shapes=[dma((len(SPREAD), parts)), dma((len(SPREAD), parts)), dma],
-        compiler_params=pltpu.CompilerParams(collective_id=2, has_side_effects=True),
-        cost_estimate=pl.CostEstimate(flops=10 * 10 ** 9, bytes_accessed=60 * 2 ** 20, transcendentals=0),
-    )(block_in)
+    shape = jax.ShapeDtypeStruct
+    third = d_w.shape[N1:]
+    kinds = len(EDGES)
+    table, down_all, proj_all, qkv_all, total = pl.pallas_call(
+        functools.partial(finish_kernel, n_tp, cuts),
+        name='finish',
+        out_shape=[shape((size, n_dp * block), F32)] + [shape((n_dp,) + src, F32) for src in (down.shape, proj.shape, third)] + [shape(small.shape, F32)],
+        in_specs=[ANY] * 3 + [VMEM] * N2,
+        out_specs=[ANY] * 4 + [VMEM],
+        scratch_shapes=[pltpu.VMEM(lead + third[N1:], F32) for lead in ((4, N2), (4, N2), (N2, N2), (N2,), (N2,))] + [pltpu.VMEM((5,) + small.shape, F32), dma,
+                        dma((8, kinds)), dma((8, kinds)), dma((3, kinds)), dma((3, kinds)), dma((4,))] + [dma((N2,))] * 5 + [dma((5,))] * N2,
+        compiler_params=pltpu.CompilerParams(collective_id=N2, has_side_effects=True, vmem_limit_bytes=32 * N2 ** 20),
+        cost_estimate=pl.CostEstimate(flops=10 * 10 ** 9, bytes_accessed=60 * N2 ** 20, transcendentals=N0),
+    )(col, down, proj, d_w, small)
+    return table, down_all.reshape(-N1, down.shape[N2]), proj_all.reshape(-N1, proj.shape[N2]), qkv_all.reshape(-N1, third[N2]), total
 
 
 def dot(a, b, dims):
@@ -940,25 +1057,25 @@
         d_b_out = jnp.sum(d_resid_one, axis=N0)
         d_attn_bf = d_resid_one.astype(BF)
         d_w_out = jnp.einsum('hse,sd->hed', ctx_own, d_attn_bf, preferred_element_type=F32)
-        d_w_out = lax.all_gather(lax.psum_scatter(d_w_out.reshape(-N1, width), ALL, scatter_dimension=N0, tiled=True), 'dp', axis=N0, tiled=True)
+        d_w_out = lax.psum_scatter(d_w_out.reshape(-N1, width), ALL, scatter_dimension=N0, tiled=True)
         d_ctx = jnp.einsum('sd,hed->hse', d_attn_bf, wo_full, preferred_element_type=F32)
-        d_w_qkv, d_b_qkv, d_cols, mine = backward(
+        d_w_qkv, d_b_qkv, d_cols, (d_w_gate, d_w_lin), d_w_down = backward(
             d_ctx.reshape(n_tp, blocks, own // blocks, dims), (ALPHA * d_resid_one).reshape(blocks, own // blocks, width), saved, cos_tab, sin_tab, wq, swap.T, emb_bf,
             (prod_gate, prod_lin, prod_down), heads, n_tp, n_dp)
-        d_b_qkv = jnp.dot(d_b_qkv, swap.astype(F32).T, precision=lax.Precision.HIGHEST)[N0]
-        d_w_qkv = lax.psum(d_w_qkv, 'dp')
-        d_w_gate, d_w_lin, d_w_down = [lax.all_gather(grad, 'dp', axis=N0, tiled=True) for grad in mine]
+        d_w_gate, d_w_lin = d_w_gate.reshape(-N1, ffn), d_w_lin.reshape(-N1, ffn)
+        d_b_qkv = jnp.dot(d_b_qkv, swap.astype(F32).T, precision=lax.Precision.HIGHEST)
         all_ids = tok_all.reshape(-N1) - tp * vocab_loc
         all_ids = jnp.where((all_ids >= N0) & (all_ids < vocab_loc), all_ids, vocab_loc)
-        d_table = gathered_columns(table_rows(all_ids, d_cols.reshape(n_dp * seq_len, -N1), vocab_loc), n_dp)
+        col = table_rows(all_ids, d_cols.reshape(n_dp * seq_len, -N1), vocab_loc)
 
         slot = (jnp.arange(n_tp) == tp).astype(F32)[:, None]
-        d_bq_rows = jnp.pad(slot * d_b_qkv[None], ((N0, N0), (N0, ffn - d_b_qkv.shape[N0])))
-        small = jnp.concatenate([d_b_gate, d_b_lin, d_bq_rows, jnp.stack([d_b_out, d_ln1_gain, d_ln1_bias, d_b_down, d_ln2_gain])], axis=N0)
-        small = lax.psum(small, ALL)
+        d_bq_rows = jnp.pad(slot * d_b_qkv, ((N0, N0), (N0, ffn - 3 * dims)))
+        small = jnp.concatenate([d_b_gate, d_b_lin, d_bq_rows, jnp.stack([d_b_out, d_ln1_gain, d_ln1_bias, d_b_down, d_ln2_gain]), jnp.zeros((7, width), F32)], axis=N0)
+        d_table, d_w_down, d_w_out, d_w_qkv, small = finish(
+            col, d_w_down, d_w_out.reshape(N2, -N1, width), d_w_qkv.reshape(n_dp, N2, -N1, 3 * dims), small, n_tp, n_dp)
         d_b_gate = lax.dynamic_index_in_dim(small[:n_tp], tp, N0, keepdims=False)
         d_b_lin = lax.dynamic_index_in_dim(small[n_tp:N2 * n_tp], tp, N0, keepdims=False)
-        d_b_qkv = lax.dynamic_index_in_dim(small[N2 * n_tp:3 * n_tp], tp, N0, keepdims=False)[:d_b_qkv.shape[N0]].reshape(heads, 3 * head_dim)
+        d_b_qkv = lax.dynamic_index_in_dim(small[N2 * n_tp:3 * n_tp], tp, N0, keepdims=False)[:3 * dims].reshape(heads, 3 * head_dim)
         d_b_out, d_ln1_gain, d_ln1_bias, d_b_down, d_ln2_gain = [small[3 * n_tp + i] for i in range(5)]
         return (d_table, d_w_qkv, d_b_qkv, d_w_out, d_b_out, d_ln1_gain, d_ln1_bias, d_w_gate, d_b_gate, d_w_lin, d_b_lin, d_w_down, d_b_down, d_ln2_gain)
 

time: 1390 us -> 1280 us (0.921)
  waiting for transfers between devices: 178 us -> 0.02 us
  Pallas kernels: 951 us -> 1020 us
    all_gather x4 -> x0, waiting for transfers between devices: 141 us -> none  [the longest x3 116 us: device_step(): lax.all_gather(grad, 'dp', axis=N0, tiled=True)]
    pallas_call x1, Pallas kernels: 147 us -> 199 us  [finish(): pl.pallas_call(functools.partial(finish_kernel, n_tp, cuts), name='finish...]
    psum x2 -> x0, waiting for transfers between devices: 34.6 us -> none  [the longest x1 34.6 us: device_step(): d_w_qkv = lax.psum(d_w_qkv, 'dp')]
    pallas_call x1, Pallas kernels: 393 us -> 407 us  [backward(): pl.pallas_call(functools.partial(backward_kernel, n_tp, rows, chunks, job...]
    unnamed x72 -> x78, local copies, waits for them, and re-layouts: 40.9 us -> 49.5 us
  transfers between devices with their start and end apart: 7 -> 1, of which waited for: 5 -> 0; matrix products, arithmetic and copies ran while one was open for 4% -> 4% of each run, Pallas kernels for 42% -> 35%
where the time goes in v4:
time: 1280 us; the launch traced here: 1270 us
  Pallas kernels  1020 us (80%)
  matrix products  132 us (10%)
  local copies, waits for them, and re-layouts  82.1 us (6%)
  other arithmetic  27.2 us (2%)
  between operations  14.9 us (1%)
    pallas_call x1, Pallas kernels, backward(): pl.pallas_call(functools.partial(backward_kernel, n_tp, rows, chunks, job...  407 us
    pallas_call x1, Pallas kernels, embed(): pl.pallas_call(functools.partial(emb_kernel, n_tp, rows, chunks, cuts, he...  377 us
    pallas_call x1, Pallas kernels, finish(): pl.pallas_call(functools.partial(finish_kernel, n_tp, cuts), name='finish...  199 us
    unnamed x78, local copies, waits for them, and re-layouts  49.5 us
    pallas_call x1, Pallas kernels, table_rows(): pl.pallas_call(table_kernel, name='table_rows', grid_spec=pltpu.PrefetchS...  33.2 us
    dot_general x3, matrix products, product(): jnp.einsum(spec, lhs, rhs, preferred_element_type=F32)  28.8 us
    dot_general x1, matrix products, device_step(): jnp.einsum('sk,tkc->tsc', hidden, wl_full, preferred_element_type=F32)  26.9 us
  transfers between devices with their start and end apart: 1, of which 0 were waited for; matrix products, arithmetic and copies ran while one was open for 4% of the time, Pallas kernels for 35%

profile of v4, /device:TPU:0, one launch (start us, length us, event | category | flops | bytes accessed | tf_op | source)
XLA Modules:
  0.0 1272.4 jit_solution(3736019832055904586)
XLA Ops:
  19.9 4.0 fusion.37.wq
  23.9 18.4 %gather_fusion = bf16[2048,1024]{1,0:T(8,128)(2,1)} fusion(bf16[7648,1024]{1,0:T(8,128)(2,1)} %param.21, s32[2048]{0:T(1024)S(1)} %broadcast_clamp_fusion), kind=kCustom, calls=%fused_computation | custom fusion | bytes 8396800 | tf_op jit(solution)/shard_map/jit(_take)/gather | solution.py:1012
  42.3 3.9 broadcast_select_fusion.found
  46.1 377.1 %embed.1 = (bf16[2048,1024]{1,0:T(8,128)(2,1)}, bf16[4,8,128,1024]{3,2,1,0:T(8,128)(2,1)}, bf16[4,8,128,1024]{3,2,1,0:T(8,128)(2,1)}, bf16[4,8,128,1024]{3,2,1,0...) custom-call(bf16[2048,1024]{1,0:T(8,128)(2,1)} %broadcast_select_fus, ...), custom_call_target="tpu_custom_call" | custom-call | flops 20000000000 | bytes 83886080 | tf_op jit(solution)/shard_map/embed/pallas_call | solution.py:357
  430.5 3.1 fusion.70
  434.5 6.8 fusion.48
  441.4 26.9 %fusion.1 = (bf16[4,512,1024]{2,1,0:T(8,128)(2,1)S(1)}, f32[4,512,1024]{2,1,0:T(8,128)}, f32[4,512,1024]{2,1,0:T(8,128)}, f32[4,1024,512]{1,2,0:T(8,128)}) fusion(f32[4,1024]{1,0:T(4,128)S(1)} %bitcast.248, f32[4,1024,512]{1,2,0:T(8,128)} %fusion.48, f32[4,1024]{1,0:T(4,128)S(1)} %bitcast.246, bf16[4,1024,1024]{2,1,0:T(8,128)(2,1)S(1)} %bitcast.263, ...), kind=kOutput, calls=%fused_computation.6 | convolution fusion | flops 4437573632 | bytes 47218688 | tf_op jit(solution)/shard_map/sk,tkc->tsc/dot_general | solution.py:1033
  468.3 4.7 fusion.71
  474.4 2.1 fusion.66
  476.4 22.1 %fusion.63 = (f32[4,1024]{1,0:T(4,128)S(1)}, bf16[4,512,1024]{2,1,0:T(8,128)(2,1)}, f32[4,1024]{1,0:T(4,128)}, bf16[4,1024,512]{1,2,0:T(8,128)(2,1)}) fusion(f32[4,512,1024]{2,1,0:T(8,128)} %get-tuple-element.77, f32[4,1024,512]{1,2,0:T(8,128)} %get-tuple-element.93, f32[4,1024]{1,0:T(4,128)S(1)} %bitcast.249, f32[4,1024,512]{1,2,0:T(8,128)} %fusion.48, ...), kind=kOutput, calls=%fused_computation.125 | convolution fusion | flops 4342145024 | bytes 52496384 | tf_op jit(solution)/shard_map/sd,tcd->tsc/dot_general | solution.py:1046
  498.6 10.5 fusion.34
  509.1 14.6 %multiply_reduce_fusion = (f32[1024]{0:T(1024)S(1)}, f32[512]{0:T(512)S(1)}, f32[1024]{0:T(1024)S(1)}, f32[512,1024]{1,0:T(8,128)}) fusion(f32[512,1024]{1,0:T(8,128)S(1)} %get-tuple-element.92, f32[512]{0:T(512)S(1)} %fusion.57, f32[512]{0:T(512)S(1)} %broadcast_multiply_fusion.2, f32[1024]{0:T(1024)S(1)} %convert_element_type.106, ...), kind=kOutput, calls=%fused_computation.57 | convolution fusion | flops 4307547648 | bytes 29380608 | tf_op jit(solution)/shard_map/tsc,tkc->sk/dot_general | solution.py:1054
  523.7 2.3 fusion.65
  527.4 3.3 fusion.60
  532.3 4.3 convolution_bitcast_fusion
  536.6 2.9 copy.44
  542.4 11.1 fusion.32
  553.5 8.5 fusion.53
  562.0 9.2 fusion.45
  571.2 406.7 %backward.1 = (f32[8,2,64,1024]{3,2,1,0:T(8,128)}, f32[8,2,64,1024]{3,2,1,0:T(8,128)}, f32[8,2048,128]{2,1,0:T(8,128)}, f32[2,64,1024]{2,1,0:T(8,128)}, f32[1024...) custom-call(f32[4,8,64,256]{3,2,1,0:T(8,128)} %bitcast.233, ...), custom_call_target="tpu_custom_call" | custom-call | flops 20000000000 | bytes 104857600 | tf_op jit(solution)/shard_map/backward/pallas_call | solution.py:695
  978.0 1.8 fusion.41
  980.6 1.8 add_reduce_fusion.1
  984.0 33.2 %table_rows.1.col = f32[7648,128]{1,0:T(8,128)S(1)} custom-call(s32[16384]{0:T(1024)S(1)} %and_select_fusion.ids, f32[16384,128]{1,0:T(8,128)} %bitcast.227), custom_call_target="tpu_custom_call" | custom-call | flops 3000000000 | bytes 16777216 | tf_op jit(solution)/shard_map/table_rows/pallas_call | solution.py:740
  1017.3 1.9 copy-done.2
  1019.2 2.1 copy-done.3
  1022.2 1.9 copy-done.7
  1025.2 198.9 %finish.1 = (f32[7648,1024]{1,0:T(8,128)}, f32[8,2,64,1024]{3,2,1,0:T(8,128)S(1)}, f32[8,2,16,1024]{3,2,1,0:T(8,128)S(1)}, f32[8,2,64,768]{3,2,1,0:T(8,128)S(1)}, f32[24,1024]{1,0:T(8,128)S(1)}) custom-call(f32[7648,128]{1,0:T(8,128)S(1)} %copy-done.3, f32[2,64,1024]{2,1,0:T(8,128)S(1)} %copy-done.8, f32[2,16,1024]{2,1,0:T(8,128)S(1)} %bitcast.220, ...), custom_call_target="tpu_custom_call" | custom-call | flops 10000000000 | bytes 62914560 | tf_op jit(solution)/shard_map/finish/pallas_call | solution.py:876
  1224.0 2.0 copy-done
  1229.5 22.1 %copy.68 = f32[7648,1024]{1,0:T(8,128)} copy(f32[7648,1024]{1,0:T(8,128)} %get-tuple-element.120) | data formatting | bytes 62652416
  1255.7 2.1 copy.71
  1259.4 2.1 copy.72
  1263.1 2.0 copy.73
  (133 shorter events, 42.8 us)
Async XLA Ops:
  7.2 6.7 copy-start.26
  7.2 6.7 copy-start.21
  7.2 6.7 copy-start.22
  7.2 6.7 copy-start.23
  7.2 6.7 copy-start.24
  7.2 6.8 copy-start.25
  7.2 1012.0 %reduce-scatter.2.cloned.1.call-start = ((), (), s32[]{:S(2)}) async-start(), calls=%async_computation.1 | async-start | bytes 4325376 | tf_op jit(solution)/shard_map/reduce_scatter | solution.py:1060
  12.7 6.1 copy-start.19
  430.4 3.9 slice-start.4
  430.4 4.1 slice-start.5
  433.9 7.4 slice-start.2
  434.5 6.8 slice-start.3
  434.5 33.7 %slice-start.6 = ((s8[8388608]{0:T(1024)(128)(4,1)}), s8[4194304]{0:T(1024)(128)(4,1)S(1)}, s32[]{:S(2)}) async-start(s8[8388608]{0:T(1024)(128)(4,1)} %bitcast.269), calls=%async_computation.8 | async-start | bytes 8388608
  441.4 26.9 %slice-start.7 = ((s8[8388608]{0:T(1024)(128)(4,1)}), s8[4194304]{0:T(1024)(128)(4,1)S(1)}, s32[]{:S(2)}) async-start(s8[8388608]{0:T(1024)(128)(4,1)} %bitcast.269), calls=%async_computation.9 | async-start | bytes 8388608
  468.3 4.8 copy-start.13
  523.7 3.7 copy-start.16
  530.7 1.6 copy-start.10
  532.3 7.2 copy-start.20
  539.5 2.9 copy-start.12
  542.4 11.1 copy-start.11
  542.4 11.1 copy-start.14
  542.4 19.6 %slice-start = ((s8[8388608]{0:T(1024)(128)(4,1)}), s8[4194304]{0:T(1024)(128)(4,1)S(1)}, s32[]{:S(2)}) async-start(s8[8388608]{0:T(1024)(128)(4,1)} %bitcast.222), calls=%async_computation.2 | async-start | bytes 8388608
  553.5 8.5 slice-start.1
  553.5 8.5 copy-start.15
  1017.3 1.9 copy-start.2
  1019.2 2.1 copy-start.3
  1022.2 1.9 copy-start.7
  1224.0 2.0 copy-start
  1251.6 2.0 copy-start.5
  1251.6 4.0 copy-start.18
  1255.7 3.7 copy-start.17
  1259.4 3.7 copy-start.1
  (4 other events, 4.2 us)
Sparse Core Ops, SparseCore 0:
  530.9 150.2 reduce-scatter.1

commit v5 on v4

--- a/solution.py
+++ b/solution.py
@@ -22,17 +22,6 @@
 VMEM = pl.BlockSpec(memory_space=pltpu.VMEM)
 
 
-def norm_scaled(values, gain):
-    mean_val = jnp.mean(values, axis=-1, keepdims=True)
-    centered = values - mean_val
-    variance = jnp.mean(centered * centered, axis=-1, keepdims=True)
-    return centered * lax.rsqrt(variance + EPS) * gain
-
-
-def geglu(gate_pre, lin_pre):
-    return jax.nn.gelu(gate_pre, approximate=False) * lin_pre
-
-
 def rope_tables(seq_len, head_dim, heads):
     half_dim = head_dim // 2
     inv_freq = (ROPE_BASE ** (-2.0 * np.arange(half_dim) / head_dim)).astype(np.float32)
@@ -230,8 +219,8 @@
                     give(t, j)
         others(d, body)
 
-    k_all[...] = jnp.zeros_like(k_all)
-    v[...] = jnp.zeros_like(v)
+    k_all[:] = jnp.zeros_like(k_all)
+    v[:] = jnp.zeros_like(v)
     arrive(N1)
 
     @pl.loop(N0, blocks)
@@ -467,10 +456,10 @@
         pairs = ((ctx.at[at_q], ctx_in), (resid.at[i], res_in), (cos.at[at_q], cos_in), (sin.at[at_q], sin_in), (emb.at[at_q], emb_in))
         return [pltpu.make_async_copy(src, dst.at[slot], isem.at[j, slot]) for j, (src, dst) in enumerate(pairs)]
 
-    dk[...] = jnp.zeros_like(dk)
-    dv[...] = jnp.zeros_like(dv)
-    d_w[...] = jnp.zeros_like(d_w)
-    d_bias[...] = jnp.zeros_like(d_bias)
+    dk[:] = jnp.zeros_like(dk)
+    dv[:] = jnp.zeros_like(dv)
+    d_w[:] = jnp.zeros_like(d_w)
+    d_bias[:] = jnp.zeros_like(d_bias)
     for copy in inputs(blocks - N1):
         copy.start()
 
@@ -495,8 +484,8 @@
         def _():
             slot = i % N2
             got = grad_rows(i, qb, cos_in[slot], sin_in[slot], dq, dk, dv, d_bias)
-            d_w[...] += dot(emb_in[slot], dot(got, back[...], NN).astype(BF), TN)
-            part[rows_of(i, N0, qb), :] = dot(got, wq[...], NT)
+            d_w[:] += dot(emb_in[slot], dot(got, back[:], NN).astype(BF), TN)
+            part[rows_of(i, N0, qb), :] = dot(got, wq[:], NT)
             part[rows_of(i, z, share), :] = part[rows_of(i, z, share), :] + res_in[i % N2]
 
     def sides(u):
@@ -574,7 +563,7 @@
 
         def add_from(ref, sem):
             rcopy(ref, ref, csend, sem, tp=z).wait_recv()
-            keep[slot] = keep[slot] + ref[...]
+            keep[slot] = keep[slot] + ref[:]
         if send:
             @pl.when(ok & (z < t))
             def _():
@@ -717,7 +706,7 @@
     @pl.when(step == 0)
     def _():
         for table in tables:
-            table[...] = jnp.zeros_like(table)
+            table[:] = jnp.zeros_like(table)
 
     @pl.loop(0, part, unroll=4)
     def _(r):
@@ -728,10 +717,10 @@
 
     @pl.when(step == pl.num_programs(0) - 1)
     def _():
-        total = tables[0][...]
+        total = tables[0][:]
         for table in tables[1:]:
-            total = total + table[...]
-        out[...] = SHRINK * total[:out.shape[0]]
+            total = total + table[:]
+        out[:] = SHRINK * total[:out.shape[0]]
 
 
 def table_rows(ids, rows, vocab_loc):
@@ -793,9 +782,9 @@
 
     def round_end(r):
         exchange(r).wait()
-        total[...] = total[...] + inbox[r]
-
-    total[...] = small[...]
+        total[:] = total[:] + inbox[r]
+
+    total[:] = small[:]
     for i in range(4):
         rcopy(d_w.at[at(N2 * i + N1)], landed.at[i], csem.at[N0], csem.at[N1], dp=at(N1)).start()
     for copy in own_copies[:3]:
@@ -909,7 +898,7 @@
 def project(i, qb, emb, wq, bq, cos, sin, q, k, v):
     at_q = pl.ds(pl.multiple_of(i * qb, qb), qb)
     dims = q.shape[1]
-    qkv = (dot(emb[at_q, :], wq[...], NN) + bq[...]).astype(BF)
+    qkv = (dot(emb[at_q, :], wq[:], NN) + bq[:]).astype(BF)
     for ref, part in ((q, 0), (k, 1)):
         ref[at_q, :] = turned(qkv[:, part * dims:(part + 1) * dims].astype(F32), cos[at_q, :], sin[at_q, :]).astype(BF)
     v[at_q, :] = qkv[:, 2 * dims:]
@@ -961,7 +950,7 @@
     q = jnp.where(lane_head((qb, dims), heads, 2) == h, q_ref[at_q, :].astype(F32), 0.0).astype(BF)
     dc = jnp.where(lane_head((qb, dims), heads, 1) == h, dctx_ref[at_q, :], 0.0).astype(BF)
     ones = jnp.ones((8, dims), F32)
-    mean = lax.dot_general(ones, dc.astype(F32) * ctx_ref[...], (NT, ((), ())), precision=lax.Precision.HIGHEST, preferred_element_type=F32)[:1]
+    mean = lax.dot_general(ones, dc.astype(F32) * ctx_ref[:], (NT, ((), ())), precision=lax.Precision.HIGHEST, preferred_element_type=F32)[:1]
     top, inv = top_ref[pl.ds(h, 1), at_q], inv_ref[pl.ds(h, 1), at_q]
 
     def step(j, dq):
@@ -973,15 +962,124 @@
         dk_ref[at_k, :] += dot(ds, q, NN)
         return dq + dot(ds, keys, TN)
     dq = lax.fori_loop(0, (i + 2) // 2, step, jnp.zeros((qb, dims), F32))
-    dq_ref[...] = jnp.where(lane_head((qb, dims), heads, 2) == h, dq, dq_ref[...])
+    dq_ref[:] = jnp.where(lane_head((qb, dims), heads, 2) == h, dq, dq_ref[:])
 
 
 def grad_rows(i, qb, cos, sin, dq, dk, dv, d_bias):
     at_q = pl.ds(pl.multiple_of(i * qb, qb), qb)
-    back = [turned(values, cos, -sin) for values in (dq[...], dk[at_q, :])]
+    back = [turned(values, cos, -sin) for values in (dq[:], dk[at_q, :])]
     rows = jnp.concatenate(back + [dv[at_q, :]], axis=1)
-    d_bias[...] += jnp.sum(rows, axis=0, keepdims=True)
+    d_bias[:] += jnp.sum(rows, axis=0, keepdims=True)
     return rows.astype(BF)
+
+
+def standard(values):
+    mean = jnp.mean(values, axis=1, keepdims=True)
+    centered = values - mean
+    scale = lax.rsqrt(jnp.mean(centered * centered, axis=1, keepdims=True) + EPS)
+    return centered * scale, scale
+
+
+def standard_grad(d_out, unit, scale):
+    return scale * (d_out - jnp.mean(d_out, axis=1, keepdims=True) - unit * jnp.mean(d_out * unit, axis=1, keepdims=True))
+
+
+def over_rows(values):
+    return jnp.sum(values, axis=0, keepdims=True)
+
+
+def layer_kernel(n, ctx, wo, emb, cot, vectors, gate_bias, lin_bias, wg, wl, wd, hidden, d_ffn, d_attn, resid, d_ctx, sums, inner, d_gate, d_lin, gate, lin, acc, unit1, scale1):
+    i = pl.program_id(N0)
+    t = i % n
+    tile = 256 if acc.shape[N1] % 256 == N0 else acc.shape[N1]
+    tiles = range(N0, acc.shape[N1], tile)
+    b_out, gain1, bias1, b_down, gain2 = [vectors[pl.ds(j, N1), :] for j in range(5)]
+
+    @pl.when(i == N0)
+    def _():
+        total = ALPHA * emb[:].astype(F32) + b_out
+        for h in range(n):
+            total = total + dot(ctx[h].astype(BF), wo[h], NN)
+        unit, scale1[:] = standard(total)
+        unit1[:] = unit
+        hidden[:] = (unit * gain1 + bias1).astype(BF)
+        acc[:] = jnp.zeros_like(acc)
+
+    @pl.when(i < n)
+    def _():
+        for lo in tiles:
+            cols = pl.ds(lo, tile)
+            g = dot(hidden[:], wg[N0, :, cols], NN) + gate_bias[pl.ds(t, N1), cols]
+            l = dot(hidden[:], wl[N0, :, cols], NN) + lin_bias[pl.ds(t, N1), cols]
+            gate[t, :, cols] = g
+            lin[t, :, cols] = l
+            inner[N0, :, cols] = (0.5 * g * (1.0 + lax.erf(g * 0.5 ** 0.5)) * l).astype(BF)
+        for lo in tiles:
+            cols = pl.ds(lo, tile)
+            acc[:, cols] += dot(inner[N0], wd[N0, :, cols], NN)
+
+    @pl.when(i == n - N1)
+    def _():
+        unit, scale = standard(ALPHA * hidden[:].astype(F32) + acc[:] + b_down)
+        g = cot[:].astype(F32)
+        d_y = standard_grad(g * gain2, unit, scale)
+        sums[pl.ds(N2 * n + 3, N1), :] = over_rows(d_y)
+        sums[pl.ds(N2 * n + 4, N1), :] = over_rows(g * unit)
+        d_ffn[:] = d_y.astype(BF)
+        acc[:] = ALPHA * d_y
+
+    @pl.when(i >= n)
+    def _():
+        for lo in tiles:
+            cols = pl.ds(lo, tile)
+            d_inner = dot(d_ffn[:], wd[N0, cols, :], NT).astype(BF).astype(F32)
+            g, l = gate[t, :, cols], lin[t, :, cols]
+            cdf = 0.5 * (1.0 + lax.erf(g * 0.5 ** 0.5))
+            slope = cdf + g * (jnp.exp(-0.5 * g * g) * (N2 * np.pi) ** -0.5)
+            d_l = d_inner * (g * cdf)
+            d_g = d_inner * l * slope
+            sums[pl.ds(t, N1), cols] = over_rows(d_g)
+            sums[pl.ds(n + t, N1), cols] = over_rows(d_l)
+            d_gate[N0, :, cols] = d_g.astype(BF)
+            d_lin[N0, :, cols] = d_l.astype(BF)
+        for lo in tiles:
+            cols = pl.ds(lo, tile)
+            acc[:, cols] += dot(d_gate[N0], wg[N0, cols, :], NT) + dot(d_lin[N0], wl[N0, cols, :], NT)
+
+    @pl.when(i == N2 * n - N1)
+    def _():
+        d_h, unit = acc[:], unit1[:]
+        d_x = standard_grad(d_h * gain1, unit, scale1[:])
+        sums[pl.ds(N2 * n, N1), :] = over_rows(d_x)
+        sums[pl.ds(N2 * n + N1, N1), :] = over_rows(d_h * unit)
+        sums[pl.ds(N2 * n + N2, N1), :] = over_rows(d_h)
+        resid[:] = ALPHA * d_x
+        d_attn[:] = d_x.astype(BF)
+        for h in range(n):
+            d_ctx[h] = dot(d_attn[:], wo[h], NT)
+
+
+def layer(ctx, wo, emb, cot, vectors, gate_bias, lin_bias, wg, wl, wd):
+    n, own, dims = ctx.shape
+    width = emb.shape[N1]
+    ffn = wg.shape[N2]
+    once = pl.BlockSpec(memory_space=pltpu.VMEM)
+    weight = [pl.BlockSpec((N1,) + w.shape[N1:], lambda i: (i % n, N0, N0)) for w in (wg, wl, wd)]
+    early = pl.BlockSpec((N1, own, ffn), lambda i: (jnp.minimum(i, n - N1), N0, N0))
+    late = pl.BlockSpec((N1, own, ffn), lambda i: (jnp.maximum(i - n, N0), N0, N0))
+    shape = jax.ShapeDtypeStruct
+    slots = shape((n, own, ffn), BF)
+    return pl.pallas_call(
+        functools.partial(layer_kernel, n),
+        name='layer',
+        grid=(N2 * n,),
+        in_specs=[once] * 7 + weight,
+        out_specs=[once] * 6 + [early, late, late],
+        out_shape=[shape((own, width), BF)] * 3 + [shape((own, width), F32), shape((n, own, dims), F32), shape((N2 * n + 8, width), F32), slots, slots, slots],
+        scratch_shapes=[pltpu.VMEM((n, own, ffn), F32)] * N2 + [pltpu.VMEM((own, width), F32)] * N2 + [pltpu.VMEM((own, N1), F32)],
+        compiler_params=pltpu.CompilerParams(dimension_semantics=('arbitrary',), vmem_limit_bytes=62 * N2 ** 20),
+        cost_estimate=pl.CostEstimate(flops=15 * 10 ** 9, bytes_accessed=70 * N2 ** 20, transcendentals=N0),
+    )(ctx, wo, emb, cot, vectors, gate_bias, lin_bias, wg, wl, wd)
 
 
 def solution(mesh):
@@ -1017,50 +1115,28 @@
         bq = jnp.dot(b_qkv.reshape(N1, -N1), swap, preferred_element_type=F32)
         cos_tab, sin_tab = rope_tables(seq_len, head_dim, heads)
         emb_bf, (wg_full, wl_full, wd_full, wo_full), biases, tok_all, ctx_own, saved = embed(found, in_shard[:, None].astype(F32), piece, tokens.reshape(-N1, min(128, seq_len // 8)), (w_gate, w_lin, w_down, w_out), wq, bq, cos_tab, sin_tab, heads, n_tp, n_dp)
-        ctx_own = ctx_own.reshape(n_tp, own, dims).astype(BF)
         is_own = (jnp.arange(n_tp) == tp)[:, None]
         bg_full, bl_full = [jnp.where(is_own, b[None].astype(F32), biases[:, i]) for i, b in enumerate((b_gate, b_lin))]
 
         blocks = 8
 
         def owned(values):
-            return lax.dynamic_index_in_dim(values.reshape(blocks, n_tp, -N1, width), tp, N1, keepdims=False).reshape(own, width).astype(F32)
+            return lax.dynamic_index_in_dim(values.reshape(blocks, n_tp, -N1, width), tp, N1, keepdims=False).reshape(own, width)
         emb_own, cot_own = owned(emb_bf), owned(cotangent[N0])
-        attn_out = jnp.einsum('hse,hed->sd', ctx_own, wo_full, preferred_element_type=F32) + b_out.astype(F32)
-        normed_one, norm_one_pull = jax.vjp(norm_scaled, ALPHA * emb_own + attn_out, ln1_gain.astype(F32))
-        hidden = (normed_one + ln1_bias.astype(F32)).astype(BF)
-        gate_pre = jnp.einsum('sk,tkc->tsc', hidden, wg_full, preferred_element_type=F32) + bg_full[:, None]
-        lin_pre = jnp.einsum('sk,tkc->tsc', hidden, wl_full, preferred_element_type=F32) + bl_full[:, None]
-        inner_val, act_pull = jax.vjp(geglu, gate_pre, lin_pre)
-        inner_act = inner_val.astype(BF)
-        ffn_out = jnp.einsum('tsc,tcd->sd', inner_act, wd_full, preferred_element_type=F32) + b_down.astype(F32)
-        norm_two_pull = jax.vjp(norm_scaled, ALPHA * hidden.astype(F32) + ffn_out, ln2_gain.astype(F32))[N1]
+        vectors = jnp.stack([b_out, ln1_gain, ln1_bias, b_down, ln2_gain] + [b_out] * 3).astype(F32)
+        hidden, d_ffn_bf, d_attn_bf, resid, d_ctx, row_sums, inner_act, d_gate_bf, d_lin_bf = layer(
+            ctx_own.reshape(n_tp, own, dims), wo_full, emb_own, cot_own, vectors, bg_full, bl_full, wg_full, wl_full, wd_full)
 
         def product(lhs, rhs, spec):
             return jnp.einsum(spec, lhs, rhs, preferred_element_type=F32).reshape(n_tp, n_dp, -N1, width)
 
-        d_resid_two, d_ln2_gain = norm_two_pull(cot_own)
-        d_b_down = jnp.sum(d_resid_two, axis=N0)
-        d_ffn_bf = d_resid_two.astype(BF)
         prod_down = product(inner_act, d_ffn_bf, 'tsc,sd->tcd')
-        d_inner = jnp.einsum('sd,tcd->tsc', d_ffn_bf, wd_full, preferred_element_type=F32).astype(BF)
-        d_gate_pre, d_lin_pre = act_pull(d_inner.astype(F32))
-        d_b_gate = jnp.sum(d_gate_pre, axis=N1)
-        d_b_lin = jnp.sum(d_lin_pre, axis=N1)
-        d_gate_bf = d_gate_pre.astype(BF)
-        d_lin_bf = d_lin_pre.astype(BF)
         prod_gate = product(hidden, d_gate_bf, 'sk,tsc->tkc')
         prod_lin = product(hidden, d_lin_bf, 'sk,tsc->tkc')
-        d_hidden = ALPHA * d_resid_two + jnp.einsum('tsc,tkc->sk', d_gate_bf, wg_full, preferred_element_type=F32) + jnp.einsum('tsc,tkc->sk', d_lin_bf, wl_full, preferred_element_type=F32)
-        d_ln1_bias = jnp.sum(d_hidden, axis=N0)
-        d_resid_one, d_ln1_gain = norm_one_pull(d_hidden)
-        d_b_out = jnp.sum(d_resid_one, axis=N0)
-        d_attn_bf = d_resid_one.astype(BF)
-        d_w_out = jnp.einsum('hse,sd->hed', ctx_own, d_attn_bf, preferred_element_type=F32)
+        d_w_out = jnp.einsum('hse,sd->hed', ctx_own.reshape(n_tp, own, dims).astype(BF), d_attn_bf, preferred_element_type=F32)
         d_w_out = lax.psum_scatter(d_w_out.reshape(-N1, width), ALL, scatter_dimension=N0, tiled=True)
-        d_ctx = jnp.einsum('sd,hed->hse', d_attn_bf, wo_full, preferred_element_type=F32)
         d_w_qkv, d_b_qkv, d_cols, (d_w_gate, d_w_lin), d_w_down = backward(
-            d_ctx.reshape(n_tp, blocks, own // blocks, dims), (ALPHA * d_resid_one).reshape(blocks, own // blocks, width), saved, cos_tab, sin_tab, wq, swap.T, emb_bf,
+            d_ctx.reshape(n_tp, blocks, own // blocks, dims), resid.reshape(blocks, own // blocks, width), saved, cos_tab, sin_tab, wq, swap.T, emb_bf,
             (prod_gate, prod_lin, prod_down), heads, n_tp, n_dp)
         d_w_gate, d_w_lin = d_w_gate.reshape(-N1, ffn), d_w_lin.reshape(-N1, ffn)
         d_b_qkv = jnp.dot(d_b_qkv, swap.astype(F32).T, precision=lax.Precision.HIGHEST)
@@ -1070,7 +1146,8 @@
 
         slot = (jnp.arange(n_tp) == tp).astype(F32)[:, None]
         d_bq_rows = jnp.pad(slot * d_b_qkv, ((N0, N0), (N0, ffn - 3 * dims)))
-        small = jnp.concatenate([d_b_gate, d_b_lin, d_bq_rows, jnp.stack([d_b_out, d_ln1_gain, d_ln1_bias, d_b_down, d_ln2_gain]), jnp.zeros((7, width), F32)], axis=N0)
+        kept = N2 * n_tp
+        small = jnp.concatenate([row_sums[:kept], d_bq_rows, row_sums[kept:kept + 5], jnp.zeros((7, width), F32)], axis=N0)
         d_table, d_w_down, d_w_out, d_w_qkv, small = finish(
             col, d_w_down, d_w_out.reshape(N2, -N1, width), d_w_qkv.reshape(n_dp, N2, -N1, 3 * dims), small, n_tp, n_dp)
         d_b_gate = lax.dynamic_index_in_dim(small[:n_tp], tp, N0, keepdims=False)

time: 1280 us -> 1230 us (0.961)
  matrix products: 132 us -> 41.7 us
  Pallas kernels: 1020 us -> 1070 us
  other arithmetic: 27.2 us -> 14 us
    dot_general x9 -> x1, matrix products: 96.4 us -> 4.47 us  [device_step(): jnp.einsum('hse,sd->hed', ctx_own.reshape(n_tp, own, dims).astype(BF), d_...]
    pallas_call x0 -> x1, Pallas kernels: none -> 48.5 us  [layer(): pl.pallas_call(functools.partial(layer_kernel, n), name='layer', grid=(N2...]
    unnamed x78 -> x56, local copies, waits for them, and re-layouts: 49.5 us -> 47.2 us
  transfers between devices with their start and end apart: 1 -> 1, of which waited for: 0 -> 0; matrix products, arithmetic and copies ran while one was open for 4% -> 3% of each run, Pallas kernels for 35% -> 37%
where the time goes in v5:
time: 1230 us; the launch traced here: 1220 us
  Pallas kernels  1070 us (87%)
  local copies, waits for them, and re-layouts  80.5 us (7%)
  matrix products  41.7 us (3%)
  between operations  14.8 us (1%)
  other arithmetic  14 us (1%)
    pallas_call x1, Pallas kernels, backward(): pl.pallas_call(functools.partial(backward_kernel, n_tp, rows, chunks, job...  415 us
    pallas_call x1, Pallas kernels, embed(): pl.pallas_call(functools.partial(emb_kernel, n_tp, rows, chunks, cuts, he...  377 us
    pallas_call x1, Pallas kernels, finish(): pl.pallas_call(functools.partial(finish_kernel, n_tp, cuts), name='finish...  194 us
    pallas_call x1, Pallas kernels, layer(): pl.pallas_call(functools.partial(layer_kernel, n), name='layer', grid=(N2...  48.5 us
    unnamed x56, local copies, waits for them, and re-layouts  47.2 us
    pallas_call x1, Pallas kernels, table_rows(): pl.pallas_call(table_kernel, name='table_rows', grid_spec=pltpu.PrefetchS...  33.4 us
    dot_general x3, matrix products, product(): jnp.einsum(spec, lhs, rhs, preferred_element_type=F32)  31.8 us
  transfers between devices with their start and end apart: 1, of which 0 were waited for; matrix products, arithmetic and copies ran while one was open for 3% of the time, Pallas kernels for 37%

profile of v5, /device:TPU:0, one launch (start us, length us, event | category | flops | bytes accessed | tf_op | source)
XLA Modules:
  0.0 1219.7 jit_solution(4528691547270916907)
XLA Ops:
  12.2 1.1 fusion.17.mask
  16.0 1.1 constant_dynamic-slice_fusion.5
  17.6 1.4 convert_element_type.42.piece
  20.1 2.6 fusion.5.wq
  22.7 18.4 %gather_fusion = bf16[2048,1024]{1,0:T(8,128)(2,1)} fusion(bf16[7648,1024]{1,0:T(8,128)(2,1)} %param.21, s32[2048]{0:T(1024)S(1)} %broadcast_clamp_fusion), kind=kCustom, calls=%fused_computation | custom fusion | bytes 8396800 | tf_op jit(solution)/shard_map/jit(_take)/gather | solution.py:1110
  41.1 3.9 broadcast_select_fusion.found
  44.9 377.2 %embed.1 = (bf16[2048,1024]{1,0:T(8,128)(2,1)}, bf16[4,8,128,1024]{3,2,1,0:T(8,128)(2,1)}, bf16[4,8,128,1024]{3,2,1,0:T(8,128)(2,1)}, bf16[4,8,128,1024]{3,2,1,0...) custom-call(bf16[2048,1024]{1,0:T(8,128)(2,1)} %broadcast_select_fus, ...), custom_call_target="tpu_custom_call" | custom-call | flops 20000000000 | bytes 83886080 | tf_op jit(solution)/shard_map/embed/pallas_call | solution.py:346
  422.2 1.3 copy.47
  423.5 2.3 constant_dynamic-slice_fusion.2
  425.7 2.3 constant_dynamic-slice_fusion.3
  429.3 48.5 %layer.1 = (bf16[512,1024]{1,0:T(8,128)(2,1)}, bf16[512,1024]{1,0:T(8,128)(2,1)}, bf16[512,1024]{1,0:T(8,128)(2,1)}, f32[512,1024]{1,0:T(8,128)}, f32[4,512,256]...) custom-call(f32[4,512,256]{2,1,0:T(8,128)} %bitcast.89, ...), custom_call_target="tpu_custom_call" | custom-call | flops 15000000512 | bytes 73400320 | tf_op jit(solution)/shard_map/layer/pallas_call | solution.py:1072
  477.8 4.5 fusion.27
  483.8 1.3 fusion.3.back
  485.1 13.0 %fusion.15 = f32[4,1024,1024]{1,2,0:T(8,128)} fusion(bf16[4,512,1024]{2,1,0:T(8,128)(2,1)} %get-tuple-element.64, bf16[512,1024]{1,0:T(8,128)(2,1)S(1)} %copy-done.10), kind=kOutput, calls=%fused_computation.20 | convolution fusion | flops 4294967296 | bytes 22020096 | tf_op jit(solution)/shard_map/sk,tsc->tkc/dot_general | solution.py:1131
  498.1 10.6 fusion.13
  508.7 8.2 fusion.11
  516.8 415.2 %backward.1 = (f32[8,2,64,1024]{3,2,1,0:T(8,128)}, f32[8,2,64,1024]{3,2,1,0:T(8,128)}, f32[8,2048,128]{2,1,0:T(8,128)}, f32[2,64,1024]{2,1,0:T(8,128)}, f32[1024...) custom-call(f32[4,8,64,256]{3,2,1,0:T(8,128)} %bitcast.114, ...), custom_call_target="tpu_custom_call" | custom-call | flops 20000000000 | bytes 104857600 | tf_op jit(solution)/shard_map/backward/pallas_call | solution.py:684
  932.1 1.8 fusion.9
  935.8 33.4 %table_rows.1.col = f32[7648,128]{1,0:T(8,128)S(1)} custom-call(s32[16384]{0:T(1024)S(1)} %and_select_fusion.ids, f32[16384,128]{1,0:T(8,128)} %bitcast.86), custom_call_target="tpu_custom_call" | custom-call | flops 3000000000 | bytes 16777216 | tf_op jit(solution)/shard_map/table_rows/pallas_call | solution.py:729
  969.2 1.9 copy-done.2
  971.1 2.1 copy-done.3
  974.2 1.9 copy-done.7
  977.1 194.3 %finish.1 = (f32[7648,1024]{1,0:T(8,128)}, f32[8,2,64,1024]{3,2,1,0:T(8,128)S(1)}, f32[8,2,16,1024]{3,2,1,0:T(8,128)S(1)}, f32[8,2,64,768]{3,2,1,0:T(8,128)S(1)}, f32[24,1024]{1,0:T(8,128)S(1)}) custom-call(f32[7648,128]{1,0:T(8,128)S(1)} %copy-done.3, f32[2,64,1024]{2,1,0:T(8,128)S(1)} %copy-done.8, f32[2,16,1024]{2,1,0:T(8,128)S(1)} %bitcast.82, ...), custom_call_target="tpu_custom_call" | custom-call | flops 10000000000 | bytes 62914560 | tf_op jit(solution)/shard_map/finish/pallas_call | solution.py:865
  1171.4 2.0 copy-done
  1176.9 22.1 %copy.67 = f32[7648,1024]{1,0:T(8,128)} copy(f32[7648,1024]{1,0:T(8,128)} %get-tuple-element.110) | data formatting | bytes 62652416
  1199.0 1.7 copy.68
  1201.9 1.1 copy-done.12
  1203.0 2.1 copy.70
  1205.2 1.6 copy-done.11
  1206.8 2.1 copy.71
  1208.9 1.6 copy-done.1
  1210.5 2.0 copy.72
  (88 shorter events, 20.4 us)
Async XLA Ops:
  7.2 6.2 copy-start.21
  7.2 6.2 copy-start.16
  7.2 6.2 copy-start.17
  7.2 6.3 copy-start.18
  7.2 6.3 copy-start.19
  7.2 6.3 copy-start.20
  7.2 963.9 %reduce-scatter.2.cloned.1.call-start = ((), (), s32[]{:S(2)}) async-start(), calls=%async_computation.1 | async-start | bytes 4325376 | tf_op jit(solution)/shard_map/reduce_scatter | solution.py:1137
  12.2 6.8 copy-start.15
  12.2 7.8 copy-start.22
  422.2 5.8 copy-start.13
  482.3 0.8 copy-start.14
  482.3 2.7 copy-start.10
  485.1 13.0 %copy-start.9 = (bf16[4,512,1024]{2,1,0:T(8,128)(2,1)S(1)}, bf16[4,512,1024]{2,1,0:T(8,128)(2,1)}, u32[]{:S(2)}) copy-start(bf16[4,512,1024]{2,1,0:T(8,128)(2,1)} %get-tuple-element.66) | copy-start | bytes 12582916
  498.1 10.6 copy-start.23
  498.1 10.6 copy-start.24
  969.2 1.9 copy-start.2
  971.1 2.1 copy-start.3
  973.2 0.9 copy-start.6
  974.1 1.9 copy-start.7
  976.0 1.0 copy-start.8
  1171.4 2.0 copy-start
  1173.4 1.0 copy-start.4
  1199.0 2.0 copy-start.5
  1199.0 4.0 copy-start.12
  1203.0 3.7 copy-start.11
  1206.7 3.7 copy-start.1
Sparse Core Ops, SparseCore 0:
  482.5 150.3 reduce-scatter.1

commit v6 on v5

--- a/solution.py
+++ b/solution.py
@@ -360,8 +360,8 @@
 
 
 RING = 4
-HOLD, LIVE, PAIR = 4, 8, 4
-ADD, LOAD, CROSSED, LAND, PLANE = 1, 4, 5, 7, 8
+HOLD, LIVE, PAIR = 4, 12, 4
+ADD, LOAD, CROSSED, LAND, PLANE, HOP, BEAT = 1, 4, 5, 9, 10, 2, 4
 GATHER = (37, 41)
 
 
@@ -411,7 +411,7 @@
 def backward_kernel(n, rows, chunks, jobs, heads, d_ctx, resid, q, k_all, v, ctx, top, inv, cos, sin, wq, back, emb, *refs):
     prods = refs[:jobs]
     whole = refs[jobs:N2 * jobs - N1]
-    out, grads, d_w, d_bias, landed, cross, last, part, left, right, total, dctx, dq, dk, dv, ctx_in, res_in, cos_in, sin_in, emb_in, work, fresh, xin, yin, keep, pass_on, along, final, *sems = refs[N2 * jobs - N1:]
+    out, grads, d_w, d_bias, landed, cross, last, part, left, right, total, dctx, dq, dk, dv, ctx_in, res_in, cos_in, sin_in, emb_in, q_in, work, fresh, xin, yin, keep, pass_on, along, final, *sems = refs[N2 * jobs - N1:]
     send_r, send_l, recv_l, recv_r, osend, orecv, csend, crecv, esem, fsem, xsend, xrecv, xsem, ysend, yrecv, ysem, ksem, zrecv, frecv, asend, arecv, aself, isem, gsend, grecv = sems
     z = lax.axis_index('tp')
     p, at = plane()
@@ -453,7 +453,7 @@
     def inputs(i):
         slot = i % N2
         at_q = rows_of(i, N0, qb)
-        pairs = ((ctx.at[at_q], ctx_in), (resid.at[i], res_in), (cos.at[at_q], cos_in), (sin.at[at_q], sin_in), (emb.at[at_q], emb_in))
+        pairs = ((ctx.at[at_q], ctx_in), (resid.at[i], res_in), (cos.at[at_q], cos_in), (sin.at[at_q], sin_in), (emb.at[at_q], emb_in), (q.at[at_q], q_in))
         return [pltpu.make_async_copy(src, dst.at[slot], isem.at[j, slot]) for j, (src, dst) in enumerate(pairs)]
 
     dk[:] = jnp.zeros_like(dk)
@@ -478,7 +478,7 @@
             exchange(i, N0).wait()
             others = dctx.at[pl.ds(N0, (n - N1) * share)]
             rcopy(others, others, asend, arecv.at[i], tp=z).wait_recv()
-        attend_grad(i, h, heads, qb, q, k_all, v, ctx_in.at[i % N2], dctx, top, inv, dq, dk, dv)
+        attend_grad(i, h, heads, qb, q_in.at[i % N2], k_all, v, ctx_in.at[i % N2], dctx, top, inv, dq, dk, dv)
 
         @pl.when(h == heads - N1)
         def _():
@@ -497,7 +497,7 @@
 
         @pl.when(u >= HOLD)
         def _():
-            rcopy(xin.at[N0], cross.at[N0], xsend.at[slot], xrecv.at[N0], dp=p).wait_send()
+            rcopy(xin, cross.at[N0], xsend.at[slot], xrecv.at[N0], dp=p).wait_send()
         for m in range(jobs):
             @pl.when(u // span == m)
             def _(m=m):
@@ -521,11 +521,11 @@
 
     def load_cross(u):
         rcopy(cross.at[u], cross.at[u], xsend.at[N0], xrecv.at[u], dp=p).wait_recv()
-        pltpu.make_async_copy(cross.at[u], xin.at[u % N2], xsem.at[u % N2]).start()
+        pltpu.make_async_copy(cross.at[u], xin, xsem).start()
 
     def crossed(u):
         slot = u % HOLD
-        pltpu.make_async_copy(cross.at[u], xin.at[u % N2], xsem.at[u % N2]).wait()
+        pltpu.make_async_copy(cross.at[u], xin, xsem).wait()
 
         @pl.when(u >= LIVE)
         def _():
@@ -534,8 +534,8 @@
         @pl.when(u >= PAIR)
         def _():
             rcopy(pass_on.at[u % PAIR], last.at[u], ysend.at[u % PAIR], yrecv.at[u], dp=p).wait_send()
-        keep[u % LIVE] = xin[u % N2, N0] + work[slot, N0]
-        pass_on[u % PAIR] = xin[u % N2, N1] + work[slot, N2 - u % N2]
+        keep[u % LIVE] = xin[N0] + work[slot, N0]
+        pass_on[u % PAIR] = xin[N1] + work[slot, N2 - u % N2]
 
     def crossed_send(u):
         side, first, second = sides(u)
@@ -543,19 +543,19 @@
 
     def load_last(u):
         rcopy(last.at[u], last.at[u], ysend.at[N0], yrecv.at[u], dp=p).wait_recv()
-        pltpu.make_async_copy(last.at[u], yin.at[u % N2], ysem.at[u % N2]).start()
+        pltpu.make_async_copy(last.at[u], yin, ysem).start()
 
     def in_plane(u):
-        pltpu.make_async_copy(last.at[u], yin.at[u % N2], ysem.at[u % N2]).wait()
-        keep[u % LIVE] = keep[u % LIVE] + yin[u % N2]
+        pltpu.make_async_copy(last.at[u], yin, ysem).wait()
+        keep[u % LIVE] = keep[u % LIVE] + yin[:]
 
     def unit(k):
-        u = (k // 3) * N2 + k % 3
-        return u, (k >= N0) & (k % 3 < N2) & (u < units)
+        u = (k // BEAT) * (BEAT - N1) + k % BEAT
+        return u, (k >= N0) & (k % BEAT < BEAT - N1) & (u < units)
 
     def along_tp(k, t, send):
         toward = jnp.where(z < t, z, n - N1 - z)
-        late = jnp.where(z == t, max(t, n - N1 - t), toward)
+        late = HOP * jnp.where(z == t, max(t, n - N1 - t), toward)
         u, ok = unit(k - PLANE - N1 - late)
         mine = (u // span) * N2 + u % N2
         slot = u % LIVE
@@ -593,6 +593,14 @@
 
     spread = [Spread(at, functools.partial(block_of, whole[m], at), gsend.at[m], grecv.at[m]) for m in range(jobs - N1)]
 
+    def settle(u):
+        pltpu.make_async_copy(keep.at[u % LIVE], keep.at[u % LIVE], ksem.at[u % LIVE]).wait()
+
+    def begin(m):
+        for u in range(max(m * span, units - LIVE), (m + N1) * span):
+            settle(u)
+        spread[m].start()
+
     def place(c):
         return (blocks - N1 - c // per) * per + c % per
 
@@ -617,7 +625,7 @@
     def staged(k, offset, stage):
         u, ok = unit(k - offset)
         pl.when(ok)(functools.partial(stage, u))
-    steps = max(heads + chunks + LAG * (n - N1) + N1, (units // N2) * 3 + PLANE + n)
+    steps = max(heads + chunks + LAG * (n - N1) + N1, units // (BEAT - N1) * BEAT + PLANE + HOP * (n - N1), GATHER[-N1] + 7)
 
     @pl.loop(N0, steps)
     def _(k):
@@ -642,7 +650,7 @@
         for t in range(n):
             along_tp(k, t, True)
         for m, gather in enumerate(spread):
-            for offset, stage in ((N0, gather.start), (3, gather.cross), (6, gather.diagonal)):
+            for offset, stage in ((N0, functools.partial(begin, m)), (3, gather.cross), (6, gather.diagonal)):
                 pl.when(k == GATHER[m] + offset)(stage)
 
     chain_drain(z, n, part, left, right, send_r, send_l, recv_l, recv_r)
@@ -651,11 +659,11 @@
     for rel in range(N1, 8):
         rcopy(out.at[at(rel)], out.at[at(rel)], csend, orecv.at[rel], dp=p).wait_recv()
     for slot in range(HOLD):
-        rcopy(xin.at[N0], cross.at[N0], xsend.at[slot], xrecv.at[N0], dp=p).wait_send()
+        rcopy(xin, cross.at[N0], xsend.at[slot], xrecv.at[N0], dp=p).wait_send()
     for slot in range(PAIR):
         rcopy(pass_on.at[slot], last.at[N0], ysend.at[slot], yrecv.at[N0], dp=p).wait_send()
-    for slot in range(LIVE):
-        pltpu.make_async_copy(keep.at[slot], keep.at[slot], ksem.at[slot]).wait()
+    for u in range(max((jobs - N1) * span, units - LIVE), units):
+        settle(u)
     rcopy(landed, landed, csend, crecv.at[N0], dp=p).wait_send()
     for gather in spread:
         gather.finish()
@@ -676,17 +684,17 @@
     shape = jax.ShapeDtypeStruct
     qb = seq // 8
     vmem = [(seq, width)] * 3 + [(RING, rows, width), (seq, dims), (qb, dims), (seq, dims), (seq, dims), (2, qb, dims), (2, qb // n_tp, width)] + [(2, qb, dims // 2)] * 2 + [
-            (HOLD, 4) + piece, (4,) + piece, (2, 2) + piece, (2,) + piece, (LIVE,) + piece, (PAIR,) + piece, (units,) + piece, (2 * jobs,) + piece]
-    sems = [(), (), (chunks,), (chunks,), (RING,), (8,), (), (units,), (HOLD,), (), (HOLD,), (units,), (2,), (PAIR,), (units,), (2,), (LIVE,), (units,), (2 * jobs,), (), (8,), (8,), (5, 2), (jobs - 1, len(EDGES)), (jobs - 1, len(EDGES))]
+            (HOLD, 4) + piece, (4,) + piece, (2,) + piece, piece, (LIVE,) + piece, (PAIR,) + piece, (units,) + piece, (2 * jobs,) + piece]
+    sems = [(), (), (chunks,), (chunks,), (RING,), (8,), (), (units,), (HOLD,), (), (HOLD,), (units,), (), (PAIR,), (units,), (), (LIVE,), (units,), (2 * jobs,), (), (8,), (8,), (6, 2), (jobs - 1, len(EDGES)), (jobs - 1, len(EDGES))]
     scratch = [pltpu.VMEM(size, F32) for size in vmem]
-    scratch.insert(12, pltpu.VMEM((2, qb, width), BF))
+    scratch[12:12] = [pltpu.VMEM((2, qb, width), BF), pltpu.VMEM((2, qb, dims), BF)]
     full = shape((n_dp, 2) + piece, F32)
     *whole, cols, grads, d_w, d_bias, _, _, _ = pl.pallas_call(
         functools.partial(backward_kernel, n_tp, rows, chunks, jobs, heads),
         name='backward',
         out_shape=[full] * (jobs - 1) + [shape((n_dp, seq, width // n_dp), F32), shape((2,) + piece, F32), shape((width, 3 * dims), F32), shape((1, 3 * dims), F32),
                    shape((units, 4) + piece, F32), shape((units, 2) + piece, F32), shape((units,) + piece, F32)],
-        in_specs=[ANY, ANY] + [VMEM] * 3 + [ANY] + [VMEM] * 2 + [ANY] * 2 + [VMEM] * 2 + [ANY] * (1 + jobs),
+        in_specs=[ANY] * 3 + [VMEM] * 2 + [ANY] + [VMEM] * 2 + [ANY] * 2 + [VMEM] * 2 + [ANY] * (1 + jobs),
         out_specs=[ANY] * (jobs - 1) + [ANY, ANY, VMEM, VMEM, ANY, ANY, ANY],
         scratch_shapes=scratch + [dma(size) for size in sems],
         compiler_params=pltpu.CompilerParams(collective_id=1, has_side_effects=True, vmem_limit_bytes=67_000_000),
@@ -944,10 +952,10 @@
 
 def attend_grad(i, h, heads, qb, q_ref, k_ref, v_ref, ctx_ref, dctx_ref, top_ref, inv_ref, dq_ref, dk_ref, dv_ref):
     kb = 2 * qb
-    dims = q_ref.shape[1]
+    dims = dk_ref.shape[1]
     scale = (dims // heads) ** -0.5
     at_q = pl.ds(pl.multiple_of(i * qb, qb), qb)
-    q = jnp.where(lane_head((qb, dims), heads, 2) == h, q_ref[at_q, :].astype(F32), 0.0).astype(BF)
+    q = jnp.where(lane_head((qb, dims), heads, 2) == h, q_ref[:].astype(F32), 0.0).astype(BF)
     dc = jnp.where(lane_head((qb, dims), heads, 1) == h, dctx_ref[at_q, :], 0.0).astype(BF)
     ones = jnp.ones((8, dims), F32)
     mean = lax.dot_general(ones, dc.astype(F32) * ctx_ref[:], (NT, ((), ())), precision=lax.Precision.HIGHEST, preferred_element_type=F32)[:1]

time: 1230 us -> 1190 us (0.967)
  Pallas kernels: 1070 us -> 1030 us
    pallas_call x1, Pallas kernels: 415 us -> 376 us  [backward(): pl.pallas_call(functools.partial(backward_kernel, n_tp, rows, chunks, job...]
  transfers between devices with their start and end apart: 1 -> 1, of which waited for: 0 -> 0; matrix products, arithmetic and copies ran while one was open for 3% -> 3% of each run, Pallas kernels for 37% -> 35%
where the time goes in v6:
time: 1190 us; the launch traced here: 1180 us
  Pallas kernels  1030 us (87%)
  local copies, waits for them, and re-layouts  80.5 us (7%)
  matrix products  41.7 us (4%)
  between operations  14.8 us (1%)
  other arithmetic  14 us (1%)
    pallas_call x1, Pallas kernels, embed(): pl.pallas_call(functools.partial(emb_kernel, n_tp, rows, chunks, cuts, he...  377 us
    pallas_call x1, Pallas kernels, backward(): pl.pallas_call(functools.partial(backward_kernel, n_tp, rows, chunks, job...  376 us
    pallas_call x1, Pallas kernels, finish(): pl.pallas_call(functools.partial(finish_kernel, n_tp, cuts), name='finish...  191 us
    pallas_call x1, Pallas kernels, layer(): pl.pallas_call(functools.partial(layer_kernel, n), name='layer', grid=(N2...  48.5 us
    unnamed x56, local copies, waits for them, and re-layouts  47.2 us
    pallas_call x1, Pallas kernels, table_rows(): pl.pallas_call(table_kernel, name='table_rows', grid_spec=pltpu.PrefetchS...  33.4 us
    dot_general x3, matrix products, product(): jnp.einsum(spec, lhs, rhs, preferred_element_type=F32)  31.8 us
  transfers between devices with their start and end apart: 1, of which 0 were waited for; matrix products, arithmetic and copies ran while one was open for 3% of the time, Pallas kernels for 35%

profile of v6, /device:TPU:0, one launch (start us, length us, event | category | flops | bytes accessed | tf_op | source)
XLA Modules:
  0.0 1177.7 jit_solution(6363695131494162280)
XLA Ops:
  12.2 1.1 fusion.17.mask
  16.0 1.1 constant_dynamic-slice_fusion.5
  17.6 1.4 convert_element_type.42.piece
  20.1 2.6 fusion.5.wq
  22.7 18.4 %gather_fusion = bf16[2048,1024]{1,0:T(8,128)(2,1)} fusion(bf16[7648,1024]{1,0:T(8,128)(2,1)} %param.21, s32[2048]{0:T(1024)S(1)} %broadcast_clamp_fusion), kind=kCustom, calls=%fused_computation | custom fusion | bytes 8396800 | tf_op jit(solution)/shard_map/jit(_take)/gather | solution.py:1118
  41.1 3.9 broadcast_select_fusion.found
  44.9 377.2 %embed.1 = (bf16[2048,1024]{1,0:T(8,128)(2,1)}, bf16[4,8,128,1024]{3,2,1,0:T(8,128)(2,1)}, bf16[4,8,128,1024]{3,2,1,0:T(8,128)(2,1)}, bf16[4,8,128,1024]{3,2,1,0...) custom-call(bf16[2048,1024]{1,0:T(8,128)(2,1)} %broadcast_select_fus, ...), custom_call_target="tpu_custom_call" | custom-call | flops 20000000000 | bytes 83886080 | tf_op jit(solution)/shard_map/embed/pallas_call | solution.py:346
  422.2 1.3 copy.47
  423.5 2.3 constant_dynamic-slice_fusion.2
  425.7 2.3 constant_dynamic-slice_fusion.3
  429.3 48.5 %layer.1 = (bf16[512,1024]{1,0:T(8,128)(2,1)}, bf16[512,1024]{1,0:T(8,128)(2,1)}, bf16[512,1024]{1,0:T(8,128)(2,1)}, f32[512,1024]{1,0:T(8,128)}, f32[4,512,256]...) custom-call(f32[4,512,256]{2,1,0:T(8,128)} %bitcast.89, ...), custom_call_target="tpu_custom_call" | custom-call | flops 15000000512 | bytes 73400320 | tf_op jit(solution)/shard_map/layer/pallas_call | solution.py:1080
  477.8 4.5 fusion.27
  483.8 1.3 fusion.3.back
  485.1 13.0 %fusion.15 = f32[4,1024,1024]{1,2,0:T(8,128)} fusion(bf16[4,512,1024]{2,1,0:T(8,128)(2,1)} %get-tuple-element.64, bf16[512,1024]{1,0:T(8,128)(2,1)S(1)} %copy-done.10), kind=kOutput, calls=%fused_computation.20 | convolution fusion | flops 4294967296 | bytes 22020096 | tf_op jit(solution)/shard_map/sk,tsc->tkc/dot_general | solution.py:1139
  498.1 10.6 fusion.13
  508.7 8.2 fusion.11
  516.8 376.1 %backward.1 = (f32[8,2,64,1024]{3,2,1,0:T(8,128)}, f32[8,2,64,1024]{3,2,1,0:T(8,128)}, f32[8,2048,128]{2,1,0:T(8,128)}, f32[2,64,1024]{2,1,0:T(8,128)}, f32[1024...) custom-call(f32[4,8,64,256]{3,2,1,0:T(8,128)} %bitcast.114, ...), custom_call_target="tpu_custom_call" | custom-call | flops 20000000000 | bytes 104857600 | tf_op jit(solution)/shard_map/backward/pallas_call | solution.py:692
  893.0 1.8 fusion.9
  896.6 33.4 %table_rows.1.col = f32[7648,128]{1,0:T(8,128)S(1)} custom-call(s32[16384]{0:T(1024)S(1)} %and_select_fusion.ids, f32[16384,128]{1,0:T(8,128)} %bitcast.86), custom_call_target="tpu_custom_call" | custom-call | flops 3000000000 | bytes 16777216 | tf_op jit(solution)/shard_map/table_rows/pallas_call | solution.py:737
  930.0 1.9 copy-done.2
  931.9 2.1 copy-done.3
  935.0 1.9 copy-done.7
  937.9 191.4 %finish.1 = (f32[7648,1024]{1,0:T(8,128)}, f32[8,2,64,1024]{3,2,1,0:T(8,128)S(1)}, f32[8,2,16,1024]{3,2,1,0:T(8,128)S(1)}, f32[8,2,64,768]{3,2,1,0:T(8,128)S(1)}, f32[24,1024]{1,0:T(8,128)S(1)}) custom-call(f32[7648,128]{1,0:T(8,128)S(1)} %copy-done.3, f32[2,64,1024]{2,1,0:T(8,128)S(1)} %copy-done.8, f32[2,16,1024]{2,1,0:T(8,128)S(1)} %bitcast.82, ...), custom_call_target="tpu_custom_call" | custom-call | flops 10000000000 | bytes 62914560 | tf_op jit(solution)/shard_map/finish/pallas_call | solution.py:873
  1129.4 2.0 copy-done
  1134.9 22.1 %copy.67 = f32[7648,1024]{1,0:T(8,128)} copy(f32[7648,1024]{1,0:T(8,128)} %get-tuple-element.110) | data formatting | bytes 62652416
  1157.0 1.7 copy.68
  1159.9 1.1 copy-done.12
  1161.0 2.1 copy.70
  1163.1 1.6 copy-done.11
  1164.7 2.1 copy.71
  1166.8 1.6 copy-done.1
  1168.4 2.0 copy.72
  (88 shorter events, 20.4 us)
Async XLA Ops:
  7.2 6.2 copy-start.21
  7.2 6.2 copy-start.16
  7.2 6.2 copy-start.17
  7.2 6.3 copy-start.18
  7.2 6.3 copy-start.19
  7.2 6.3 copy-start.20
  7.2 924.7 %reduce-scatter.2.cloned.1.call-start = ((), (), s32[]{:S(2)}) async-start(), calls=%async_computation.1 | async-start | bytes 4325376 | tf_op jit(solution)/shard_map/reduce_scatter | solution.py:1145
  12.2 6.8 copy-start.15
  12.2 7.8 copy-start.22
  422.2 5.8 copy-start.13
  482.3 0.8 copy-start.14
  482.3 2.7 copy-start.10
  485.1 13.0 %copy-start.9 = (bf16[4,512,1024]{2,1,0:T(8,128)(2,1)S(1)}, bf16[4,512,1024]{2,1,0:T(8,128)(2,1)}, u32[]{:S(2)}) copy-start(bf16[4,512,1024]{2,1,0:T(8,128)(2,1)} %get-tuple-element.66) | copy-start | bytes 12582916
  498.1 10.6 copy-start.23
  498.1 10.6 copy-start.24
  930.0 1.9 copy-start.2
  931.9 2.1 copy-start.3
  934.1 0.9 copy-start.6
  935.0 1.9 copy-start.7
  936.9 1.0 copy-start.8
  1129.3 2.0 copy-start
  1131.4 1.0 copy-start.4
  1157.0 2.0 copy-start.5
  1157.0 4.0 copy-start.12
  1161.0 3.7 copy-start.11
  1164.7 3.7 copy-start.1
Sparse Core Ops, SparseCore 0:
  482.5 150.5 reduce-scatter.1

commit v7 on v6

--- a/solution.py
+++ b/solution.py
@@ -13,7 +13,6 @@
 SHRINK = 0.1
 ROPE_BASE = 10000.0
 WEIGHT_SPECS = (P(None, 'tp'), P('tp', None), P('tp', None), P(), P(), P(), P(None, 'tp'), P('tp'), P(None, 'tp'), P('tp'), P('tp', None), P(), P())
-ALL = ('tp', 'dp')
 BF = jnp.bfloat16
 N0, N1, N2 = range(3)
 F32 = jnp.float32
@@ -332,31 +331,31 @@
     seq, width = found.shape
     chunks = 32
     rows = seq // chunks
-    dims = wq.shape[1] // 3
-    cuts, lo = [], 0
+    dims = wq.shape[N1] // 3
+    cuts, lo = [], N0
     for weight in local:
-        cuts.append((lo, lo + weight.shape[0] // n_dp))
-        lo = cuts[-1][1]
+        cuts.append((lo, lo + weight.shape[N0] // n_dp))
+        lo = cuts[-N1][N1]
     dma = pltpu.SemaphoreType.DMA
     shape = jax.ShapeDtypeStruct
     shapes = [shape((seq, width), BF)]
-    shapes += [shape((n_tp, n_dp, w.shape[0] // n_dp, w.shape[1]), BF) for w in local]
-    shapes += [shape((n_tp, piece.shape[0] - lo, width), F32), shape((n_dp,) + toks.shape, toks.dtype), shape((n_tp, n_dp) + piece.shape, F32), shape((n_tp, 8, seq // n_tp // 8, dims), F32)]
-    shapes += [shape((seq, dims), BF)] * 3 + [shape((seq, dims), F32)] + [shape((heads, seq), F32)] * 2
+    shapes += [shape((n_tp, n_dp, w.shape[N0] // n_dp, w.shape[N1]), BF) for w in local]
+    shapes += [shape((n_tp, piece.shape[N0] - lo, width), F32), shape((n_dp,) + toks.shape, toks.dtype), shape((n_tp, n_dp) + piece.shape, F32), shape((n_tp, 8, seq // n_tp // 8, dims), F32)]
+    shapes += [shape((seq, dims), BF)] * 3 + [shape((seq, dims), F32)] + [shape((heads, seq), F32)] * N2
     out = pl.pallas_call(
         functools.partial(emb_kernel, n_tp, rows, chunks, cuts, heads),
         name='embed',
         out_shape=shapes,
-        in_specs=[VMEM] * 6 + [ANY] * (2 + len(local)),
+        in_specs=[VMEM] * 6 + [ANY] * (N2 + len(local)),
         out_specs=[VMEM] + [ANY] * (4 + len(local)) + [VMEM] * 6,
-        scratch_shapes=[pltpu.VMEM((seq, width), F32)] * 3 + [pltpu.VMEM((2, lo, width), F32), pltpu.VMEM((2, lo, width), BF), pltpu.VMEM((seq, seq // 8), F32), dma, dma, dma((chunks,)), dma((chunks,)),
-                        dma((8,)), dma((8,)), dma, dma((n_tp,)), dma((n_tp,)), dma((n_tp, len(EDGES))), dma((n_tp, len(EDGES))), dma((len(local),)), dma((2,)), dma((2, len(local))), dma((2,)),
+        scratch_shapes=[pltpu.VMEM((seq, width), F32)] * 3 + [pltpu.VMEM((N2, lo, width), F32), pltpu.VMEM((N2, lo, width), BF), pltpu.VMEM((seq, seq // 8), F32), dma, dma, dma((chunks,)), dma((chunks,)),
+                        dma((8,)), dma((8,)), dma, dma((n_tp,)), dma((n_tp,)), dma((n_tp, len(EDGES))), dma((n_tp, len(EDGES))), dma((len(local),)), dma((N2,)), dma((N2, len(local))), dma((N2,)),
                         dma, dma((n_tp,)), dma],
-        compiler_params=pltpu.CompilerParams(collective_id=0, has_side_effects=True, vmem_limit_bytes=60 * 2 ** 20),
-        cost_estimate=pl.CostEstimate(flops=20 * 10 ** 9, bytes_accessed=80 * 2 ** 20, transcendentals=0),
-    )(found, mask, wq, bq, cos, sin, piece, toks, *[w.reshape(n_dp, w.shape[0] // n_dp, w.shape[1]) for w in local])
-    m = 1 + len(local)
-    return out[0], [w.reshape(n_tp, -1, w.shape[3]) for w in out[1:m]], out[m], out[m + 1], out[m + 3], out[m + 4:]
+        compiler_params=pltpu.CompilerParams(collective_id=N0, has_side_effects=True, vmem_limit_bytes=60 * N2 ** 20),
+        cost_estimate=pl.CostEstimate(flops=20 * 10 ** 9, bytes_accessed=80 * N2 ** 20, transcendentals=N0),
+    )(found, mask, wq, bq, cos, sin, piece, toks, *[w.reshape(n_dp, w.shape[N0] // n_dp, w.shape[N1]) for w in local])
+    m = N1 + len(local)
+    return out[N0], [w.reshape(n_tp, -N1, w.shape[3]) for w in out[N1:m]], out[m], out[m + N1], out[m + 3], out[m + 4:]
 
 
 RING = 4
@@ -674,31 +673,31 @@
 def backward(d_ctx, resid, saved, cos, sin, wq, back, emb, prods, heads, n_tp, n_dp):
     q, k, v, ctx, top, inv = saved
     seq, dims = q.shape
-    width = wq.shape[0]
+    width = wq.shape[N0]
     chunks = 32
     rows = seq // chunks
     jobs = len(prods)
-    piece = (prods[0].shape[2] // 2, prods[0].shape[3])
-    units = jobs * 2 * n_tp
+    piece = (prods[N0].shape[N2] // N2, prods[N0].shape[3])
+    units = jobs * N2 * n_tp
     dma = pltpu.SemaphoreType.DMA
     shape = jax.ShapeDtypeStruct
     qb = seq // 8
-    vmem = [(seq, width)] * 3 + [(RING, rows, width), (seq, dims), (qb, dims), (seq, dims), (seq, dims), (2, qb, dims), (2, qb // n_tp, width)] + [(2, qb, dims // 2)] * 2 + [
-            (HOLD, 4) + piece, (4,) + piece, (2,) + piece, piece, (LIVE,) + piece, (PAIR,) + piece, (units,) + piece, (2 * jobs,) + piece]
-    sems = [(), (), (chunks,), (chunks,), (RING,), (8,), (), (units,), (HOLD,), (), (HOLD,), (units,), (), (PAIR,), (units,), (), (LIVE,), (units,), (2 * jobs,), (), (8,), (8,), (6, 2), (jobs - 1, len(EDGES)), (jobs - 1, len(EDGES))]
+    vmem = [(seq, width)] * 3 + [(RING, rows, width), (seq, dims), (qb, dims), (seq, dims), (seq, dims), (N2, qb, dims), (N2, qb // n_tp, width)] + [(N2, qb, dims // N2)] * N2 + [
+            (HOLD, 4) + piece, (4,) + piece, (N2,) + piece, piece, (LIVE,) + piece, (PAIR,) + piece, (units,) + piece, (N2 * jobs,) + piece]
+    sems = [(), (), (chunks,), (chunks,), (RING,), (8,), (), (units,), (HOLD,), (), (HOLD,), (units,), (), (PAIR,), (units,), (), (LIVE,), (units,), (N2 * jobs,), (), (8,), (8,), (6, N2), (jobs - N1, len(EDGES)), (jobs - N1, len(EDGES))]
     scratch = [pltpu.VMEM(size, F32) for size in vmem]
-    scratch[12:12] = [pltpu.VMEM((2, qb, width), BF), pltpu.VMEM((2, qb, dims), BF)]
-    full = shape((n_dp, 2) + piece, F32)
+    scratch[12:12] = [pltpu.VMEM((N2, qb, width), BF), pltpu.VMEM((N2, qb, dims), BF)]
+    full = shape((n_dp, N2) + piece, F32)
     *whole, cols, grads, d_w, d_bias, _, _, _ = pl.pallas_call(
         functools.partial(backward_kernel, n_tp, rows, chunks, jobs, heads),
         name='backward',
-        out_shape=[full] * (jobs - 1) + [shape((n_dp, seq, width // n_dp), F32), shape((2,) + piece, F32), shape((width, 3 * dims), F32), shape((1, 3 * dims), F32),
-                   shape((units, 4) + piece, F32), shape((units, 2) + piece, F32), shape((units,) + piece, F32)],
-        in_specs=[ANY] * 3 + [VMEM] * 2 + [ANY] + [VMEM] * 2 + [ANY] * 2 + [VMEM] * 2 + [ANY] * (1 + jobs),
-        out_specs=[ANY] * (jobs - 1) + [ANY, ANY, VMEM, VMEM, ANY, ANY, ANY],
+        out_shape=[full] * (jobs - N1) + [shape((n_dp, seq, width // n_dp), F32), shape((N2,) + piece, F32), shape((width, 3 * dims), F32), shape((N1, 3 * dims), F32),
+                   shape((units, 4) + piece, F32), shape((units, N2) + piece, F32), shape((units,) + piece, F32)],
+        in_specs=[ANY] * 3 + [VMEM] * N2 + [ANY] + [VMEM] * N2 + [ANY] * N2 + [VMEM] * N2 + [ANY] * (N1 + jobs),
+        out_specs=[ANY] * (jobs - N1) + [ANY, ANY, VMEM, VMEM, ANY, ANY, ANY],
         scratch_shapes=scratch + [dma(size) for size in sems],
-        compiler_params=pltpu.CompilerParams(collective_id=1, has_side_effects=True, vmem_limit_bytes=67_000_000),
-        cost_estimate=pl.CostEstimate(flops=20 * 10 ** 9, bytes_accessed=100 * 2 ** 20, transcendentals=0),
+        compiler_params=pltpu.CompilerParams(collective_id=N1, has_side_effects=True, vmem_limit_bytes=67_000_000),
+        cost_estimate=pl.CostEstimate(flops=20 * 10 ** 9, bytes_accessed=100 * N2 ** 20, transcendentals=N0),
     )(d_ctx, resid, q, k, v, ctx, top, inv, cos, sin, wq, back, emb, *prods)
     return d_w, d_bias, cols, whole, grads
 
@@ -750,7 +749,45 @@
     )(ids, rows)
 
 
-def finish_kernel(n, cuts, col, down, proj, d_w, small, table, down_all, proj_all, qkv_all, total, landed, work, cross, last, mine, inbox, sem, send, recv, dsend, drecv, osem, csem, xsend, xrecv, ysend, yrecv, rsend, rrecv):
+class PlaneSum:
+    def __init__(self, at, block, landed, work, cross, last, mine, sems):
+        self.at, self.block, self.landed, self.work, self.cross, self.last, self.mine, self.sems = at, block, landed, work, cross, last, mine, sems
+
+    def copy(self, src, dst, kind, side, rel):
+        return rcopy(src, dst, self.sems.at[kind, side, N0], self.sems.at[kind, side, N1], dp=self.at(rel))
+
+    def start(self):
+        for i in range(4):
+            self.copy(self.block(N2 * i + N1), self.landed.at[i], N0, N0, N1).start()
+
+    def first(self):
+        self.copy(self.landed, self.landed, N0, N0, N0).wait()
+        for i in range(4):
+            self.work[i] = self.block(N2 * i)[:] + self.landed[i]
+
+    def first_send(self):
+        for side in range(N2):
+            self.copy(self.work.at[N1 + side, side], self.cross.at[side, N0], N1, side, N2 * (N1 + side)).start()
+            self.copy(self.work.at[3, side], self.cross.at[side, N1], N1, side, N2 * (N1 + side)).start()
+
+    def second(self):
+        for side in range(N2):
+            self.copy(self.cross.at[side], self.cross.at[side], N1, side, N0).wait()
+            self.cross[side, N0] = self.cross[side, N0] + self.work[N0, side]
+            self.cross[side, N1] = self.cross[side, N1] + self.work[N2 - side, side]
+
+    def second_send(self):
+        for side in range(N2):
+            self.copy(self.cross.at[side, N1], self.last.at[side], N2, side, N2 * (N2 - side)).start()
+
+    def end(self):
+        for side in range(N2):
+            self.copy(self.last.at[side], self.last.at[side], N2, side, N0).wait()
+            self.mine[side] = self.cross[side, N0] + self.last[side]
+
+
+def finish_kernel(n, cuts, col, down, proj, d_w, small, table, down_all, proj_all, qkv_all, total, *refs):
+    scratch, (summed, inbox, arrived, sem, send, recv, dsend, drecv, osem, psem, zsem, rsem) = refs[:10], refs[10:]
     z = lax.axis_index('tp')
     p, at = plane()
     entry_barrier(z, n, at)
@@ -762,9 +799,12 @@
             return table.at[pl.ds(cuts[i][N0], cuts[i][N1] - cuts[i][N0]), pl.ds(pl.multiple_of(at(rel) * block, block), block)]
         return Spread(at, region, send.at[i], recv.at[i], col.at[pl.ds(cuts[i][N0], cuts[i][N1] - cuts[i][N0])])
     parts = [part(i) for i in range(len(cuts))]
-    spread = [Spread(at, functools.partial(block_of, ref, at), dsend.at[i], drecv.at[i], own) for i, (ref, own) in enumerate(((down_all, down), (proj_all, proj), (qkv_all, mine)))]
+    qkv_sum = PlaneSum(at, lambda rel: d_w.at[at(rel)], *scratch[:5], psem.at[N0])
+    proj_sum = PlaneSum(at, lambda rel: summed.at[at(rel)], *scratch[5:], psem.at[N1])
+    pairs = ((down, down_all), (proj_sum.mine, proj_all), (qkv_sum.mine, qkv_all))
+    spread = [Spread(at, functools.partial(block_of, ref, at), dsend.at[i], drecv.at[i], own) for i, (own, ref) in enumerate(pairs)]
     own_copies = [pltpu.make_async_copy(col, table.at[:, pl.ds(pl.multiple_of(p * block, block), block)], osem.at[N0])]
-    own_copies += [pltpu.make_async_copy(src, dst.at[p], osem.at[i]) for i, (src, dst) in enumerate(((down, down_all), (proj, proj_all), (mine, qkv_all)), N1)]
+    own_copies += [pltpu.make_async_copy(src, dst.at[p], osem.at[i]) for i, (src, dst) in enumerate(pairs, N1)]
     order = list(range(len(cuts)))
     flipped = order[half:] + order[:half]
     peers = [{'dp': at(N1)}, {'dp': at(N2)}, {'dp': at(4)}, {'tp': z + N1 - N2 * (z % N2)}, {'tp': (z + n // N2) % n}]
@@ -786,67 +826,72 @@
         parts[two].give(6)
 
     def exchange(r):
-        return rcopy(total, inbox.at[r], rsend.at[r], rrecv.at[r], **peers[r])
+        return rcopy(total, inbox.at[r], rsem.at[N0, r], rsem.at[N1, r], **peers[r])
 
     def round_end(r):
         exchange(r).wait()
         total[:] = total[:] + inbox[r]
 
     total[:] = small[:]
-    for i in range(4):
-        rcopy(d_w.at[at(N2 * i + N1)], landed.at[i], csem.at[N0], csem.at[N1], dp=at(N1)).start()
-    for copy in own_copies[:3]:
+    for d in range(N1, n):
+        to = (z + d) % n
+        rcopy(proj.at[to], arrived.at[z], zsem.at[N0, to], zsem.at[N1, z], tp=to).start()
+    qkv_sum.start()
+    for copy in own_copies[:N2]:
         copy.start()
     next_part(N0)
     exchange(N0).start()
     spread[N0].start()
-    spread[N1].start()
     next_part(N1)
-    rcopy(landed, landed, csem.at[N0], csem.at[N1], dp=p).wait()
-    for i in range(4):
-        work[i] = d_w[at(N2 * i)] + landed[i]
+    qkv_sum.first()
     round_end(N0)
-    for side, first in ((N0, N2), (N1, 4)):
-        rcopy(work.at[N1 + side, side], cross.at[side, N0], xsend.at[side], xrecv.at[side], dp=at(first)).start()
-        rcopy(work.at[3, side], cross.at[side, N1], xsend.at[side], xrecv.at[side], dp=at(first)).start()
+    qkv_sum.first_send()
     exchange(N1).start()
     next_part(N2)
     relay_part(N0)
     round_end(N1)
-    for side, first in ((N0, N2), (N1, 4)):
-        rcopy(cross.at[side], cross.at[side], xsend.at[side], xrecv.at[side], dp=p).wait()
-        cross[side, N0] = cross[side, N0] + work[N0, side]
-        cross[side, N1] = cross[side, N1] + work[N2 - side, side]
+    qkv_sum.second()
     exchange(N2).start()
-    for side, second in ((N0, 4), (N1, N2)):
-        rcopy(cross.at[side, N1], last.at[side], ysend.at[side], yrecv.at[side], dp=at(second)).start()
+    qkv_sum.second_send()
     next_part(3)
     spread[N0].cross()
-    spread[N1].cross()
     relay_part(N1)
     round_end(N2)
-    for side in range(N2):
-        rcopy(last.at[side], last.at[side], ysend.at[side], yrecv.at[side], dp=p).wait()
-        mine[side] = cross[side, N0] + last[side]
+    qkv_sum.end()
     exchange(3).start()
     next_part(4)
     spread[N2].start()
     own_copies[3].start()
     spread[N0].diagonal()
-    spread[N1].diagonal()
     relay_part(N2)
+    summed[:] = proj[z]
+    for d in range(N1, n):
+        src = (z + d) % n
+        rcopy(proj.at[src], arrived.at[src], zsem.at[N0, src], zsem.at[N1, src], tp=src).wait()
+        summed[:] = summed[:] + arrived[src]
     round_end(3)
     next_part(5)
     exchange(4).start()
+    proj_sum.start()
     relay_part(3)
     spread[N2].cross()
+    proj_sum.first()
     next_part(6)
+    proj_sum.first_send()
     round_end(4)
     relay_part(4)
+    proj_sum.second()
     next_part(7)
+    proj_sum.second_send()
     spread[N2].diagonal()
-    for i in range(5, len(cuts)):
-        relay_part(i)
+    relay_part(5)
+    proj_sum.end()
+    relay_part(6)
+    spread[N1].start()
+    own_copies[N2].start()
+    relay_part(7)
+    spread[N1].cross()
+    spread[N1].diagonal()
     for i in range(half):
         for via, where in ((3, i), (4, i + half)):
             parts[where].take(via)
@@ -868,20 +913,21 @@
     cuts = [(8 * (tiles * i // 8), 8 * (tiles * (i + N1) // 8)) for i in range(8)]
     dma = pltpu.SemaphoreType.DMA
     shape = jax.ShapeDtypeStruct
-    third = d_w.shape[N1:]
+    ours = (d_w.shape[N1:], proj.shape[N2:])
     kinds = len(EDGES)
+    vmem = [lead + src[N1:] for src in ours for lead in ((4, N2), (4, N2), (N2, N2), (N2,), (N2,))] + [proj.shape[N1:], (5,) + small.shape, proj.shape]
+    sems = [(), (8, kinds), (8, kinds), (3, kinds), (3, kinds), (4,), (N2, 3, N2, N2), (N2, n_tp), (N2, 5)]
     table, down_all, proj_all, qkv_all, total = pl.pallas_call(
         functools.partial(finish_kernel, n_tp, cuts),
         name='finish',
-        out_shape=[shape((size, n_dp * block), F32)] + [shape((n_dp,) + src, F32) for src in (down.shape, proj.shape, third)] + [shape(small.shape, F32)],
-        in_specs=[ANY] * 3 + [VMEM] * N2,
+        out_shape=[shape((size, n_dp * block), F32)] + [shape((n_dp,) + src, F32) for src in (down.shape, ours[N1], ours[N0])] + [shape(small.shape, F32)],
+        in_specs=[ANY] * N2 + [VMEM] * 3,
         out_specs=[ANY] * 4 + [VMEM],
-        scratch_shapes=[pltpu.VMEM(lead + third[N1:], F32) for lead in ((4, N2), (4, N2), (N2, N2), (N2,), (N2,))] + [pltpu.VMEM((5,) + small.shape, F32), dma,
-                        dma((8, kinds)), dma((8, kinds)), dma((3, kinds)), dma((3, kinds)), dma((4,))] + [dma((N2,))] * 5 + [dma((5,))] * N2,
-        compiler_params=pltpu.CompilerParams(collective_id=N2, has_side_effects=True, vmem_limit_bytes=32 * N2 ** 20),
+        scratch_shapes=[pltpu.VMEM(dims, F32) for dims in vmem] + [dma(dims) for dims in sems],
+        compiler_params=pltpu.CompilerParams(collective_id=N2, has_side_effects=True, vmem_limit_bytes=48 * N2 ** 20),
         cost_estimate=pl.CostEstimate(flops=10 * 10 ** 9, bytes_accessed=60 * N2 ** 20, transcendentals=N0),
     )(col, down, proj, d_w, small)
-    return table, down_all.reshape(-N1, down.shape[N2]), proj_all.reshape(-N1, proj.shape[N2]), qkv_all.reshape(-N1, third[N2]), total
+    return [table] + [grad.reshape(-N1, grad.shape[3]) for grad in (down_all, proj_all, qkv_all)] + [total]
 
 
 def dot(a, b, dims):
@@ -1115,7 +1161,7 @@
         local_ids = tokens - tp * vocab_loc
         in_shard = (local_ids >= N0) & (local_ids < vocab_loc)
         safe_ids = jnp.where(in_shard, local_ids, N0)
-        found = jnp.take(emb_table, safe_ids, axis=N0)
+        found = jnp.take(emb_table, safe_ids, axis=N0, mode='clip')
         dims = heads * head_dim
         place = column_order(heads, head_dim)
         swap = (jnp.arange(3 * dims)[:, None] == jnp.asarray(place)[None, :]).astype(BF)
@@ -1142,7 +1188,6 @@
         prod_gate = product(hidden, d_gate_bf, 'sk,tsc->tkc')
         prod_lin = product(hidden, d_lin_bf, 'sk,tsc->tkc')
         d_w_out = jnp.einsum('hse,sd->hed', ctx_own.reshape(n_tp, own, dims).astype(BF), d_attn_bf, preferred_element_type=F32)
-        d_w_out = lax.psum_scatter(d_w_out.reshape(-N1, width), ALL, scatter_dimension=N0, tiled=True)
         d_w_qkv, d_b_qkv, d_cols, (d_w_gate, d_w_lin), d_w_down = backward(
             d_ctx.reshape(n_tp, blocks, own // blocks, dims), resid.reshape(blocks, own // blocks, width), saved, cos_tab, sin_tab, wq, swap.T, emb_bf,
             (prod_gate, prod_lin, prod_down), heads, n_tp, n_dp)
@@ -1157,7 +1202,7 @@
         kept = N2 * n_tp
         small = jnp.concatenate([row_sums[:kept], d_bq_rows, row_sums[kept:kept + 5], jnp.zeros((7, width), F32)], axis=N0)
         d_table, d_w_down, d_w_out, d_w_qkv, small = finish(
-            col, d_w_down, d_w_out.reshape(N2, -N1, width), d_w_qkv.reshape(n_dp, N2, -N1, 3 * dims), small, n_tp, n_dp)
+            col, d_w_down, d_w_out.reshape(n_tp, n_dp, N2, -N1, width), d_w_qkv.reshape(n_dp, N2, -N1, 3 * dims), small, n_tp, n_dp)
         d_b_gate = lax.dynamic_index_in_dim(small[:n_tp], tp, N0, keepdims=False)
         d_b_lin = lax.dynamic_index_in_dim(small[n_tp:N2 * n_tp], tp, N0, keepdims=False)
         d_b_qkv = lax.dynamic_index_in_dim(small[N2 * n_tp:3 * n_tp], tp, N0, keepdims=False)[:3 * dims].reshape(heads, 3 * head_dim)

time: 1190 us -> 1150 us (0.966)
  between operations: 14.8 us -> 1.5 us
    pallas_call x1, Pallas kernels: 376 us -> 353 us  [backward(): pl.pallas_call(functools.partial(backward_kernel, n_tp, rows, chunks, job...]
    pallas_call x1, Pallas kernels: 191 us -> 207 us  [finish(): pl.pallas_call(functools.partial(finish_kernel, n_tp, cuts), name='finish...]
    unnamed x56 -> x60, local copies, waits for them, and re-layouts: 47.2 us -> 39.9 us
  transfers between devices with their start and end apart: 1 -> 0, of which waited for: 0 -> 0; matrix products, arithmetic and copies ran while one was open for 3% -> 0% of each run, Pallas kernels for 35% -> 0%
where the time goes in v7:
time: 1150 us; the launch traced here: 1140 us
  Pallas kernels  1020 us (89%)
  local copies, waits for them, and re-layouts  70.1 us (6%)
  matrix products  42.6 us (4%)
    pallas_call x1, Pallas kernels, embed(): pl.pallas_call(functools.partial(emb_kernel, n_tp, rows, chunks, cuts, he...  377 us
    pallas_call x1, Pallas kernels, backward(): pl.pallas_call(functools.partial(backward_kernel, n_tp, rows, chunks, job...  353 us
    pallas_call x1, Pallas kernels, finish(): pl.pallas_call(functools.partial(finish_kernel, n_tp, cuts), name='finish...  207 us
    pallas_call x1, Pallas kernels, layer(): pl.pallas_call(functools.partial(layer_kernel, n), name='layer', grid=(N2...  48.5 us
    unnamed x60, local copies, waits for them, and re-layouts  39.9 us
    dot_general x3, matrix products, product(): jnp.einsum(spec, lhs, rhs, preferred_element_type=F32)  34.5 us
    pallas_call x1, Pallas kernels, table_rows(): pl.pallas_call(table_kernel, name='table_rows', grid_spec=pltpu.PrefetchS...  33.4 us

profile of v7, /device:TPU:0, one launch (start us, length us, event | category | flops | bytes accessed | tf_op | source)
XLA Modules:
  0.0 1142.1 jit_solution(14054927995007491894)
XLA Ops:
  2.1 18.5 %gather_fusion = bf16[2048,1024]{1,0:T(8,128)(2,1)} fusion(bf16[7648,1024]{1,0:T(8,128)(2,1)} %param.21, s32[2048]{0:T(1024)S(1)} %broadcast_clamp_fusion), kind=kCustom, calls=%fused_computation | custom fusion | bytes 8396800 | tf_op jit(solution)/shard_map/jit(_take)/gather | solution.py:1164
  20.6 1.1 fusion.18.mask
  21.8 2.6 fusion.5.wq
  24.5 1.1 fusion.1.bq
  25.6 1.0 constant_dynamic-slice_fusion.7
  26.5 1.1 constant_dynamic-slice_fusion.5
  29.0 1.4 convert_element_type.42.piece
  30.4 377.3 %embed.1 = (bf16[2048,1024]{1,0:T(8,128)(2,1)}, bf16[4,8,128,1024]{3,2,1,0:T(8,128)(2,1)}, bf16[4,8,128,1024]{3,2,1,0:T(8,128)(2,1)}, bf16[4,8,128,1024]{3,2,1,0...) custom-call(bf16[2048,1024]{1,0:T(8,128)(2,1)} %gather_fusion, ...), custom_call_target="tpu_custom_call" | custom-call | flops 20000000000 | bytes 83886080 | tf_op jit(solution)/shard_map/embed/pallas_call | solution.py:345
  407.8 0.9 broadcast_subtract_fusion
  409.3 2.3 constant_dynamic-slice_fusion.3
  411.6 2.3 constant_dynamic-slice_fusion.2
  415.5 48.5 %layer.1 = (bf16[512,1024]{1,0:T(8,128)(2,1)}, bf16[512,1024]{1,0:T(8,128)(2,1)}, bf16[512,1024]{1,0:T(8,128)(2,1)}, f32[512,1024]{1,0:T(8,128)}, f32[4,512,256]...) custom-call(f32[4,512,256]{2,1,0:T(8,128)} %bitcast.90, ...), custom_call_target="tpu_custom_call" | custom-call | flops 15000000512 | bytes 73400320 | tf_op jit(solution)/shard_map/layer/pallas_call | solution.py:1126
  464.0 1.3 fusion.3.back
  465.3 15.7 %fusion.16 = f32[4,1024,1024]{1,2,0:T(8,128)} fusion(bf16[4,512,1024]{2,1,0:T(8,128)(2,1)} %get-tuple-element.64, bf16[512,1024]{1,0:T(8,128)(2,1)} %get-tuple-element.65), kind=kOutput, calls=%fused_computation.19 | convolution fusion | flops 4294967296 | bytes 22020096 | tf_op jit(solution)/shard_map/sk,tsc->tkc/dot_general | solution.py:1185
  481.1 10.6 fusion.14
  491.7 8.2 fusion.12
  499.9 353.4 %backward.1 = (f32[8,2,64,1024]{3,2,1,0:T(8,128)}, f32[8,2,64,1024]{3,2,1,0:T(8,128)}, f32[8,2048,128]{2,1,0:T(8,128)}, f32[2,64,1024]{2,1,0:T(8,128)}, f32[1024...) custom-call(f32[4,8,64,256]{3,2,1,0:T(8,128)} %bitcast.115, ...), custom_call_target="tpu_custom_call" | custom-call | flops 20000000000 | bytes 104857600 | tf_op jit(solution)/shard_map/backward/pallas_call | solution.py:691
  854.1 33.4 %table_rows.1.col = f32[7648,128]{1,0:T(8,128)S(1)} custom-call(s32[16384]{0:T(1024)S(1)} %copy-done.3, f32[16384,128]{1,0:T(8,128)} %bitcast.85), custom_call_target="tpu_custom_call" | custom-call | flops 3000000000 | bytes 16777216 | tf_op jit(solution)/shard_map/table_rows/pallas_call | solution.py:736
  887.5 1.9 copy-done
  890.7 3.3 fusion.10.proj
  894.0 1.2 fusion.9
  895.4 207.2 %finish.1 = (f32[7648,1024]{1,0:T(8,128)}, f32[8,2,64,1024]{3,2,1,0:T(8,128)}, f32[8,2,16,1024]{3,2,1,0:T(8,128)S(1)}, f32[8,2,64,768]{3,2,1,0:T(8,128)S(1)}, f32[24,1024]{1,0:T(8,128)S(1)}) custom-call(f32[7648,128]{1,0:T(8,128)} %copy-done, f32[2,64,1024]{2,1,0:T(8,128)S(1)} %copy-done.4, f32[4,8,2,16,1024]{4,3,2,1,0:T(8,128)} %fusion.10.proj, ...), custom_call_target="tpu_custom_call" | custom-call | flops 10000000000 | bytes 62914560 | tf_op jit(solution)/shard_map/finish/pallas_call | solution.py:920
  1102.6 1.0 copy-done.1
  1106.1 22.1 %copy.69 = f32[7648,1024]{1,0:T(8,128)} copy(f32[7648,1024]{1,0:T(8,128)} %get-tuple-element.110) | data formatting | bytes 62652416
  1128.2 1.7 copy.70
  1130.2 1.0 copy.71
  1131.1 1.1 copy-done.8
  1132.2 2.1 copy.72
  1134.4 1.6 copy-done.7
  1135.9 2.1 copy.73
  1138.1 1.6 copy-done.9
  1139.6 2.0 copy.74
  (86 shorter events, 10.2 us)
Async XLA Ops:
  2.1 19.7 %copy-start.16 = (s32[768]{0:T(1024)S(1)}, s32[768]{0:T(1024)}, u32[]{:S(2)}) copy-start(s32[768]{0:T(1024)} %constant.50.clone) | copy-start | bytes 9220
  2.1 19.6 %copy-start.23 = (bf16[1024,768]{1,0:T(8,128)(2,1)S(1)}, bf16[1024,768]{1,0:T(8,128)(2,1)}, u32[]{:S(2)}) copy-start(bf16[1024,768]{1,0:T(8,128)(2,1)} %param.22) | copy-start | bytes 4718596
  21.8 2.7 copy-start.22
  21.8 6.7 copy-start.15
  21.8 6.7 copy-start.14
  407.7 6.1 copy-start.17
  407.7 6.1 copy-start.18
  407.8 6.1 copy-start.19
  407.8 6.1 copy-start.20
  407.8 6.2 copy-start.21
  407.8 6.8 copy-start.12
  465.3 15.7 %copy-start.5 = (bf16[4,512,1024]{2,1,0:T(8,128)(2,1)S(1)}, bf16[4,512,1024]{2,1,0:T(8,128)(2,1)}, u32[]{:S(2)}) copy-start(bf16[4,512,1024]{2,1,0:T(8,128)(2,1)} %get-tuple-element.66) | copy-start | bytes 12582916
  465.3 15.7 %copy-start.6 = (bf16[512,1024]{1,0:T(8,128)(2,1)S(1)}, bf16[512,1024]{1,0:T(8,128)(2,1)}, u32[]{:S(2)}) copy-start(bf16[512,1024]{1,0:T(8,128)(2,1)} %get-tuple-element.65) | copy-start | bytes 3145732
  481.1 10.6 copy-start.24
  481.1 10.6 copy-start.25
  853.3 0.8 copy-start.3
  854.1 35.3 %copy-start.10 = (f32[4,8,64,256]{3,2,1,0:T(8,128)S(1)}, f32[4,8,64,256]{3,2,1,0:T(8,128)}, u32[]{:S(2)}) copy-start(f32[4,8,64,256]{3,2,1,0:T(8,128)} %get-tuple-element.49) | copy-start | bytes 6291460
  887.5 1.9 copy-start
  889.5 1.2 copy-start.11
  889.6 4.4 copy-start.26
  889.6 5.6 copy-start.13
  890.1 5.2 copy-start.4
  1102.6 1.0 copy-start.1
  1128.2 2.0 copy-start.2
  1128.2 4.0 copy-start.8
  1132.2 3.7 copy-start.7
  1135.9 3.7 copy-start.9

commit v8 on v7

--- a/solution.py
+++ b/solution.py
@@ -1136,6 +1136,48 @@
     )(ctx, wo, emb, cot, vectors, gate_bias, lin_bias, wg, wl, wd)
 
 
+def products_kernel(n, hidden, d_ffn, inner, d_gate, d_lin, gate, lin, down, turned_hidden):
+    i = pl.program_id(N0)
+    size = hidden.shape[N1]
+    tile = 256 if size % 256 == N0 else size
+
+    @pl.when(i == N0)
+    def _():
+        turned_hidden[:] = hidden[:].T
+
+    def fill(out, lhs, rhs, dims):
+        for lo in range(N0, size, tile):
+            cols = pl.ds(lo, tile)
+            out[N0, :, cols] = dot(lhs, rhs[:, cols], dims)
+    pl.when(i < n)(lambda: fill(gate, turned_hidden[:], d_gate.at[N0], NN))
+    pl.when((i >= n) & (i < N2 * n))(lambda: fill(lin, turned_hidden[:], d_lin.at[N0], NN))
+
+    @pl.when(i >= N2 * n)
+    def _():
+        fill(down, inner[N0].T, d_ffn, NN)
+
+
+def products(hidden, d_ffn, inner, d_gate, d_lin):
+    n, own, ffn = inner.shape
+    width = hidden.shape[N1]
+    once = pl.BlockSpec(memory_space=pltpu.VMEM)
+
+    def slot(rows, first):
+        return pl.BlockSpec((N1, rows, ffn), lambda i: (jnp.clip(i - first * n, N0, n - N1), N0, N0))
+    shape = jax.ShapeDtypeStruct((n, width, ffn), F32)
+    return pl.pallas_call(
+        functools.partial(products_kernel, n),
+        name='products',
+        grid=(3 * n,),
+        in_specs=[once, once, slot(own, N2), slot(own, N0), slot(own, N1)],
+        out_specs=[slot(width, N0), slot(width, N1), slot(width, N2)],
+        out_shape=[shape] * 3,
+        scratch_shapes=[pltpu.VMEM((width, own), BF)],
+        compiler_params=pltpu.CompilerParams(dimension_semantics=('arbitrary',), vmem_limit_bytes=58 * N2 ** 20),
+        cost_estimate=pl.CostEstimate(flops=12 * 10 ** 9, bytes_accessed=70 * N2 ** 20, transcendentals=N0),
+    )(hidden, d_ffn, inner, d_gate, d_lin)
+
+
 def solution(mesh):
     n_tp, n_dp = mesh.shape['tp'], mesh.shape['dp']
     in_specs = (P('dp', None), P('dp', None, None), P('tp', None)) + WEIGHT_SPECS
@@ -1181,16 +1223,11 @@
         hidden, d_ffn_bf, d_attn_bf, resid, d_ctx, row_sums, inner_act, d_gate_bf, d_lin_bf = layer(
             ctx_own.reshape(n_tp, own, dims), wo_full, emb_own, cot_own, vectors, bg_full, bl_full, wg_full, wl_full, wd_full)
 
-        def product(lhs, rhs, spec):
-            return jnp.einsum(spec, lhs, rhs, preferred_element_type=F32).reshape(n_tp, n_dp, -N1, width)
-
-        prod_down = product(inner_act, d_ffn_bf, 'tsc,sd->tcd')
-        prod_gate = product(hidden, d_gate_bf, 'sk,tsc->tkc')
-        prod_lin = product(hidden, d_lin_bf, 'sk,tsc->tkc')
+        prods = [grad.reshape(n_tp, n_dp, -N1, width) for grad in products(hidden, d_ffn_bf, inner_act, d_gate_bf, d_lin_bf)]
         d_w_out = jnp.einsum('hse,sd->hed', ctx_own.reshape(n_tp, own, dims).astype(BF), d_attn_bf, preferred_element_type=F32)
         d_w_qkv, d_b_qkv, d_cols, (d_w_gate, d_w_lin), d_w_down = backward(
             d_ctx.reshape(n_tp, blocks, own // blocks, dims), resid.reshape(blocks, own // blocks, width), saved, cos_tab, sin_tab, wq, swap.T, emb_bf,
-            (prod_gate, prod_lin, prod_down), heads, n_tp, n_dp)
+            prods, heads, n_tp, n_dp)
         d_w_gate, d_w_lin = d_w_gate.reshape(-N1, ffn), d_w_lin.reshape(-N1, ffn)
         d_b_qkv = jnp.dot(d_b_qkv, swap.astype(F32).T, precision=lax.Precision.HIGHEST)
         all_ids = tok_all.reshape(-N1) - tp * vocab_loc

time: 1150 us -> 1140 us (level)
  matrix products: 42.6 us -> 8.12 us
  Pallas kernels: 1020 us -> 1050 us
    dot_general x3 -> x0, matrix products: 34.5 us -> none  [product(): jnp.einsum(spec, lhs, rhs, preferred_element_type=F32)]
    pallas_call x0 -> x1, Pallas kernels: none -> 27.7 us  [products(): pl.pallas_call(functools.partial(products_kernel, n), name='products', gr...]
    unnamed x60 -> x52, local copies, waits for them, and re-layouts: 39.9 us -> 39.6 us
where the time goes in v8:
time: 1140 us
  Pallas kernels  1050 us (92%)
  local copies, waits for them, and re-layouts  70.1 us (6%)
    pallas_call x1, Pallas kernels, embed(): pl.pallas_call(functools.partial(emb_kernel, n_tp, rows, chunks, cuts, he...  377 us
    pallas_call x1, Pallas kernels, backward(): pl.pallas_call(functools.partial(backward_kernel, n_tp, rows, chunks, job...  353 us
    pallas_call x1, Pallas kernels, finish(): pl.pallas_call(functools.partial(finish_kernel, n_tp, cuts), name='finish...  207 us
    pallas_call x1, Pallas kernels, layer(): pl.pallas_call(functools.partial(layer_kernel, n), name='layer', grid=(N2...  48.3 us
    unnamed x52, local copies, waits for them, and re-layouts  39.6 us
    pallas_call x1, Pallas kernels, table_rows(): pl.pallas_call(table_kernel, name='table_rows', grid_spec=pltpu.PrefetchS...  33.3 us
    pallas_call x1, Pallas kernels, products(): pl.pallas_call(functools.partial(products_kernel, n), name='products', gr...  27.7 us

profile of v8, /device:TPU:0, one launch (start us, length us, event | category | flops | bytes accessed | tf_op | source)
XLA Modules:
  0.0 1135.1 jit_solution(15883111020607012759)
XLA Ops:
  2.1 18.5 %gather_fusion = bf16[2048,1024]{1,0:T(8,128)(2,1)} fusion(bf16[7648,1024]{1,0:T(8,128)(2,1)} %param.21, s32[2048]{0:T(1024)S(1)} %broadcast_clamp_fusion), kind=kCustom, calls=%fused_computation | custom fusion | bytes 8396800 | tf_op jit(solution)/shard_map/jit(_take)/gather | solution.py:1206
  20.6 1.1 fusion.12.mask
  21.8 2.6 fusion.5.wq
  24.5 1.1 fusion.1.bq
  25.6 1.0 constant_dynamic-slice_fusion.7
  26.5 1.1 constant_dynamic-slice_fusion.5
  27.6 0.8 constant_dynamic-slice_fusion.4
  29.0 1.4 convert_element_type.42.piece
  30.4 377.4 %embed.1 = (bf16[2048,1024]{1,0:T(8,128)(2,1)}, bf16[4,8,128,1024]{3,2,1,0:T(8,128)(2,1)}, bf16[4,8,128,1024]{3,2,1,0:T(8,128)(2,1)}, bf16[4,8,128,1024]{3,2,1,0...) custom-call(bf16[2048,1024]{1,0:T(8,128)(2,1)} %gather_fusion, ...), custom_call_target="tpu_custom_call" | custom-call | flops 20000000000 | bytes 83886080 | tf_op jit(solution)/shard_map/embed/pallas_call | solution.py:345
  407.8 0.9 broadcast_subtract_fusion
  409.4 2.3 constant_dynamic-slice_fusion.3
  411.6 2.3 constant_dynamic-slice_fusion.2
  415.6 48.3 %layer.1 = (bf16[512,1024]{1,0:T(8,128)(2,1)}, bf16[512,1024]{1,0:T(8,128)(2,1)}, bf16[512,1024]{1,0:T(8,128)(2,1)}, f32[512,1024]{1,0:T(8,128)}, f32[4,512,256]...) custom-call(f32[4,512,256]{2,1,0:T(8,128)} %bitcast.72, ...), custom_call_target="tpu_custom_call" | custom-call | flops 15000000512 | bytes 73400320 | tf_op jit(solution)/shard_map/layer/pallas_call | solution.py:1126
  463.9 1.3 fusion.3.back
  465.2 27.7 %products.1 = (f32[4,1024,1024]{2,1,0:T(8,128)}, f32[4,1024,1024]{2,1,0:T(8,128)}, f32[4,1024,1024]{2,1,0:T(8,128)}) custom-call(bf16[512,1024]{1,0:T(8,128)(2,1)} %get-tuple-element.67.hidden, bf16[512,1024]{1,0:T(8,128)(2,1)} %get-tuple-element.68.d_ffn, bf16[4,512,1024]{2,1,0:T(8,128)(2,1)} %get-tuple-element.69.inner, ...), custom_call_target="tpu_custom_call" | custom-call | flops 12000000000 | bytes 73400320 | tf_op jit(solution)/shard_map/products/pallas_call | solution.py:1168
  492.9 353.4 %backward.1 = (f32[8,2,64,1024]{3,2,1,0:T(8,128)}, f32[8,2,64,1024]{3,2,1,0:T(8,128)}, f32[8,2048,128]{2,1,0:T(8,128)}, f32[2,64,1024]{2,1,0:T(8,128)}, f32[1024...) custom-call(f32[4,8,64,256]{3,2,1,0:T(8,128)} %bitcast.99, ...), custom_call_target="tpu_custom_call" | custom-call | flops 20000000000 | bytes 104857600 | tf_op jit(solution)/shard_map/backward/pallas_call | solution.py:691
  846.3 0.8 copy-done.3
  847.1 33.3 %table_rows.1.col = f32[7648,128]{1,0:T(8,128)S(1)} custom-call(s32[16384]{0:T(1024)S(1)} %copy-done.3, f32[16384,128]{1,0:T(8,128)} %bitcast.67), custom_call_target="tpu_custom_call" | custom-call | flops 3000000000 | bytes 16777216 | tf_op jit(solution)/shard_map/table_rows/pallas_call | solution.py:736
  880.4 1.9 copy-done
  883.6 3.3 fusion.10.proj
  886.8 1.2 fusion.9
  888.3 207.4 %finish.1 = (f32[7648,1024]{1,0:T(8,128)}, f32[8,2,64,1024]{3,2,1,0:T(8,128)}, f32[8,2,16,1024]{3,2,1,0:T(8,128)S(1)}, f32[8,2,64,768]{3,2,1,0:T(8,128)S(1)}, f32[24,1024]{1,0:T(8,128)S(1)}) custom-call(f32[7648,128]{1,0:T(8,128)} %copy-done, f32[2,64,1024]{2,1,0:T(8,128)S(1)} %copy-done.4, f32[4,8,2,16,1024]{4,3,2,1,0:T(8,128)} %fusion.10.proj, ...), custom_call_target="tpu_custom_call" | custom-call | flops 10000000000 | bytes 62914560 | tf_op jit(solution)/shard_map/finish/pallas_call | solution.py:920
  1095.6 1.0 copy-done.1
  1099.1 22.1 %copy.58 = f32[7648,1024]{1,0:T(8,128)} copy(f32[7648,1024]{1,0:T(8,128)} %get-tuple-element.116) | data formatting | bytes 62652416
  1121.2 1.7 copy.59
  1123.2 1.0 copy.60
  1124.2 1.1 copy-done.6
  1125.3 2.1 copy.61
  1127.4 1.6 copy-done.5
  1129.0 2.1 copy.62
  1131.1 1.6 copy-done.7
  1132.7 2.0 copy.63
  (76 shorter events, 8.5 us)
Async XLA Ops:
  2.1 19.7 %copy-start.14 = (s32[768]{0:T(1024)S(1)}, s32[768]{0:T(1024)}, u32[]{:S(2)}) copy-start(s32[768]{0:T(1024)} %constant.50.clone) | copy-start | bytes 9220
  2.1 19.6 %copy-start.21 = (bf16[1024,768]{1,0:T(8,128)(2,1)S(1)}, bf16[1024,768]{1,0:T(8,128)(2,1)}, u32[]{:S(2)}) copy-start(bf16[1024,768]{1,0:T(8,128)(2,1)} %param.22) | copy-start | bytes 4718596
  21.8 2.7 copy-start.20
  21.8 6.7 copy-start.13
  21.8 6.7 copy-start.12
  407.8 6.1 copy-start.15
  407.8 6.1 copy-start.16
  407.8 6.1 copy-start.17
  407.8 6.1 copy-start.18
  407.8 6.2 copy-start.19
  407.8 6.8 copy-start.10
  846.2 0.8 copy-start.3
  847.1 35.3 %copy-start.8 = (f32[4,8,64,256]{3,2,1,0:T(8,128)S(1)}, f32[4,8,64,256]{3,2,1,0:T(8,128)}, u32[]{:S(2)}) copy-start(f32[4,8,64,256]{3,2,1,0:T(8,128)} %get-tuple-element.52) | copy-start | bytes 6291460
  880.4 1.9 copy-start
  882.3 1.2 copy-start.9
  882.4 4.4 copy-start.22
  882.5 5.6 copy-start.11
  883.3 5.0 copy-start.4
  1095.6 1.0 copy-start.1
  1121.2 2.0 copy-start.2
  1121.2 4.0 copy-start.6
  1125.3 3.7 copy-start.5
  1129.0 3.7 copy-start.7

commit v9 on v8

--- a/solution.py
+++ b/solution.py
@@ -61,7 +61,7 @@
 LAG = 3
 
 
-def chain_sum(k, z, n, rows, chunks, part, left, right, done, send_r, send_l, recv_l, recv_r, place=lambda c: c):
+def chain_sum(k, z, n, rows, chunks, part, left, right, done, send_r, send_l, recv_l, recv_r, place=lambda c: c, lag=LAG):
     last = n - 1
 
     def at_rows(c):
@@ -75,7 +75,7 @@
 
     def store(ref, c, value):
         ref[at_rows(c)] = value
-    cl, cr = k - LAG * z, k - LAG * (last - z)
+    cl, cr = k - lag * z, k - lag * (last - z)
     okl, okr = (cl >= 0) & (cl < chunks), (cr >= 0) & (cr < chunks)
 
     @pl.when(okl & (z > 0))
@@ -141,7 +141,9 @@
 
 EDGES = ((0, 0, 2), (0, 0, 4), (0, 0, 1), (2, 1, 4), (4, 2, 2), (2, 0, 1), (4, 0, 1), (6, 1, 1), (6, 2, 1))
 CROSS, DIAGONAL, LAST = ((0, 3, 5), (1, 4, 6)), ((3, 7), (4, 8)), {1: (2,), 3: (5,), 5: (6,), 7: (7, 8)}
-STEPS = (4, 10, 17, 21, 25, 29)
+STEPS = (8, 14, 20, 24, 28, 32)
+ARRIVE = {2: 2, 3: 8}
+EMB_LAG = 4
 FIRST = 18
 ORDER = (0, 2, 4, 1, 3, 5, 6, 7)
 
@@ -258,10 +260,10 @@
         for copy in stored(i, rel, s % N2):
             copy.start()
     events = [(STEPS[d - N1], functools.partial(relay, d, CROSS)) for d in range(N1, n)] + [(STEPS[d + n - N2], functools.partial(relay, d, DIAGONAL)) for d in range(N1, n)]
-    events += [(N2 * d - N2, functools.partial(arrive, d)) for d in range(N2, n)]
+    events += [(ARRIVE[d], functools.partial(arrive, d)) for d in range(N2, n)]
     events += [(FIRST - N1, functools.partial(prefetch, N0))] + [(FIRST + s, functools.partial(convert, s)) for s in range(len(plan))]
 
-    start = per + LAG * (n - N1)
+    start = per + EMB_LAG * (n - N1)
 
     share = qb // n
 
@@ -281,7 +283,7 @@
         def _():
             for d in range(n):
                 context(i, d).start()
-        chain_sum(k, z, n, rows, chunks, part, left, right, done, send_r, send_l, recv_l, recv_r)
+        chain_sum(k, z, n, rows, chunks, part, left, right, done, send_r, send_l, recv_l, recv_r, lag=EMB_LAG)
         for at_step, event in events:
             pl.when(k == at_step)(event)
 
@@ -1042,16 +1044,22 @@
     return jnp.sum(values, axis=0, keepdims=True)
 
 
-def layer_kernel(n, ctx, wo, emb, cot, vectors, gate_bias, lin_bias, wg, wl, wd, hidden, d_ffn, d_attn, resid, d_ctx, sums, inner, d_gate, d_lin, gate, lin, acc, unit1, scale1):
+def layer_kernel(n, ctx, wo, emb, cot, vectors, gate_bias, lin_bias, wg, wl, wd, hidden, d_ffn, d_attn, resid, d_ctx, sums, inner, d_gate, d_lin, gate, lin, acc, unit1, scale1, emb_own, cot_own, sem):
     i = pl.program_id(N0)
     t = i % n
     tile = 256 if acc.shape[N1] % 256 == N0 else acc.shape[N1]
     tiles = range(N0, acc.shape[N1], tile)
     b_out, gain1, bias1, b_down, gain2 = [vectors[pl.ds(j, N1), :] for j in range(5)]
 
+    def owned(src, dst, j):
+        return pltpu.make_async_copy(src.at[:, lax.axis_index('tp')], dst, sem.at[j])
+
     @pl.when(i == N0)
     def _():
-        total = ALPHA * emb[:].astype(F32) + b_out
+        owned(emb, emb_own, N0).start()
+        owned(cot, cot_own, N1).start()
+        owned(emb, emb_own, N0).wait()
+        total = ALPHA * emb_own[:].reshape(acc.shape).astype(F32) + b_out
         for h in range(n):
             total = total + dot(ctx[h].astype(BF), wo[h], NN)
         unit, scale1[:] = standard(total)
@@ -1075,7 +1083,8 @@
     @pl.when(i == n - N1)
     def _():
         unit, scale = standard(ALPHA * hidden[:].astype(F32) + acc[:] + b_down)
-        g = cot[:].astype(F32)
+        owned(cot, cot_own, N1).wait()
+        g = cot_own[:].reshape(acc.shape).astype(F32)
         d_y = standard_grad(g * gain2, unit, scale)
         sums[pl.ds(N2 * n + 3, N1), :] = over_rows(d_y)
         sums[pl.ds(N2 * n + 4, N1), :] = over_rows(g * unit)
@@ -1115,7 +1124,7 @@
 
 def layer(ctx, wo, emb, cot, vectors, gate_bias, lin_bias, wg, wl, wd):
     n, own, dims = ctx.shape
-    width = emb.shape[N1]
+    width = emb.shape[-1]
     ffn = wg.shape[N2]
     once = pl.BlockSpec(memory_space=pltpu.VMEM)
     weight = [pl.BlockSpec((N1,) + w.shape[N1:], lambda i: (i % n, N0, N0)) for w in (wg, wl, wd)]
@@ -1127,10 +1136,10 @@
         functools.partial(layer_kernel, n),
         name='layer',
         grid=(N2 * n,),
-        in_specs=[once] * 7 + weight,
+        in_specs=[once] * 2 + [ANY] * 2 + [once] * 3 + weight,
         out_specs=[once] * 6 + [early, late, late],
         out_shape=[shape((own, width), BF)] * 3 + [shape((own, width), F32), shape((n, own, dims), F32), shape((N2 * n + 8, width), F32), slots, slots, slots],
-        scratch_shapes=[pltpu.VMEM((n, own, ffn), F32)] * N2 + [pltpu.VMEM((own, width), F32)] * N2 + [pltpu.VMEM((own, N1), F32)],
+        scratch_shapes=[pltpu.VMEM((n, own, ffn), F32)] * N2 + [pltpu.VMEM((own, width), F32)] * N2 + [pltpu.VMEM((own, N1), F32)] + [pltpu.VMEM((emb.shape[0],) + emb.shape[2:], BF)] * 2 + [pltpu.SemaphoreType.DMA((2,))],
         compiler_params=pltpu.CompilerParams(dimension_semantics=('arbitrary',), vmem_limit_bytes=62 * N2 ** 20),
         cost_estimate=pl.CostEstimate(flops=15 * 10 ** 9, bytes_accessed=70 * N2 ** 20, transcendentals=N0),
     )(ctx, wo, emb, cot, vectors, gate_bias, lin_bias, wg, wl, wd)
@@ -1216,12 +1225,12 @@
 
         blocks = 8
 
-        def owned(values):
-            return lax.dynamic_index_in_dim(values.reshape(blocks, n_tp, -N1, width), tp, N1, keepdims=False).reshape(own, width)
-        emb_own, cot_own = owned(emb_bf), owned(cotangent[N0])
+        def by_owner(values):
+            return values.reshape(blocks, n_tp, -N1, width)
+
         vectors = jnp.stack([b_out, ln1_gain, ln1_bias, b_down, ln2_gain] + [b_out] * 3).astype(F32)
         hidden, d_ffn_bf, d_attn_bf, resid, d_ctx, row_sums, inner_act, d_gate_bf, d_lin_bf = layer(
-            ctx_own.reshape(n_tp, own, dims), wo_full, emb_own, cot_own, vectors, bg_full, bl_full, wg_full, wl_full, wd_full)
+            ctx_own.reshape(n_tp, own, dims), wo_full, by_owner(emb_bf), by_owner(cotangent[N0]), vectors, bg_full, bl_full, wg_full, wl_full, wd_full)
 
         prods = [grad.reshape(n_tp, n_dp, -N1, width) for grad in products(hidden, d_ffn_bf, inner_act, d_gate_bf, d_lin_bf)]
         d_w_out = jnp.einsum('hse,sd->hed', ctx_own.reshape(n_tp, own, dims).astype(BF), d_attn_bf, preferred_element_type=F32)

time: 1140 us -> 1130 us (level)
    unnamed x52 -> x50, local copies, waits for them, and re-layouts: 39.6 us -> 39.6 us
where the time goes in v9:
time: 1130 us; the launch traced here: 1120 us
  Pallas kernels  1040 us (92%)
  local copies, waits for them, and re-layouts  66.5 us (6%)
    pallas_call x1, Pallas kernels, embed(): pl.pallas_call(functools.partial(emb_kernel, n_tp, rows, chunks, cuts, he...  369 us
    pallas_call x1, Pallas kernels, backward(): pl.pallas_call(functools.partial(backward_kernel, n_tp, rows, chunks, job...  356 us
    pallas_call x1, Pallas kernels, finish(): pl.pallas_call(functools.partial(finish_kernel, n_tp, cuts), name='finish...  204 us
    pallas_call x1, Pallas kernels, layer(): pl.pallas_call(functools.partial(layer_kernel, n), name='layer', grid=(N2...  49.6 us
    unnamed x50, local copies, waits for them, and re-layouts  39.6 us
    pallas_call x1, Pallas kernels, table_rows(): pl.pallas_call(table_kernel, name='table_rows', grid_spec=pltpu.PrefetchS...  33.3 us
    pallas_call x1, Pallas kernels, products(): pl.pallas_call(functools.partial(products_kernel, n), name='products', gr...  27.5 us

profile of v9, /device:TPU:0, one launch (start us, length us, event | category | flops | bytes accessed | tf_op | source)
XLA Modules:
  0.0 1123.5 jit_solution(10671051747718644598)
XLA Ops:
  2.1 18.5 %gather_fusion = bf16[2048,1024]{1,0:T(8,128)(2,1)} fusion(bf16[7648,1024]{1,0:T(8,128)(2,1)} %param.21, s32[2048]{0:T(1024)S(1)} %broadcast_clamp_fusion), kind=kCustom, calls=%fused_computation | custom fusion | bytes 8396800 | tf_op jit(solution)/shard_map/jit(_take)/gather | solution.py:1215
  20.6 1.1 fusion.12.mask
  21.8 2.7 fusion.5.wq
  24.5 1.1 fusion.1.bq
  25.6 1.0 constant_dynamic-slice_fusion.5
  26.5 1.1 constant_dynamic-slice_fusion.3
  27.6 0.8 constant_dynamic-slice_fusion.2
  29.0 1.4 convert_element_type.42.piece
  30.4 368.8 %embed.1 = (bf16[2048,1024]{1,0:T(8,128)(2,1)}, bf16[4,8,128,1024]{3,2,1,0:T(8,128)(2,1)}, bf16[4,8,128,1024]{3,2,1,0:T(8,128)(2,1)}, bf16[4,8,128,1024]{3,2,1,0...) custom-call(bf16[2048,1024]{1,0:T(8,128)(2,1)} %gather_fusion, ...), custom_call_target="tpu_custom_call" | custom-call | flops 20000000000 | bytes 83886080 | tf_op jit(solution)/shard_map/embed/pallas_call | solution.py:347
  399.2 0.9 broadcast_subtract_fusion
  401.5 1.1 copy.41
  403.3 49.6 %layer.1 = (bf16[512,1024]{1,0:T(8,128)(2,1)}, bf16[512,1024]{1,0:T(8,128)(2,1)}, bf16[512,1024]{1,0:T(8,128)(2,1)}, f32[512,1024]{1,0:T(8,128)}, f32[4,512,256]...) custom-call(f32[4,512,256]{2,1,0:T(8,128)} %bitcast.66, ...), custom_call_target="tpu_custom_call" | custom-call | flops 15000000512 | bytes 73400320 | tf_op jit(solution)/shard_map/layer/pallas_call | solution.py:1135
  452.9 1.3 fusion.3.back
  454.3 27.5 %products.1 = (f32[4,1024,1024]{2,1,0:T(8,128)}, f32[4,1024,1024]{2,1,0:T(8,128)}, f32[4,1024,1024]{2,1,0:T(8,128)}) custom-call(bf16[512,1024]{1,0:T(8,128)(2,1)} %get-tuple-element.67.hidden, bf16[512,1024]{1,0:T(8,128)(2,1)} %get-tuple-element.68.d_ffn, bf16[4,512,1024]{2,1,0:T(8,128)(2,1)} %get-tuple-element.69.inner, ...), custom_call_target="tpu_custom_call" | custom-call | flops 12000000000 | bytes 73400320 | tf_op jit(solution)/shard_map/products/pallas_call | solution.py:1177
  481.7 356.0 %backward.1 = (f32[8,2,64,1024]{3,2,1,0:T(8,128)}, f32[8,2,64,1024]{3,2,1,0:T(8,128)}, f32[8,2048,128]{2,1,0:T(8,128)}, f32[2,64,1024]{2,1,0:T(8,128)}, f32[1024...) custom-call(f32[4,8,64,256]{3,2,1,0:T(8,128)} %bitcast.91, ...), custom_call_target="tpu_custom_call" | custom-call | flops 20000000000 | bytes 104857600 | tf_op jit(solution)/shard_map/backward/pallas_call | solution.py:693
  837.7 0.8 copy-done.3
  838.5 33.3 %table_rows.1.col = f32[7648,128]{1,0:T(8,128)S(1)} custom-call(s32[16384]{0:T(1024)S(1)} %copy-done.3, f32[16384,128]{1,0:T(8,128)} %bitcast.61), custom_call_target="tpu_custom_call" | custom-call | flops 3000000000 | bytes 16777216 | tf_op jit(solution)/shard_map/table_rows/pallas_call | solution.py:738
  871.9 1.9 copy-done
  873.9 0.8 copy.43
  875.0 3.3 fusion.10.proj
  878.3 1.2 fusion.9
  879.7 204.3 %finish.1 = (f32[7648,1024]{1,0:T(8,128)}, f32[8,2,64,1024]{3,2,1,0:T(8,128)}, f32[8,2,16,1024]{3,2,1,0:T(8,128)S(1)}, f32[8,2,64,768]{3,2,1,0:T(8,128)S(1)}, f32[24,1024]{1,0:T(8,128)S(1)}) custom-call(f32[7648,128]{1,0:T(8,128)} %copy-done, f32[2,64,1024]{2,1,0:T(8,128)S(1)} %copy-done.4, f32[4,8,2,16,1024]{4,3,2,1,0:T(8,128)} %fusion.10.proj, ...), custom_call_target="tpu_custom_call" | custom-call | flops 10000000000 | bytes 62914560 | tf_op jit(solution)/shard_map/finish/pallas_call | solution.py:922
  1084.1 1.0 copy-done.1
  1087.5 22.1 %copy.52 = f32[7648,1024]{1,0:T(8,128)} copy(f32[7648,1024]{1,0:T(8,128)} %get-tuple-element.116) | data formatting | bytes 62652416
  1109.7 1.7 copy.53
  1111.6 1.0 copy.54
  1112.6 1.1 copy-done.6
  1113.7 2.1 copy.55
  1115.8 1.6 copy-done.5
  1117.4 2.1 copy.56
  1119.5 1.6 copy-done.7
  1121.1 2.0 copy.57
  (72 shorter events, 7.5 us)
Async XLA Ops:
  2.1 19.7 %copy-start.13 = (s32[768]{0:T(1024)S(1)}, s32[768]{0:T(1024)}, u32[]{:S(2)}) copy-start(s32[768]{0:T(1024)} %constant.44.clone) | copy-start | bytes 9220
  2.1 19.6 %copy-start.20 = (bf16[1024,768]{1,0:T(8,128)(2,1)S(1)}, bf16[1024,768]{1,0:T(8,128)(2,1)}, u32[]{:S(2)}) copy-start(bf16[1024,768]{1,0:T(8,128)(2,1)} %param.22) | copy-start | bytes 4718596
  21.8 2.7 copy-start.19
  21.8 6.7 copy-start.12
  21.8 6.7 copy-start.11
  30.4 370.3 %copy-start.14 = (bf16[1024]{0:T(1024)(128)(2,1)S(1)}, bf16[1024]{0:T(1024)(128)(2,1)}, u32[]{:S(2)}) copy-start(bf16[1024]{0:T(1024)(128)(2,1)} %param.25) | copy-start | bytes 6148
  30.4 370.3 %copy-start.15 = (bf16[1024]{0:T(1024)(128)(2,1)S(1)}, bf16[1024]{0:T(1024)(128)(2,1)}, u32[]{:S(2)}) copy-start(bf16[1024]{0:T(1024)(128)(2,1)} %param.26) | copy-start | bytes 6148
  30.4 370.3 %copy-start.16 = (bf16[1024]{0:T(1024)(128)(2,1)S(1)}, bf16[1024]{0:T(1024)(128)(2,1)}, u32[]{:S(2)}) copy-start(bf16[1024]{0:T(1024)(128)(2,1)} %param.27) | copy-start | bytes 6148
  30.4 370.3 %copy-start.17 = (bf16[1024]{0:T(1024)(128)(2,1)S(1)}, bf16[1024]{0:T(1024)(128)(2,1)}, u32[]{:S(2)}) copy-start(bf16[1024]{0:T(1024)(128)(2,1)} %param.33) | copy-start | bytes 6148
  30.4 370.4 %copy-start.18 = (bf16[1024]{0:T(1024)(128)(2,1)S(1)}, bf16[1024]{0:T(1024)(128)(2,1)}, u32[]{:S(2)}) copy-start(bf16[1024]{0:T(1024)(128)(2,1)} %param.34) | copy-start | bytes 6148
  837.7 0.8 copy-start.3
  838.5 35.3 %copy-start.8 = (f32[4,8,64,256]{3,2,1,0:T(8,128)S(1)}, f32[4,8,64,256]{3,2,1,0:T(8,128)}, u32[]{:S(2)}) copy-start(f32[4,8,64,256]{3,2,1,0:T(8,128)} %get-tuple-element.52) | copy-start | bytes 6291460
  871.9 1.9 copy-start
  873.8 1.2 copy-start.9
  873.9 4.4 copy-start.21
  874.7 4.8 copy-start.10
  874.7 5.0 copy-start.4
  1084.1 1.0 copy-start.1
  1109.6 2.0 copy-start.2
  1109.7 4.0 copy-start.6
  1113.7 3.7 copy-start.5
  1117.4 3.7 copy-start.7

commit v10 on v9

--- a/solution.py
+++ b/solution.py
@@ -707,7 +707,9 @@
 WAYS = 4
 
 
-def table_kernel(ids, rows_ref, out, *tables):
+def table_kernel(ids, rows_ref, one, two, out, one_out, two_out, *tables):
+    one_out[:] = one[:]
+    two_out[:] = two[:]
     step = pl.program_id(0)
     count = rows_ref.shape[0]
     part = count // WAYS
@@ -732,23 +734,25 @@
         out[:] = SHRINK * total[:out.shape[0]]
 
 
-def table_rows(ids, rows, vocab_loc):
+def table_rows(ids, rows, vocab_loc, one, two):
     count, block = rows.shape
     step = min(1024, count // 2)
+    tall = pl.BlockSpec((one.shape[0] // (count // step), one.shape[1]), lambda i, ids: (i, 0))
+    same = jax.ShapeDtypeStruct(one.shape, F32)
     return pl.pallas_call(
         table_kernel,
         name='table_rows',
         grid_spec=pltpu.PrefetchScalarGridSpec(
             num_scalar_prefetch=1,
             grid=(count // step,),
-            in_specs=[pl.BlockSpec((step, block), lambda i, ids: (i, 0))],
-            out_specs=pl.BlockSpec((vocab_loc, block), lambda i, ids: (0, 0)),
+            in_specs=[pl.BlockSpec((step, block), lambda i, ids: (i, 0)), tall, tall],
+            out_specs=[pl.BlockSpec((vocab_loc, block), lambda i, ids: (0, 0)), tall, tall],
             scratch_shapes=[pltpu.VMEM((vocab_loc + 8, block), F32)] * WAYS,
         ),
-        out_shape=jax.ShapeDtypeStruct((vocab_loc, block), F32),
+        out_shape=[jax.ShapeDtypeStruct((vocab_loc, block), F32), same, same],
         compiler_params=pltpu.CompilerParams(dimension_semantics=('arbitrary',), vmem_limit_bytes=48 * 2 ** 20),
         cost_estimate=pl.CostEstimate(flops=3 * 10 ** 9, bytes_accessed=16 * 2 ** 20, transcendentals=0),
-    )(ids, rows)
+    )(ids, rows, one, two)
 
 
 class PlaneSum:
@@ -960,8 +964,10 @@
     v[at_q, :] = qkv[:, 2 * dims:]
 
 
-def scores(i, j, kb, qb, scale, keys, q):
+def scores(i, j, kb, qb, scale, keys, q, diagonal):
     s = dot(keys, q, NT) * scale
+    if not diagonal:
+        return s
     key = j * kb + lax.broadcasted_iota(jnp.int32, (kb, qb), 0)
     query = i * qb + lax.broadcasted_iota(jnp.int32, (kb, qb), 1)
     return jnp.where(query >= key, s, -1e30)
@@ -978,11 +984,12 @@
     def at_key(j):
         return pl.ds(pl.multiple_of(j * kb, kb), kb)
 
-    def first(j, top):
-        s = scores(i, j, kb, qb, scale, k_ref[at_key(j), :], q)
+    def first(diagonal, j, top):
+        s = scores(i, j, kb, qb, scale, k_ref[at_key(j), :], q, diagonal)
         s_ref[at_key(j), :] = s
         return jnp.maximum(top, jnp.max(s, axis=0, keepdims=True))
-    top = lax.fori_loop(0, count, first, jnp.full((1, qb), -1e30, F32))
+    top = lax.fori_loop(0, count - 1, functools.partial(first, False), jnp.full((1, qb), -1e30, F32))
+    top = first(True, count - 1, top)
 
     def weigh(j, total):
         e = jnp.exp(s_ref[at_key(j), :] - top)
@@ -1009,15 +1016,16 @@
     mean = lax.dot_general(ones, dc.astype(F32) * ctx_ref[:], (NT, ((), ())), precision=lax.Precision.HIGHEST, preferred_element_type=F32)[:1]
     top, inv = top_ref[pl.ds(h, 1), at_q], inv_ref[pl.ds(h, 1), at_q]
 
-    def step(j, dq):
+    def step(diagonal, j, dq):
         at_k = pl.ds(pl.multiple_of(j * kb, kb), kb)
         keys = k_ref[at_k, :]
-        probs = (jnp.exp(scores(i, j, kb, qb, scale, keys, q) - top) * inv).astype(BF)
+        probs = (jnp.exp(scores(i, j, kb, qb, scale, keys, q, diagonal) - top) * inv).astype(BF)
         ds = (probs.astype(F32) * (dot(v_ref[at_k, :], dc, NT) - mean) * scale).astype(BF)
         dv_ref[at_k, :] += dot(probs, dc, NN)
         dk_ref[at_k, :] += dot(ds, q, NN)
         return dq + dot(ds, keys, TN)
-    dq = lax.fori_loop(0, (i + 2) // 2, step, jnp.zeros((qb, dims), F32))
+    last = (i + 2) // 2 - 1
+    dq = step(True, last, lax.fori_loop(0, last, functools.partial(step, False), jnp.zeros((qb, dims), F32)))
     dq_ref[:] = jnp.where(lane_head((qb, dims), heads, 2) == h, dq, dq_ref[:])
 
 
@@ -1241,7 +1249,7 @@
         d_b_qkv = jnp.dot(d_b_qkv, swap.astype(F32).T, precision=lax.Precision.HIGHEST)
         all_ids = tok_all.reshape(-N1) - tp * vocab_loc
         all_ids = jnp.where((all_ids >= N0) & (all_ids < vocab_loc), all_ids, vocab_loc)
-        col = table_rows(all_ids, d_cols.reshape(n_dp * seq_len, -N1), vocab_loc)
+        col, d_w_gate, d_w_lin = table_rows(all_ids, d_cols.reshape(n_dp * seq_len, -N1), vocab_loc, d_w_gate, d_w_lin)
 
         slot = (jnp.arange(n_tp) == tp).astype(F32)[:, None]
         d_bq_rows = jnp.pad(slot * d_b_qkv, ((N0, N0), (N0, ffn - 3 * dims)))

time: 1130 us -> 1130 us (level)
    unnamed x50 -> x44, local copies, waits for them, and re-layouts: 39.6 us -> 32.2 us
where the time goes in v10:
time: 1130 us; the launch traced here: 1120 us
  Pallas kernels  1040 us (92%)
  local copies, waits for them, and re-layouts  59.1 us (5%)
    pallas_call x1, Pallas kernels, embed(): pl.pallas_call(functools.partial(emb_kernel, n_tp, rows, chunks, cuts, he...  369 us
    pallas_call x1, Pallas kernels, backward(): pl.pallas_call(functools.partial(backward_kernel, n_tp, rows, chunks, job...  355 us
    pallas_call x1, Pallas kernels, finish(): pl.pallas_call(functools.partial(finish_kernel, n_tp, cuts), name='finish...  207 us
    pallas_call x1, Pallas kernels, layer(): pl.pallas_call(functools.partial(layer_kernel, n), name='layer', grid=(N2...  49.6 us
    pallas_call x1, Pallas kernels, table_rows(): pl.pallas_call(table_kernel, name='table_rows', grid_spec=pltpu.PrefetchS...  35.8 us
    unnamed x44, local copies, waits for them, and re-layouts  32.2 us
    pallas_call x1, Pallas kernels, products(): pl.pallas_call(functools.partial(products_kernel, n), name='products', gr...  27.4 us

profile of v10, /device:TPU:0, one launch (start us, length us, event | category | flops | bytes accessed | tf_op | source)
XLA Modules:
  0.0 1120.8 jit_solution(7389160605658770464)
XLA Ops:
  0.6 0.7 subtract_bitcast_fusion
  2.1 18.5 %gather_fusion = bf16[2048,1024]{1,0:T(8,128)(2,1)} fusion(bf16[7648,1024]{1,0:T(8,128)(2,1)} %param.21, s32[2048]{0:T(1024)S(1)} %broadcast_clamp_fusion), kind=kCustom, calls=%fused_computation | custom fusion | bytes 8396800 | tf_op jit(solution)/shard_map/jit(_take)/gather | solution.py:1223
  20.6 1.1 fusion.12.mask
  21.8 2.6 fusion.5.wq
  24.5 1.1 fusion.1.bq
  25.6 1.0 constant_dynamic-slice_fusion.5
  26.5 1.1 constant_dynamic-slice_fusion.3
  27.6 0.8 constant_dynamic-slice_fusion.2
  29.0 1.4 convert_element_type.42.piece
  30.4 368.8 %embed.1 = (bf16[2048,1024]{1,0:T(8,128)(2,1)}, bf16[4,8,128,1024]{3,2,1,0:T(8,128)(2,1)}, bf16[4,8,128,1024]{3,2,1,0:T(8,128)(2,1)}, bf16[4,8,128,1024]{3,2,1,0...) custom-call(bf16[2048,1024]{1,0:T(8,128)(2,1)} %gather_fusion, ...), custom_call_target="tpu_custom_call" | custom-call | flops 20000000000 | bytes 83886080 | tf_op jit(solution)/shard_map/embed/pallas_call | solution.py:347
  399.3 0.9 broadcast_subtract_fusion
  400.1 0.6 and_select_fusion.ids
  401.5 1.1 copy.41
  402.7 0.7 fusion.16
  403.4 49.6 %layer.1 = (bf16[512,1024]{1,0:T(8,128)(2,1)}, bf16[512,1024]{1,0:T(8,128)(2,1)}, bf16[512,1024]{1,0:T(8,128)(2,1)}, f32[512,1024]{1,0:T(8,128)}, f32[4,512,256]...) custom-call(f32[4,512,256]{2,1,0:T(8,128)} %bitcast.66, ...), custom_call_target="tpu_custom_call" | custom-call | flops 15000000512 | bytes 73400320 | tf_op jit(solution)/shard_map/layer/pallas_call | solution.py:1143
  453.0 1.3 fusion.3.back
  454.3 27.4 %products.1 = (f32[4,1024,1024]{2,1,0:T(8,128)}, f32[4,1024,1024]{2,1,0:T(8,128)}, f32[4,1024,1024]{2,1,0:T(8,128)}) custom-call(bf16[512,1024]{1,0:T(8,128)(2,1)} %get-tuple-element.70.hidden, bf16[512,1024]{1,0:T(8,128)(2,1)} %get-tuple-element.71.d_ffn, bf16[4,512,1024]{2,1,0:T(8,128)(2,1)} %get-tuple-element.72.inner, ...), custom_call_target="tpu_custom_call" | custom-call | flops 12000000000 | bytes 73400320 | tf_op jit(solution)/shard_map/products/pallas_call | solution.py:1185
  481.8 355.1 %backward.1 = (f32[8,2,64,1024]{3,2,1,0:T(8,128)}, f32[8,2,64,1024]{3,2,1,0:T(8,128)}, f32[8,2048,128]{2,1,0:T(8,128)}, f32[2,64,1024]{2,1,0:T(8,128)}, f32[1024...) custom-call(f32[4,8,64,256]{3,2,1,0:T(8,128)} %bitcast.91, ...), custom_call_target="tpu_custom_call" | custom-call | flops 20000000000 | bytes 104857600 | tf_op jit(solution)/shard_map/backward/pallas_call | solution.py:693
  836.9 0.8 copy-done.2
  837.7 35.8 %table_rows.1 = (f32[7648,128]{1,0:T(8,128)S(1)}, f32[1024,1024]{1,0:T(8,128)}, f32[1024,1024]{1,0:T(8,128)}) custom-call(s32[16384]{0:T(1024)S(1)} %copy-done.2, f32[16384,128]{1,0:T(8,128)} %bitcast.61, f32[1024,1024]{1,0:T(8,128)} %bitcast.64, f32[1024,1024]{1,0:T(8,128)} %bitcast.65), custom_call_target="tpu_custom_call" | custom-call | flops 3000000000 | bytes 16777216 | tf_op jit(solution)/shard_map/table_rows/pallas_call | solution.py:742
  873.5 1.9 copy-done.3
  875.5 0.8 copy.43
  876.6 3.3 fusion.10.proj
  879.9 1.2 fusion.9
  881.3 207.4 %finish.1 = (f32[7648,1024]{1,0:T(8,128)}, f32[8,2,64,1024]{3,2,1,0:T(8,128)}, f32[8,2,16,1024]{3,2,1,0:T(8,128)S(1)}, f32[8,2,64,768]{3,2,1,0:T(8,128)S(1)}, f32[24,1024]{1,0:T(8,128)S(1)}) custom-call(f32[7648,128]{1,0:T(8,128)} %copy-done.3, f32[2,64,1024]{2,1,0:T(8,128)S(1)} %copy-done.4, f32[4,8,2,16,1024]{4,3,2,1,0:T(8,128)} %fusion.10.proj, ...), custom_call_target="tpu_custom_call" | custom-call | flops 10000000000 | bytes 62914560 | tf_op jit(solution)/shard_map/finish/pallas_call | solution.py:926
  1088.7 1.0 copy-done
  1089.7 0.7 reshape.182
  1092.2 22.1 %copy.50 = f32[7648,1024]{1,0:T(8,128)} copy(f32[7648,1024]{1,0:T(8,128)} %get-tuple-element.122) | data formatting | bytes 62652416
  1114.3 1.7 copy.51
  1116.2 1.0 copy.52
  1117.2 1.1 copy-done.5
  1118.3 2.0 copy.53
  (66 shorter events, 4.8 us)
Async XLA Ops:
  2.1 19.7 %copy-start.11 = (s32[768]{0:T(1024)S(1)}, s32[768]{0:T(1024)}, u32[]{:S(2)}) copy-start(s32[768]{0:T(1024)} %constant.44.clone) | copy-start | bytes 9220
  2.1 19.6 %copy-start.18 = (bf16[1024,768]{1,0:T(8,128)(2,1)S(1)}, bf16[1024,768]{1,0:T(8,128)(2,1)}, u32[]{:S(2)}) copy-start(bf16[1024,768]{1,0:T(8,128)(2,1)} %param.22) | copy-start | bytes 4718596
  21.8 2.7 copy-start.17
  21.8 6.7 copy-start.10
  21.8 6.7 copy-start.9
  30.4 370.4 %copy-start.12 = (bf16[1024]{0:T(1024)(128)(2,1)S(1)}, bf16[1024]{0:T(1024)(128)(2,1)}, u32[]{:S(2)}) copy-start(bf16[1024]{0:T(1024)(128)(2,1)} %param.25) | copy-start | bytes 6148
  30.4 370.4 %copy-start.13 = (bf16[1024]{0:T(1024)(128)(2,1)S(1)}, bf16[1024]{0:T(1024)(128)(2,1)}, u32[]{:S(2)}) copy-start(bf16[1024]{0:T(1024)(128)(2,1)} %param.26) | copy-start | bytes 6148
  30.4 370.4 %copy-start.14 = (bf16[1024]{0:T(1024)(128)(2,1)S(1)}, bf16[1024]{0:T(1024)(128)(2,1)}, u32[]{:S(2)}) copy-start(bf16[1024]{0:T(1024)(128)(2,1)} %param.27) | copy-start | bytes 6148
  30.4 370.4 %copy-start.15 = (bf16[1024]{0:T(1024)(128)(2,1)S(1)}, bf16[1024]{0:T(1024)(128)(2,1)}, u32[]{:S(2)}) copy-start(bf16[1024]{0:T(1024)(128)(2,1)} %param.33) | copy-start | bytes 6148
  30.4 370.4 %copy-start.16 = (bf16[1024]{0:T(1024)(128)(2,1)S(1)}, bf16[1024]{0:T(1024)(128)(2,1)}, u32[]{:S(2)}) copy-start(bf16[1024]{0:T(1024)(128)(2,1)} %param.34) | copy-start | bytes 6148
  836.9 0.8 copy-start.2
  837.7 37.7 %copy-start.6 = (f32[4,8,64,256]{3,2,1,0:T(8,128)S(1)}, f32[4,8,64,256]{3,2,1,0:T(8,128)}, u32[]{:S(2)}) copy-start(f32[4,8,64,256]{3,2,1,0:T(8,128)} %get-tuple-element.55) | copy-start | bytes 6291460
  873.5 1.9 copy-start.3
  875.4 1.2 copy-start.7
  875.5 4.4 copy-start.19
  876.3 4.8 copy-start.8
  876.3 5.0 copy-start.4
  1088.7 1.0 copy-start
  1114.3 2.0 copy-start.1
  1114.3 4.0 copy-start.5
